TPU v7x, 512 devices: a whole 4x8x8 slice. The times are simulated.
512 devices in a mesh: op: 32 (over x, y_hi, core), sec: 16 (over z, y_lo).
Axes of the slice: x: 4, y: 8 (y_hi: 4, y_lo: 2; y = y_hi * 2 + y_lo), z: 8, core: 2. Of those that a mesh axis runs over, the one named last changes fastest.
Arguments:
- psi: bfloat16 [32, 512, 512], P('sec', 'op'), may hold values from -6 to 6
- left_ops: bfloat16 [64, 32, 512, 512], P('op', 'sec'), may hold values from -0.25 to 0.25
- right_ops: bfloat16 [64, 32, 512, 512], P('op', 'sec'), may hold values from -0.03125 to 0.03125
- conn: int32 [64, 32], P('op', 'sec'), may hold values from 0 to 31, as said below
- dims: int32 [32], P('sec'), may hold values from 128 to 512
Outputs:
- sigma: bfloat16 [32, 512, 512], P('sec', 'op')
Inputs may be any that keep to these rules, and one draw needn't show every extreme that they name: conn[k, s] lies in the same group of 2 consecutive sectors as s or in the next group, cyclically over the 32 sectors; both occur.
All inputs are finite; a program needn't handle non-finite values.
Results may differ from a plain program's by a relative error of at most 0.0049.
Values may be sent and summed in bfloat16 or wider, within the bound.
No kernel may reach another device: no remote copies, remote signals or barrier semaphores. Data moves between devices by JAX's collectives and lax.ppermute only.
A program may use at most 64 MiB of HBM per device.

v0:
```python
import jax
import jax.numpy as jnp
from jax import lax
from jax.sharding import Mesh
from jax.sharding import PartitionSpec as P

OP = ("op_0", "op_1", "op_2")


def in_blocks(x, dim, count):
    before, after = (x.shape[:dim], x.shape[dim + 1 :])
    return jnp.moveaxis(x.reshape(*before, count, -1, *after), dim, 0)


def sent_and_summed(x, axis, dim):
    tiles = in_blocks(x, dim, lax.axis_size(axis))
    arrived = lax.all_to_all(tiles, axis, split_axis=0, concat_axis=0, tiled=True)
    return arrived.sum(axis=0)


def sum_in_two_steps(x, axes, dim):
    far, near = axes
    tiles = in_blocks(x, dim, lax.axis_size(far))
    nearer = sent_and_summed(tiles, near, dim + 1)
    arrived = lax.all_to_all(nearer, far, split_axis=0, concat_axis=0, tiled=True)
    return arrived.sum(axis=0)


def side_by_side(arrays, axis, dim, along):
    widths = [a.shape[along] for a in arrays]
    both = jnp.concatenate(arrays, axis=along)
    whole = sum_in_two_steps(both, axis, dim)
    return tuple(jnp.split(whole, [sum(widths[:k]) for k in range(1, len(widths))], axis=along))


def from_behind(block, axis, distance):
    devices = range(lax.axis_size(axis))
    route = [((i - distance) % len(devices), i) for i in devices]
    return lax.ppermute(block, axis, route)


def row_mask(dims, row_start, rows, width):
    row_ids = row_start + jnp.arange(rows, dtype=jnp.int32)
    col_ids = jnp.arange(width, dtype=jnp.int32)
    return (row_ids[None, :, None] < dims[:, None, None]) & (
        col_ids[None, None, :] < dims[:, None, None]
    )


def on_device(psi, left_ops, right_ops, conn, dims):
    sdev, rows, width = psi.shape
    row_start = lax.axis_index(OP) * rows
    masked = jnp.where(row_mask(dims, row_start, rows, width), psi, jnp.zeros_like(psi))
    gathered = lax.all_gather(masked, OP, axis=1, tiled=True)
    half = jnp.einsum(
        "ksij,sjm->ksim", left_ops, gathered, preferred_element_type=jnp.float32
    ).astype(jnp.bfloat16)
    term = jnp.einsum("ksim,ksnm->ksin", half, right_ops, preferred_element_type=jnp.float32)
    group = lax.axis_index("sec")
    slot = conn % sdev
    elsewhere = conn // sdev != group
    slots = jnp.arange(sdev, dtype=jnp.int32)
    hits = slot[:, :, None] == slots[None, None, :]
    own_hot = (hits & ~elsewhere[:, :, None]).astype(jnp.float32)
    next_hot = (hits & elsewhere[:, :, None]).astype(jnp.float32)
    own = jnp.einsum("kst,ksin->tin", own_hot, term, precision=lax.Precision.HIGHEST)
    onward = jnp.einsum("kst,ksin->tin", next_hot, term, precision=lax.Precision.HIGHEST)
    own_rows, onward_rows = side_by_side((own, onward), (("op_0", "op_1"), "op_2"), 1, 0)
    summed = own_rows + from_behind(onward_rows, "sec", 1)
    summed = jnp.where(row_mask(dims, row_start, rows, width), summed, jnp.zeros_like(summed))
    return summed.astype(jnp.bfloat16)


def solution(mesh):
    finer = Mesh(mesh.devices.reshape(4, 4, 2, mesh.shape["sec"]), ("op_0", "op_1", "op_2", "sec"))
    in_specs = (
        P("sec", OP, None),
        P(OP, "sec", None, None),
        P(OP, "sec", None, None),
        P(OP, "sec"),
        P("sec"),
    )
    out_specs = P("sec", OP, None)
    return jax.shard_map(
        on_device, mesh=finer, in_specs=in_specs, out_specs=out_specs, check_vma=False
    )
```

profile of v0, /device:TPU:6, one launch (start us, length us, event | category | flops | bytes accessed | tf_op | source)
XLA Modules:
  0.0 198.3 jit_solution(11831326014869320493)
XLA Ops:
  6.5 0.0 copy-start
  6.5 0.0 all-gather.2.cloned.1.call-start
  6.5 0.9 iota_compare_fusion
  7.4 0.7 broadcast_compare_fusion.2
  8.1 1.4 and_select_fusion.1
  9.6 0.0 all-gather.2.cloned.1.call-update
  9.6 0.7 and_select_fusion.3
  10.3 0.7 fusion.27
  11.0 60.2 %all-gather.2.cloned.1.call-done = bf16[2,512,512]{2,1,0:T(8,128)(2,1)} async-done(((bf16[2,16,512]{2,1,0:T(8,128)(2,1)}), bf16[2,512,512]{2,1,0:T(8,128)(2,1)}) %all-gather.2.cloned.1.call-update) | async-done | bytes 1048592 | tf_op jit(solution)/shard_map/all_gather | solution.py:54
  71.2 0.0 copy-done
  71.2 6.4 %fusion.4 = f32[2,2,512,512]{3,2,1,0:T(8,128)} fusion(bf16[2,2,512,512]{3,2,1,0:T(8,128)(2,1)S(1)} %copy-done, bf16[2,2,512,512]{3,2,1,0:T(8,128)(2,1)} %param.6, bf16[2,512,512]{2,1,0:T(8,128)(2,1)} %all-gather.2.cloned.1.call-done), kind=kOutput, calls=%fused_computation.5 | convolution fusion | flops 2148532224 | bytes 9437184 | tf_op jit(solution)/shard_map/ksim,ksnm->ksin/dot_general | solution.py:58
  77.6 0.0 copy-start.1
  77.6 14.6 %fusion.12 = f32[2,512,512]{2,0,1:T(2,128)S(1)} fusion(f32[2,2,512,512]{3,2,1,0:T(8,128)} %fusion.4, pred[2,2]{1,0:T(4,128)(4,1)S(1)} %get-tuple-element.6, s32[2,2]{1,0:T(2,128)S(1)} %and_select_fusion.3), kind=kOutput, calls=%fused_computation.10 | convolution fusion | flops 25165840 | bytes 6291476 | tf_op jit(solution)/shard_map/kst,ksin->tin/dot_general | solution.py:67
  92.1 0.0 copy-done.1
  92.1 9.7 %fusion.9 = f32[2,512,512]{2,0,1:T(2,128)S(1)} fusion(f32[2,2,512,512]{3,2,1,0:T(8,128)S(1)} %copy-done.1, pred[2,2]{1,0:T(4,128)(4,1)S(1)} %get-tuple-element.5, s32[2,2]{1,0:T(2,128)S(1)} %and_select_fusion.3), kind=kOutput, calls=%fused_computation.9 | convolution fusion | flops 25165840 | bytes 6291476 | tf_op jit(solution)/shard_map/kst,ksin->tin/dot_general | solution.py:66
  101.8 1.9 pad_maximum_fusion
  103.7 1.3 copy.20
  105.0 3.6 %copy.21 = f32[2,16,4,16,512]{4,2,3,1,0:T(4,128)S(1)} copy(f32[2,16,4,16,512]{4,3,0,2,1:T(8,128)S(1)} %bitcast.28) | data formatting | bytes 8388608 | tf_op jit(solution)/shard_map/transpose | solution.py:12
  108.6 8.2 %all_to_all.10 = f32[2,16,4,16,512]{4,2,3,1,0:T(4,128)} all-to-all(f32[2,16,4,16,512]{4,2,3,1,0:T(4,128)S(1)} %copy.21), channel_id=1, replica_groups=mesh['op_0'=4,'op_1'=4,'op_2'=2,'sec'=16] {'op_2'}, dimensions={0} | all-to-all | bytes 8388608 | tf_op jit(solution)/shard_map/all_to_all | solution.py:17
  116.8 5.3 %reduce_sum.18 = f32[16,4,16,512]{3,1,2,0:T(4,128)} reduce(f32[2,16,4,16,512]{4,2,3,1,0:T(4,128)} %all_to_all.10, f32[]{:T(128)} %constant.53.clone.1), dimensions={0}, to_apply=%region_0.1 | reduce | flops 524288 | bytes 6291460 | tf_op jit(solution)/shard_map/reduce_sum | solution.py:18
  122.1 58.4 %all_to_all.11 = f32[16,4,16,512]{3,1,2,0:T(4,128)} all-to-all(f32[16,4,16,512]{3,1,2,0:T(4,128)} %reduce_sum.18), channel_id=1, replica_groups=mesh['op_0'=4,'op_1'=4,'op_2'=2,'sec'=16] {'op_0','op_1'}, dimensions={0} | all-to-all | bytes 4194304 | tf_op jit(solution)/shard_map/all_to_all | solution.py:25
  180.4 1.9 reduce_sum.19
  182.4 0.1 fusion.29
  182.5 1.9 collective-permute-start
  184.4 6.3 %collective-permute-done = f32[2,16,512]{2,1,0:T(8,128)S(1)} collective-permute-done((f32[2,16,512]{2,1,0:T(8,128)S(1)}, f32[2,16,512]{2,1,0:T(8,128)S(1)}, u32[]{:S(2)}, u32[]{:S(2)}) %collective-permute-start) | collective-permute-done | bytes 65568 | tf_op jit(solution)/shard_map/ppermute | solution.py:39
  190.7 0.7 fusion.17
  (2 shorter events, 0.0 us)
Async XLA Ops:
  6.5 64.7 %copy-start = (bf16[2,2,512,512]{3,2,1,0:T(8,128)(2,1)S(1)}, bf16[2,2,512,512]{3,2,1,0:T(8,128)(2,1)}, u32[]{:S(2)}) copy-start(bf16[2,2,512,512]{3,2,1,0:T(8,128)(2,1)} %param.7) | copy-start | bytes 6291460
  6.5 64.6 %all-gather.2.cloned.1.call-start = ((), (), s32[]{:S(2)}) async-start(), calls=%async_computation.2 | async-start | bytes 1081344 | tf_op jit(solution)/shard_map/all_gather | solution.py:54
  77.6 14.6 %copy-start.1 = (f32[2,2,512,512]{3,2,1,0:T(8,128)S(1)}, f32[2,2,512,512]{3,2,1,0:T(8,128)}, u32[]{:S(2)}) copy-start(f32[2,2,512,512]{3,2,1,0:T(8,128)} %fusion.4) | copy-start | bytes 12582916
  182.5 8.3 %collective-permute-start = (f32[2,16,512]{2,1,0:T(8,128)S(1)}, f32[2,16,512]{2,1,0:T(8,128)S(1)}, u32[]{:S(2)}, u32[]{:S(2)}) collective-permute-start(f32[2,16,512]{2,1,0:T(8,128)S(1)} %copy.30), channel_id=1, source_target_pairs={{15,0},{0,1},{1,2},{2,3},{3,4},{4,5},{5,6},{6,7},{7,8},{8,9},{9,10... | collective-permute-start | bytes 196616 | tf_op jit(solution)/shard_map/ppermute | solution.py:39
Sparse Core Ops, SparseCore 0:
  10.6 60.5 all-gather.1
where the time goes:
time: 199 us; the launch traced here: 198 us
  waiting for transfers between devices  66.5 us (33%)
  blocking collectives  66.5 us (33%)
  matrix products  30.6 us (15%)
  other arithmetic  14.2 us (7%)
  between operations  13.5 us (7%)
  local copies, waits for them, and re-layouts  4.98 us (3%)
    all_gather x1, waiting for transfers between devices, on_device(): gathered = lax.all_gather(masked, OP, axis=1, tiled=True)  60.2 us
    all_to_all x1, blocking collectives, sum_in_two_steps(): lax.all_to_all(nearer, far, split_axis=0, concat_axis=0, tiled=True)  58.4 us
    dot_general x1, matrix products, on_device(): jnp.einsum('kst,ksin->tin', next_hot, term, precision=lax.Precision.HIGHEST)  14.6 us
    dot_general x1, matrix products, on_device(): jnp.einsum('kst,ksin->tin', own_hot, term, precision=lax.Precision.HIGHEST)  9.66 us
    all_to_all x1, blocking collectives, sent_and_summed(): lax.all_to_all(tiles, axis, split_axis=0, concat_axis=0, tiled=True)  8.16 us
    dot_general x1, matrix products, on_device(): jnp.einsum('ksim,ksnm->ksin', half, right_ops, preferred_element_type=jnp...  6.38 us
    ppermute x1, waiting for transfers between devices, from_behind(): return lax.ppermute(block, axis, route)  6.34 us
    reduce_sum x1, other arithmetic, sent_and_summed(): return arrived.sum(axis=0)  5.27 us
  transfers between devices with their start and end apart: 2, of which 2 were waited for; matrix products, arithmetic and copies ran while one was open for 1% of the time, Pallas kernels for 0%

commit v1 on v0

v1 whole, which is shorter than its diff:
```python
import jax
import jax.numpy as jnp
from jax import lax
from jax.experimental import pallas as pl
from jax.experimental.pallas import tpu as pltpu
from jax.sharding import Mesh
from jax.sharding import PartitionSpec as P

OP = ("x", "y", "c")
F32 = jnp.float32
BF16 = jnp.bfloat16


def exchanged(x, axis):
    return lax.all_to_all(x, axis, split_axis=0, concat_axis=0, tiled=True)


def shared(x, axis):
    return exchanged(jnp.broadcast_to(x[None], (lax.axis_size(axis),) + x.shape), axis)


def from_partner(x):
    return lax.ppermute(x, "c", [(0, 1), (1, 0)])


def from_behind(x):
    n = lax.axis_size("sec")
    return lax.ppermute(x, "sec", [(i, (i + 1) % n) for i in range(n)])


def in_vmem(x):
    return pltpu.with_memory_space_constraint(x, pltpu.VMEM)


def sums_kernel(where_ref, conn_ref, conn2_ref, dims_ref, near_ref, far_ref, left_ref, right_ref, left2_ref, right2_ref, out_ref, psi_ref, rows_ref, half_ref, term_ref, rights_ref, sems):
    kdev, sdev, width, _ = right_ref.shape
    chips, _, tall, _ = near_ref.shape
    group = where_ref[0]
    core = where_ref[1]
    many = chips * tall
    fetches = []
    for whose in range(2):
        for s in range(sdev):
            group_of = []
            for k in range(kdev):
                right = (right_ref, right2_ref)[whose].at[k, s]
                group_of.append(pltpu.make_async_copy(right, rights_ref.at[whose, k, s], sems.at[whose, s, k]))
                if whose == 1:
                    rows = rows_ref.at[s, kdev + k]
                    group_of.append(pltpu.make_async_copy(left2_ref.at[k, s, :, core], rows, sems.at[2, s, k]))
            fetches.append(group_of)
    for group_of in fetches:
        for fetch in group_of:
            fetch.start()
    cols = lax.broadcasted_iota(jnp.int32, (tall, width), 1)
    row = lax.broadcasted_iota(jnp.int32, (tall, width), 0)
    for s in range(sdev):
        size = dims_ref[s]
        inside = cols < size
        for chip in range(chips):
            for ref, seat in ((near_ref, core), (far_ref, 1 - core)):
                start = pl.multiple_of((chip * 2 + seat) * tall, tall)
                kept = jnp.where(inside & (row + start < size), ref[chip, s].astype(F32), 0.0)
                psi_ref[s, pl.ds(start, tall), :] = kept.astype(BF16)
            for k in range(kdev):
                rows_ref[s, k, chip] = left_ref[k, s, chip, core]
    shares = [None] * (2 * kdev * sdev)
    for whose in range(2):
        conns = (conn_ref, conn2_ref)[whose]
        for s in range(sdev):
            for fetch in fetches[whose * sdev + s]:
                fetch.wait()
            left = rows_ref[s, whose * kdev : (whose + 1) * kdev].reshape(kdev * many, width)
            half_ref[...] = jnp.dot(left, psi_ref[s], preferred_element_type=F32).astype(BF16)
            for k in range(kdev):
                n = (whose * sdev + s) * kdev + k
                term_ref[n] = lax.dot_general(
                    half_ref[k * many : (k + 1) * many, :],
                    rights_ref[whose, k, s],
                    (((1,), (1,)), ((), ())),
                    preferred_element_type=F32,
                )
                target = conns[k, s]
                place = target % sdev + jnp.where(target // sdev != group, sdev, 0)
                shares[n] = [jnp.where(place == t, 1.0, 0.0).astype(F32) for t in range(2 * sdev)]
    wide = width // 2
    for chip in range(chips):
        for cut in range(2):
            terms = [term_ref[n, chip * tall : (chip + 1) * tall, cut * wide : (cut + 1) * wide] for n in range(len(shares))]
            for t in range(2 * sdev):
                total = shares[0][t] * terms[0]
                for n in range(1, len(shares)):
                    total = total + shares[n][t] * terms[n]
                out_ref[chip, t, :, cut * wide : (cut + 1) * wide] = total.astype(BF16)


def slot_sums(where, conn, conn2, dims, near, far, left, right, left2, right2):
    kdev, sdev, width, _ = left.shape
    chips, _, tall, _ = near.shape
    smem = pl.BlockSpec(memory_space=pltpu.SMEM)
    vmem = pl.BlockSpec(memory_space=pltpu.VMEM)
    hbm = pl.BlockSpec(memory_space=pltpu.HBM)
    many = chips * tall
    by_row = (kdev, sdev, chips, 2, tall, width)
    return pl.pallas_call(
        sums_kernel,
        in_specs=[smem] * 4 + [vmem] * 3 + [hbm] * 3,
        out_specs=vmem,
        out_shape=pltpu.VMEM((chips, 2 * sdev, tall, width), BF16),
        scratch_shapes=[
            pltpu.VMEM((sdev, width, width), BF16),
            pltpu.VMEM((sdev, 2 * kdev, chips, tall, width), BF16),
            pltpu.VMEM((kdev * many, width), BF16),
            pltpu.VMEM((2 * kdev * sdev, many, width), F32),
            pltpu.VMEM((2, kdev, sdev, width, width), BF16),
            pltpu.SemaphoreType.DMA((3, sdev, kdev)),
        ],
        compiler_params=pltpu.CompilerParams(vmem_limit_bytes=24 * 2**20),
        name="slot_sums",
    )(where, conn, conn2, dims, *(in_vmem(x) for x in (near, far, left.reshape(by_row))), right, left2.reshape(by_row), right2)


def row_mask(dims, row_start, rows, width):
    row_ids = row_start + jnp.arange(rows, dtype=jnp.int32)
    col_ids = jnp.arange(width, dtype=jnp.int32)
    return (row_ids[None, :, None] < dims[:, None, None]) & (
        col_ids[None, None, :] < dims[:, None, None]
    )


def sigma_rows(psi, left_ops, right_ops, conn, dims):
    sdev, tall, width = psi.shape
    nx, ny = lax.axis_size("x"), lax.axis_size("y")
    left2 = from_partner(left_ops)
    right2 = from_partner(right_ops)
    conn2 = from_partner(conn)
    by_y = shared(psi, "y").reshape(ny, sdev, tall, width)
    by_x = shared(by_y, "x").reshape(nx * ny, sdev, tall, width)
    other = from_partner(by_x)
    where = jnp.stack([lax.axis_index("sec"), lax.axis_index("c")]).astype(jnp.int32)
    both = slot_sums(where, conn, conn2, dims, by_x, other, left_ops, right_ops, left2, right2)
    both = exchanged(both, "x").reshape(nx, ny, 2 * sdev, tall, width)
    both = both.astype(F32).sum(axis=0).astype(BF16)
    both = exchanged(both, "y").astype(F32).sum(axis=0)
    onward = from_behind(both[sdev:].astype(BF16))
    summed = both[:sdev] + onward.astype(F32)
    row_start = lax.axis_index(OP) * tall
    summed = jnp.where(row_mask(dims, row_start, tall, width), summed, jnp.zeros_like(summed))
    return summed.astype(BF16)


def solution(mesh):
    finer = Mesh(mesh.devices.reshape(4, 4, 2, mesh.shape["sec"]), OP + ("sec",))
    in_specs = (
        P("sec", OP, None),
        P(OP, "sec", None, None),
        P(OP, "sec", None, None),
        P(OP, "sec"),
        P("sec"),
    )
    out_specs = P("sec", OP, None)
    return jax.shard_map(sigma_rows, mesh=finer, in_specs=in_specs, out_specs=out_specs, check_vma=False)
```

time: 199 us -> 91.7 us (0.46)
  waiting for transfers between devices: 66.5 us -> 21.2 us
  matrix products: 30.6 us -> 0 us
  blocking collectives: 66.5 us -> 44.9 us
  between operations: 13.5 us -> 0.15 us
  starting transfers between devices: 1.92 us -> 15 us
  other arithmetic: 14.2 us -> 1.89 us
  Pallas kernels: 0 us -> 4.86 us
  local copies, waits for them, and re-layouts: 4.98 us -> 2.42 us
    all_gather x1 -> x0, waiting for transfers between devices: 60.2 us -> none  [on_device(): gathered = lax.all_gather(masked, OP, axis=1, tiled=True)]
    dot_general x3 -> x0, matrix products: 30.6 us -> none  [the longest x1 14.6 us: on_device(): jnp.einsum('kst,ksin->tin', next_hot, term, precision=lax.Precision.HIGHEST)]
    all_to_all x2 -> x3, blocking collectives: 66.5 us -> 44.9 us  [exchanged(): return lax.all_to_all(x, axis, split_axis=0, concat_axis=0, tiled=True)]
    all_to_all x0 -> x1, waiting for transfers between devices: none -> 10.2 us  [exchanged(): return lax.all_to_all(x, axis, split_axis=0, concat_axis=0, tiled=True)]
    ppermute x1 -> x5, starting transfers between devices: 1.92 us -> 11.6 us  [the longest x4 8.78 us: from_partner(): return lax.ppermute(x, 'c', [(0, 1), (1, 0)])]
    reduce_sum x2, other arithmetic: 7.21 us -> 0.97 us  [the longest x1 0.94 us: sigma_rows(): both = both.astype(F32).sum(axis=0).astype(BF16)]
    pallas_call x0 -> x1, Pallas kernels: none -> 4.86 us  [slot_sums(): pl.pallas_call(sums_kernel, in_specs=[smem] * 4 + [vmem] * 3 + [hbm] * 3,...]
    ppermute x1 -> x5, waiting for transfers between devices: 6.34 us -> 11 us  [the longest x1 10.3 us: from_behind(): return lax.ppermute(x, 'sec', [(i, (i + 1) % n) for i in range(n)])]
  transfers between devices with their start and end apart: 2 -> 6, of which waited for: 2 -> 3; matrix products, arithmetic and copies ran while one was open for 1% -> 1% of each run, Pallas kernels for 0% -> 0%
where the time goes in v1:
time: 91.7 us; the launch traced here: 90.5 us
  blocking collectives  44.9 us (49%)
  waiting for transfers between devices  21.2 us (23%)
  starting transfers between devices  15 us (16%)
  Pallas kernels  4.86 us (5%)
  local copies, waits for them, and re-layouts  2.42 us (3%)
  other arithmetic  1.89 us (2%)
    all_to_all x3, blocking collectives, exchanged(): return lax.all_to_all(x, axis, split_axis=0, concat_axis=0, tiled=True)  44.9 us
    ppermute x1, waiting for transfers between devices, from_behind(): return lax.ppermute(x, 'sec', [(i, (i + 1) % n) for i in range(n)])  10.3 us
    all_to_all x1, waiting for transfers between devices, exchanged(): return lax.all_to_all(x, axis, split_axis=0, concat_axis=0, tiled=True)  10.2 us
    ppermute x4, starting transfers between devices, from_partner(): return lax.ppermute(x, 'c', [(0, 1), (1, 0)])  8.78 us
    pallas_call x1, Pallas kernels, slot_sums(): pl.pallas_call(sums_kernel, in_specs=[smem] * 4 + [vmem] * 3 + [hbm] * 3,...  4.86 us
    all_to_all x1, starting transfers between devices, exchanged(): return lax.all_to_all(x, axis, split_axis=0, concat_axis=0, tiled=True)  3.4 us
    ppermute x1, starting transfers between devices, from_behind(): return lax.ppermute(x, 'sec', [(i, (i + 1) % n) for i in range(n)])  2.8 us
  transfers between devices with their start and end apart: 6, of which 3 were waited for; matrix products, arithmetic and copies ran while one was open for 1% of the time, Pallas kernels for 0%

profile of v1, /device:TPU:6, one launch (start us, length us, event | category | flops | bytes accessed | tf_op | source)
XLA Modules:
  0.0 90.5 jit_solution(11778924504398722307)
XLA Ops:
  0.0 0.0 copy-start
  0.0 0.0 copy-start.3
  0.0 0.0 copy-start.2
  0.0 2.1 %collective-permute-start.2 = (bf16[2,2,512,512]{3,2,1,0:T(8,128)(2,1)}, bf16[2,2,512,512]{3,2,1,0:T(8,128)(2,1)}, u32[]{:S(2)}, u32[]{:S(2)}) collective-permute-start(bf16[2,2,512,512]{3,2,1,0:T(8,128)(2,1)} %param.6), channel_id=1, source_target_pairs={{0,16},{16,0},{1,17},{17,1},{2,18},{18,2},{3,19},{19,3},{4,20},{20... | collective-permute-start | bytes 6291464 | tf_op jit(solution)/shard_map/ppermute | solution.py:23
  2.1 2.4 %collective-permute-start.3 = (bf16[2,2,512,512]{3,2,1,0:T(8,128)(2,1)}, bf16[2,2,512,512]{3,2,1,0:T(8,128)(2,1)}, u32[]{:S(2)}, u32[]{:S(2)}) collective-permute-start(bf16[2,2,512,512]{3,2,1,0:T(8,128)(2,1)} %right_ref.1), channel_id=1, source_target_pairs={{0,16},{16,0},{1,17},{17,1},{2,18},{18,2},{3,19},{19,3},{4,20},{20... | collective-permute-start | bytes 6291464 | tf_op jit(solution)/shard_map/ppermute | solution.py:23
  4.5 0.8 broadcast_in_dim.6
  5.3 16.0 %all_to_all.20 = bf16[4,2,16,512]{3,2,1,0:T(8,128)(2,1)S(1)} all-to-all(bf16[4,2,16,512]{3,2,1,0:T(8,128)(2,1)S(1)} %broadcast_in_dim.6), channel_id=1, replica_groups=mesh['x'=4,'y'=4,'c'=2,'sec'=16] {'y'}, dimensions={0} | all-to-all | bytes 262144 | tf_op jit(solution)/shard_map/all_to_all | solution.py:15
  21.3 0.1 broadcast_in_dim.7
  21.4 10.6 %all_to_all.21 = bf16[4,4,2,16,512]{4,3,2,1,0:T(8,128)(2,1)S(1)} all-to-all(bf16[4,4,2,16,512]{4,3,2,1,0:T(8,128)(2,1)S(1)} %broadcast_in_dim.7), channel_id=1, replica_groups=mesh['x'=4,'y'=4,'c'=2,'sec'=16] {'x'}, dimensions={0} | all-to-all | bytes 1048576 | tf_op jit(solution)/shard_map/all_to_all | solution.py:15
  31.9 1.9 %collective-permute-start.1 = (bf16[16,2,16,512]{3,2,1,0:T(8,128)(2,1)S(1)}, bf16[16,2,16,512]{3,2,1,0:T(8,128)(2,1)S(1)}, u32[]{:S(2)}, u32[]{:S(2)}) collective-permute-start(bf16[16,2,16,512]{3,2,1,0:T(8,128)(2,1)S(1)} %bitcast.6), channel_id=1, source_target_pairs={{0,16},{16,0},{1,17},{17,1},{2,18},{18,2},{3,19},{19,3},{4,20},{20... | collective-permute-start | bytes 1572872 | tf_op jit(solution)/shard_map/ppermute | solution.py:23
  33.9 0.0 copy-done.3
  33.9 2.4 %collective-permute-start = (s32[2,2]{1,0:T(2,128)S(1)}, s32[2,2]{1,0:T(2,128)S(1)}, u32[]{:S(2)}, u32[]{:S(2)}) collective-permute-start(s32[2,2]{1,0:T(2,128)S(1)} %copy-done.3), channel_id=1, source_target_pairs={{0,16},{16,0},{1,17},{17,1},{2,18},{18,2},{3,19},{19,3},{4,20},{20... | collective-permute-start | bytes 56 | tf_op jit(solution)/shard_map/ppermute | solution.py:23
  36.3 0.1 pad_add_fusion.where_ref
  36.4 0.7 collective-permute-done.conn2_ref
  37.1 0.0 collective-permute-done.1.far_ref
  37.1 0.0 collective-permute-done.2
  37.1 0.0 collective-permute-done.3.right2_ref
  37.1 0.0 copy-done
  37.1 0.0 copy-done.2
  37.1 0.0 copy-start.1
  37.1 1.6 %copy-done.1 = bf16[2,2,512,512]{3,2,1,0:T(8,128)(2,1)S(1)} copy-done((bf16[2,2,512,512]{3,2,1,0:T(8,128)(2,1)S(1)}, bf16[2,2,512,512]{3,2,1,0:T(8,128)(2,1)}, u32[]{:S(2)}) %copy-start.1) | copy-done | bytes 2097176
  38.7 4.9 %slot_sums.1 = bf16[16,4,16,512]{3,2,1,0:T(8,128)(2,1)S(1)} custom-call(s32[2]{0:T(128)S(1)} %pad_add_fusion.where_ref, s32[2,2]{1,0:T(2,128)S(1)} %copy-done.3, s32[2,2]{1,0:T(2,128)S(1)} %collective-permute-done.conn2_ref, s32[2]{0:T(128)S(1)} %copy-done.2, bf16[16,2,16,512]{3,2,1,0:T(8,128)(2,1)S(1)} %bitcast.7, ...), custom_call_target="tpu_custom_call" | custom-call | tf_op jit(solution)/shard_map/slot_sums/pallas_call | solution.py:105
  43.6 18.3 %all_to_all.22 = bf16[16,4,16,512]{3,2,1,0:T(8,128)(2,1)S(1)} all-to-all(bf16[16,4,16,512]{3,2,1,0:T(8,128)(2,1)S(1)} %slot_sums.1), channel_id=1, replica_groups=mesh['x'=4,'y'=4,'c'=2,'sec'=16] {'x'}, dimensions={0} | all-to-all | bytes 2097152 | tf_op jit(solution)/shard_map/all_to_all | solution.py:15
  61.9 0.9 %reduce_sum.21 = bf16[4,4,16,512]{3,2,1,0:T(8,128)(2,1)} reduce(bf16[4,4,4,16,512]{4,3,2,1,0:T(8,128)(2,1)S(1)} %bitcast.9, bf16[]{:T(256)} %constant.28.clone.1), dimensions={0}, to_apply=%region_0.0 | reduce | flops 393216 | bytes 1310722 | tf_op jit(solution)/shard_map/reduce_sum | solution.py:143
  62.8 3.4 %all-to-all-start.3 = ((bf16[4,4,16,512]{3,2,1,0:T(8,128)(2,1)}), bf16[4,4,16,512]{3,2,1,0:T(8,128)(2,1)S(1)}, u32[]{:S(2)}, u32[]{:S(2)}) async-start(bf16[4,4,16,512]{3,2,1,0:T(8,128)(2,1)} %reduce_sum.21), calls=%async_computation.3 | async-start | bytes 524288 | tf_op jit(solution)/shard_map/all_to_all | solution.py:15
  66.3 0.1 iota_compare_fusion
  66.3 10.2 %all-to-all-done.3 = bf16[4,4,16,512]{3,2,1,0:T(8,128)(2,1)S(1)} async-done(((bf16[4,4,16,512]{3,2,1,0:T(8,128)(2,1)}), bf16[4,4,16,512]{3,2,1,0:T(8,128)(2,1)S(1)}, u32[]{:S(2)}, u32[]{:S(2)}) %all-to-all-start.3) | async-done | bytes 262176 | tf_op jit(solution)/shard_map/all_to_all | solution.py:15
  76.6 2.8 %collective-permute-start.4 = (bf16[2,16,512]{2,1,0:T(8,128)(2,1)S(1)}, bf16[2,16,512]{2,1,0:T(8,128)(2,1)S(1)}, u32[]{:S(2)}, u32[]{:S(2)}) collective-permute-start(bf16[2,16,512]{2,1,0:T(8,128)(2,1)S(1)} %slice.17), channel_id=1, source_target_pairs={{0,1},{1,2},{2,3},{3,4},{4,5},{5,6},{6,7},{7,8},{8,9},{9,10},{10,1... | collective-permute-start | bytes 98312 | tf_op jit(solution)/shard_map/ppermute | solution.py:28
  79.4 0.1 broadcast_compare_fusion
  79.5 10.3 %collective-permute-done.4 = bf16[2,16,512]{2,1,0:T(8,128)(2,1)S(1)} collective-permute-done((bf16[2,16,512]{2,1,0:T(8,128)(2,1)S(1)}, bf16[2,16,512]{2,1,0:T(8,128)(2,1)S(1)}, u32[]{:S(2)}, u32[]{:S(2)}) %collective-permute-start.4) | collective-permute-done | bytes 32800 | tf_op jit(solution)/shard_map/ppermute | solution.py:28
  89.8 0.7 fusion.1
  (3 shorter events, 0.0 us)
Async XLA Ops:
  0.0 37.1 %copy-start = (bf16[2,2,512,512]{3,2,1,0:T(8,128)(2,1)S(1)}, bf16[2,2,512,512]{3,2,1,0:T(8,128)(2,1)}, u32[]{:S(2)}) copy-start(bf16[2,2,512,512]{3,2,1,0:T(8,128)(2,1)} %param.6) | copy-start | bytes 6291460
  0.0 33.9 %copy-start.3 = (s32[2,2]{1,0:T(2,128)S(1)}, s32[2,2]{1,0:T(2,128)}, u32[]{:S(2)}) copy-start(s32[2,2]{1,0:T(2,128)} %conn_ref.1) | copy-start | bytes 52
  0.0 37.1 %copy-start.2 = (s32[2]{0:T(128)S(1)}, s32[2]{0:T(128)}, u32[]{:S(2)}) copy-start(s32[2]{0:T(128)} %dims_ref.1) | copy-start | bytes 28
  0.0 37.1 %collective-permute-start.2 = (bf16[2,2,512,512]{3,2,1,0:T(8,128)(2,1)}, bf16[2,2,512,512]{3,2,1,0:T(8,128)(2,1)}, u32[]{:S(2)}, u32[]{:S(2)}) collective-permute-start(bf16[2,2,512,512]{3,2,1,0:T(8,128)(2,1)} %param.6), channel_id=1, source_target_pairs={{0,16},{16,0},{1,17},{17,1},{2,18},{18,2},{3,19},{19,3},{4,20},{20... | collective-permute-start | bytes 6291464 | tf_op jit(solution)/shard_map/ppermute | solution.py:23
  2.1 35.0 %collective-permute-start.3 = (bf16[2,2,512,512]{3,2,1,0:T(8,128)(2,1)}, bf16[2,2,512,512]{3,2,1,0:T(8,128)(2,1)}, u32[]{:S(2)}, u32[]{:S(2)}) collective-permute-start(bf16[2,2,512,512]{3,2,1,0:T(8,128)(2,1)} %right_ref.1), channel_id=1, source_target_pairs={{0,16},{16,0},{1,17},{17,1},{2,18},{18,2},{3,19},{19,3},{4,20},{20... | collective-permute-start | bytes 6291464 | tf_op jit(solution)/shard_map/ppermute | solution.py:23
  31.9 5.1 %collective-permute-start.1 = (bf16[16,2,16,512]{3,2,1,0:T(8,128)(2,1)S(1)}, bf16[16,2,16,512]{3,2,1,0:T(8,128)(2,1)S(1)}, u32[]{:S(2)}, u32[]{:S(2)}) collective-permute-start(bf16[16,2,16,512]{3,2,1,0:T(8,128)(2,1)S(1)} %bitcast.6), channel_id=1, source_target_pairs={{0,16},{16,0},{1,17},{17,1},{2,18},{18,2},{3,19},{19,3},{4,20},{20... | collective-permute-start | bytes 1572872 | tf_op jit(solution)/shard_map/ppermute | solution.py:23
  33.9 3.2 %collective-permute-start = (s32[2,2]{1,0:T(2,128)S(1)}, s32[2,2]{1,0:T(2,128)S(1)}, u32[]{:S(2)}, u32[]{:S(2)}) collective-permute-start(s32[2,2]{1,0:T(2,128)S(1)} %copy-done.3), channel_id=1, source_target_pairs={{0,16},{16,0},{1,17},{17,1},{2,18},{18,2},{3,19},{19,3},{4,20},{20... | collective-permute-start | bytes 56 | tf_op jit(solution)/shard_map/ppermute | solution.py:23
  37.1 1.6 %copy-start.1 = (bf16[2,2,512,512]{3,2,1,0:T(8,128)(2,1)S(1)}, bf16[2,2,512,512]{3,2,1,0:T(8,128)(2,1)}, u32[]{:S(2)}) copy-start(bf16[2,2,512,512]{3,2,1,0:T(8,128)(2,1)} %right_ref.1) | copy-start | bytes 6291460
  62.8 13.7 %all-to-all-start.3 = ((bf16[4,4,16,512]{3,2,1,0:T(8,128)(2,1)}), bf16[4,4,16,512]{3,2,1,0:T(8,128)(2,1)S(1)}, u32[]{:S(2)}, u32[]{:S(2)}) async-start(bf16[4,4,16,512]{3,2,1,0:T(8,128)(2,1)} %reduce_sum.21), calls=%async_computation.3 | async-start | bytes 524288 | tf_op jit(solution)/shard_map/all_to_all | solution.py:15
  76.6 13.2 %collective-permute-start.4 = (bf16[2,16,512]{2,1,0:T(8,128)(2,1)S(1)}, bf16[2,16,512]{2,1,0:T(8,128)(2,1)S(1)}, u32[]{:S(2)}, u32[]{:S(2)}) collective-permute-start(bf16[2,16,512]{2,1,0:T(8,128)(2,1)S(1)} %slice.17), channel_id=1, source_target_pairs={{0,1},{1,2},{2,3},{3,4},{4,5},{5,6},{6,7},{7,8},{8,9},{9,10},{10,1... | collective-permute-start | bytes 98312 | tf_op jit(solution)/shard_map/ppermute | solution.py:28

commit v2 on v1

--- a/solution.py
+++ b/solution.py
@@ -32,7 +32,11 @@
     return pltpu.with_memory_space_constraint(x, pltpu.VMEM)
 
 
-def sums_kernel(where_ref, conn_ref, conn2_ref, dims_ref, near_ref, far_ref, left_ref, right_ref, left2_ref, right2_ref, out_ref, psi_ref, rows_ref, half_ref, term_ref, rights_ref, sems):
+def in_hbm(x):
+    return pltpu.with_memory_space_constraint(x, pltpu.HBM)
+
+
+def sums_kernel(where_ref, conn_ref, conn2_ref, dims_ref, near_ref, far_ref, left_ref, right_ref, left2_ref, right2_ref, own_ref, onward_ref, psi_ref, rows_ref, half_ref, term_ref, rights_ref, sems):
     kdev, sdev, width, _ = right_ref.shape
     chips, _, tall, _ = near_ref.shape
     group = where_ref[0]
@@ -91,7 +95,8 @@
                 total = shares[0][t] * terms[0]
                 for n in range(1, len(shares)):
                     total = total + shares[n][t] * terms[n]
-                out_ref[chip, t, :, cut * wide : (cut + 1) * wide] = total.astype(BF16)
+                out_ref = (own_ref, onward_ref)[t // sdev]
+                out_ref[chip, t % sdev, :, cut * wide : (cut + 1) * wide] = total.astype(BF16)
 
 
 def slot_sums(where, conn, conn2, dims, near, far, left, right, left2, right2):
@@ -105,8 +110,8 @@
     return pl.pallas_call(
         sums_kernel,
         in_specs=[smem] * 4 + [vmem] * 3 + [hbm] * 3,
-        out_specs=vmem,
-        out_shape=pltpu.VMEM((chips, 2 * sdev, tall, width), BF16),
+        out_specs=[vmem] * 2,
+        out_shape=[pltpu.VMEM((chips, sdev, tall, width), BF16)] * 2,
         scratch_shapes=[
             pltpu.VMEM((sdev, width, width), BF16),
             pltpu.VMEM((sdev, 2 * kdev, chips, tall, width), BF16),
@@ -117,7 +122,7 @@
         ],
         compiler_params=pltpu.CompilerParams(vmem_limit_bytes=24 * 2**20),
         name="slot_sums",
-    )(where, conn, conn2, dims, *(in_vmem(x) for x in (near, far, left.reshape(by_row))), right, left2.reshape(by_row), right2)
+    )(where, conn, conn2, dims, *(in_vmem(x) for x in (near, far, left.reshape(by_row))), *(in_hbm(x) for x in (right, left2.reshape(by_row), right2)))
 
 
 def row_mask(dims, row_start, rows, width):
@@ -138,12 +143,12 @@
     by_x = shared(by_y, "x").reshape(nx * ny, sdev, tall, width)
     other = from_partner(by_x)
     where = jnp.stack([lax.axis_index("sec"), lax.axis_index("c")]).astype(jnp.int32)
-    both = slot_sums(where, conn, conn2, dims, by_x, other, left_ops, right_ops, left2, right2)
-    both = exchanged(both, "x").reshape(nx, ny, 2 * sdev, tall, width)
-    both = both.astype(F32).sum(axis=0).astype(BF16)
-    both = exchanged(both, "y").astype(F32).sum(axis=0)
-    onward = from_behind(both[sdev:].astype(BF16))
-    summed = both[:sdev] + onward.astype(F32)
+    own, onward = slot_sums(where, conn, conn2, dims, by_x, other, left_ops, right_ops, left2, right2)
+    by_chip = (nx, ny, sdev, tall, width)
+    onward = exchanged(onward, "x").reshape(by_chip).astype(F32).sum(axis=0).astype(BF16)
+    own = exchanged(own, "x").reshape(by_chip).astype(F32).sum(axis=0)
+    onward = from_behind(onward)
+    summed = exchanged((own + onward.astype(F32)).astype(BF16), "y").astype(F32).sum(axis=0)
     row_start = lax.axis_index(OP) * tall
     summed = jnp.where(row_mask(dims, row_start, tall, width), summed, jnp.zeros_like(summed))
     return summed.astype(BF16)

time: 91.7 us -> 89.5 us (0.976)
  blocking collectives: 44.9 us -> 39.3 us
  starting transfers between devices: 15 us -> 20.4 us
  local copies, waits for them, and re-layouts: 2.42 us -> 0.83 us
    all_to_all x3, blocking collectives: 44.9 us -> 39.3 us  [exchanged(): return lax.all_to_all(x, axis, split_axis=0, concat_axis=0, tiled=True)]
    all_to_all x1 -> x2, starting transfers between devices: 3.4 us -> 8.83 us  [exchanged(): return lax.all_to_all(x, axis, split_axis=0, concat_axis=0, tiled=True)]
    ppermute x1, waiting for transfers between devices: 10.3 us -> 7.1 us  [from_behind(): return lax.ppermute(x, 'sec', [(i, (i + 1) % n) for i in range(n)])]
    all_to_all x1 -> x2, waiting for transfers between devices: 10.2 us -> 12.9 us  [exchanged(): return lax.all_to_all(x, axis, split_axis=0, concat_axis=0, tiled=True)]
    unnamed x8, local copies, waits for them, and re-layouts: 1.6 us -> 0.02 us
  transfers between devices with their start and end apart: 6 -> 7, of which waited for: 3 -> 4; matrix products, arithmetic and copies ran while one was open for 1% -> 1% of each run, Pallas kernels for 0% -> 0%
where the time goes in v2:
time: 89.5 us; the launch traced here: 88.9 us
  blocking collectives  39.3 us (44%)
  waiting for transfers between devices  20.7 us (23%)
  starting transfers between devices  20.4 us (23%)
  Pallas kernels  5.77 us (6%)
  other arithmetic  1.77 us (2%)
    all_to_all x3, blocking collectives, exchanged(): return lax.all_to_all(x, axis, split_axis=0, concat_axis=0, tiled=True)  39.3 us
    all_to_all x2, waiting for transfers between devices, exchanged(): return lax.all_to_all(x, axis, split_axis=0, concat_axis=0, tiled=True)  12.9 us
    all_to_all x2, starting transfers between devices, exchanged(): return lax.all_to_all(x, axis, split_axis=0, concat_axis=0, tiled=True)  8.83 us
    ppermute x4, starting transfers between devices, from_partner(): return lax.ppermute(x, 'c', [(0, 1), (1, 0)])  8.78 us
    ppermute x1, waiting for transfers between devices, from_behind(): return lax.ppermute(x, 'sec', [(i, (i + 1) % n) for i in range(n)])  7.1 us
    pallas_call x1, Pallas kernels, slot_sums(): pl.pallas_call(sums_kernel, in_specs=[smem] * 4 + [vmem] * 3 + [hbm] * 3,...  5.77 us
    ppermute x1, starting transfers between devices, from_behind(): return lax.ppermute(x, 'sec', [(i, (i + 1) % n) for i in range(n)])  2.79 us
  transfers between devices with their start and end apart: 7, of which 4 were waited for; matrix products, arithmetic and copies ran while one was open for 1% of the time, Pallas kernels for 0%

profile of v2, /device:TPU:6, one launch (start us, length us, event | category | flops | bytes accessed | tf_op | source)
XLA Modules:
  0.0 88.9 jit_solution(501788709502885889)
XLA Ops:
  0.0 0.0 copy-start
  0.0 0.0 copy-start.3
  0.0 0.0 copy-start.2
  0.0 2.1 %collective-permute-start.2 = (bf16[2,2,512,512]{3,2,1,0:T(8,128)(2,1)}, bf16[2,2,512,512]{3,2,1,0:T(8,128)(2,1)}, u32[]{:S(2)}, u32[]{:S(2)}) collective-permute-start(bf16[2,2,512,512]{3,2,1,0:T(8,128)(2,1)} %param.6), channel_id=1, source_target_pairs={{0,16},{16,0},{1,17},{17,1},{2,18},{18,2},{3,19},{19,3},{4,20},{20... | collective-permute-start | bytes 6291464 | tf_op jit(solution)/shard_map/ppermute | solution.py:23
  2.1 2.4 %collective-permute-start.3 = (bf16[2,2,512,512]{3,2,1,0:T(8,128)(2,1)}, bf16[2,2,512,512]{3,2,1,0:T(8,128)(2,1)}, u32[]{:S(2)}, u32[]{:S(2)}) collective-permute-start(bf16[2,2,512,512]{3,2,1,0:T(8,128)(2,1)} %right_ref.1), channel_id=1, source_target_pairs={{0,16},{16,0},{1,17},{17,1},{2,18},{18,2},{3,19},{19,3},{4,20},{20... | collective-permute-start | bytes 6291464 | tf_op jit(solution)/shard_map/ppermute | solution.py:23
  4.5 0.8 broadcast_in_dim.6
  5.3 16.0 %all_to_all.25 = bf16[4,2,16,512]{3,2,1,0:T(8,128)(2,1)S(1)} all-to-all(bf16[4,2,16,512]{3,2,1,0:T(8,128)(2,1)S(1)} %broadcast_in_dim.6), channel_id=1, replica_groups=mesh['x'=4,'y'=4,'c'=2,'sec'=16] {'y'}, dimensions={0} | all-to-all | bytes 262144 | tf_op jit(solution)/shard_map/all_to_all | solution.py:15
  21.4 10.6 %all_to_all.26 = bf16[4,4,2,16,512]{4,3,2,1,0:T(8,128)(2,1)S(1)} all-to-all(bf16[4,4,2,16,512]{4,3,2,1,0:T(8,128)(2,1)S(1)} %broadcast_in_dim.7), channel_id=1, replica_groups=mesh['x'=4,'y'=4,'c'=2,'sec'=16] {'x'}, dimensions={0} | all-to-all | bytes 1048576 | tf_op jit(solution)/shard_map/all_to_all | solution.py:15
  31.9 1.9 %collective-permute-start.1 = (bf16[16,2,16,512]{3,2,1,0:T(8,128)(2,1)S(1)}, bf16[16,2,16,512]{3,2,1,0:T(8,128)(2,1)S(1)}, u32[]{:S(2)}, u32[]{:S(2)}) collective-permute-start(bf16[16,2,16,512]{3,2,1,0:T(8,128)(2,1)S(1)} %bitcast.8), channel_id=1, source_target_pairs={{0,16},{16,0},{1,17},{17,1},{2,18},{18,2},{3,19},{19,3},{4,20},{20... | collective-permute-start | bytes 1572872 | tf_op jit(solution)/shard_map/ppermute | solution.py:23
  33.9 0.0 copy-done.3
  33.9 2.4 %collective-permute-start = (s32[2,2]{1,0:T(2,128)S(1)}, s32[2,2]{1,0:T(2,128)S(1)}, u32[]{:S(2)}, u32[]{:S(2)}) collective-permute-start(s32[2,2]{1,0:T(2,128)S(1)} %copy-done.3), channel_id=1, source_target_pairs={{0,16},{16,0},{1,17},{17,1},{2,18},{18,2},{3,19},{19,3},{4,20},{20... | collective-permute-start | bytes 56 | tf_op jit(solution)/shard_map/ppermute | solution.py:23
  36.3 0.1 pad_add_fusion.where_ref
  36.4 0.7 collective-permute-done.conn2_ref
  37.1 0.0 collective-permute-done.1.far_ref
  37.1 0.0 collective-permute-done.2
  37.1 0.0 collective-permute-done.3.right2_ref
  37.1 0.0 copy-done
  37.1 0.0 copy-done.2
  37.1 5.8 %slot_sums.1 = (bf16[16,2,16,512]{3,2,1,0:T(8,128)(2,1)S(1)}, bf16[16,2,16,512]{3,2,1,0:T(8,128)(2,1)S(1)}) custom-call(s32[2]{0:T(128)S(1)} %pad_add_fusion.where_ref, s32[2,2]{1,0:T(2,128)S(1)} %copy-done.3, s32[2,2]{1,0:T(2,128)S(1)} %collective-permute-done.conn2_ref, s32[2]{0:T(128)S(1)} %copy-done.2, bf16[16,2,16,512]{3,2,1,0:T(8,128)(2,1)S(1)} %bitcast.9, ...), custom_call_target="tpu_custom_call" | custom-call | tf_op jit(solution)/shard_map/slot_sums/pallas_call | solution.py:110
  42.9 0.0 copy-start.1
  42.9 12.7 %all_to_all.27 = bf16[16,2,16,512]{3,2,1,0:T(8,128)(2,1)S(1)} all-to-all(bf16[16,2,16,512]{3,2,1,0:T(8,128)(2,1)S(1)} %get-tuple-element.8), channel_id=1, replica_groups=mesh['x'=4,'y'=4,'c'=2,'sec'=16] {'x'}, dimensions={0} | all-to-all | bytes 1048576 | tf_op jit(solution)/shard_map/all_to_all | solution.py:15
  55.6 0.0 copy-done.1
  55.6 5.5 %all-to-all-start.2 = ((bf16[16,2,16,512]{3,2,1,0:T(8,128)(2,1)}), bf16[16,2,16,512]{3,2,1,0:T(8,128)(2,1)S(1)}, u32[]{:S(2)}, u32[]{:S(2)}) async-start(bf16[16,2,16,512]{3,2,1,0:T(8,128)(2,1)} %copy-done.1), calls=%async_computation.2 | async-start | bytes 1048576 | tf_op jit(solution)/shard_map/all_to_all | solution.py:15
  61.1 0.1 iota_compare_fusion
  61.2 0.1 reduce_sum.31
  61.2 2.8 %collective-permute-start.4 = (bf16[4,2,16,512]{3,2,1,0:T(8,128)(2,1)S(1)}, bf16[4,2,16,512]{3,2,1,0:T(8,128)(2,1)S(1)}, u32[]{:S(2)}, u32[]{:S(2)}) collective-permute-start(bf16[4,2,16,512]{3,2,1,0:T(8,128)(2,1)S(1)} %reduce_sum.31), channel_id=1, source_target_pairs={{0,1},{1,2},{2,3},{3,4},{4,5},{5,6},{6,7},{7,8},{8,9},{9,10},{10,1... | collective-permute-start | bytes 393224 | tf_op jit(solution)/shard_map/ppermute | solution.py:28
  64.0 4.2 %all-to-all-done.2 = bf16[16,2,16,512]{3,2,1,0:T(8,128)(2,1)S(1)} async-done(((bf16[16,2,16,512]{3,2,1,0:T(8,128)(2,1)}), bf16[16,2,16,512]{3,2,1,0:T(8,128)(2,1)S(1)}, u32[]{:S(2)}, u32[]{:S(2)}) %all-to-all-start.2) | async-done | bytes 524320 | tf_op jit(solution)/shard_map/all_to_all | solution.py:15
  68.3 0.1 convert_reduce_fusion
  68.3 7.1 %collective-permute-done.4 = bf16[4,2,16,512]{3,2,1,0:T(8,128)(2,1)S(1)} collective-permute-done((bf16[4,2,16,512]{3,2,1,0:T(8,128)(2,1)S(1)}, bf16[4,2,16,512]{3,2,1,0:T(8,128)(2,1)S(1)}, u32[]{:S(2)}, u32[]{:S(2)}) %collective-permute-start.4) | collective-permute-done | bytes 131104 | tf_op jit(solution)/shard_map/ppermute | solution.py:28
  75.4 0.7 add_convert_fusion
  76.1 3.3 %all-to-all-start.4 = ((bf16[4,2,16,512]{3,2,1,0:T(8,128)(2,1)}), bf16[4,2,16,512]{3,2,1,0:T(8,128)(2,1)S(1)}, u32[]{:S(2)}, u32[]{:S(2)}) async-start(bf16[4,2,16,512]{3,2,1,0:T(8,128)(2,1)} %add_convert_fusion), calls=%async_computation.4 | async-start | bytes 262144 | tf_op jit(solution)/shard_map/all_to_all | solution.py:15
  79.4 0.1 broadcast_compare_fusion
  79.5 8.6 %all-to-all-done.4 = bf16[4,2,16,512]{3,2,1,0:T(8,128)(2,1)S(1)} async-done(((bf16[4,2,16,512]{3,2,1,0:T(8,128)(2,1)}), bf16[4,2,16,512]{3,2,1,0:T(8,128)(2,1)S(1)}, u32[]{:S(2)}, u32[]{:S(2)}) %all-to-all-start.4) | async-done | bytes 131104 | tf_op jit(solution)/shard_map/all_to_all | solution.py:15
  88.2 0.7 select_convert_fusion
  (3 shorter events, 0.1 us)
Async XLA Ops:
  0.0 37.1 %copy-start = (bf16[2,2,512,512]{3,2,1,0:T(8,128)(2,1)S(1)}, bf16[2,2,512,512]{3,2,1,0:T(8,128)(2,1)}, u32[]{:S(2)}) copy-start(bf16[2,2,512,512]{3,2,1,0:T(8,128)(2,1)} %param.6) | copy-start | bytes 6291460
  0.0 33.9 %copy-start.3 = (s32[2,2]{1,0:T(2,128)S(1)}, s32[2,2]{1,0:T(2,128)}, u32[]{:S(2)}) copy-start(s32[2,2]{1,0:T(2,128)} %conn_ref.1) | copy-start | bytes 52
  0.0 37.1 %copy-start.2 = (s32[2]{0:T(128)S(1)}, s32[2]{0:T(128)}, u32[]{:S(2)}) copy-start(s32[2]{0:T(128)} %dims_ref.1) | copy-start | bytes 28
  0.0 37.1 %collective-permute-start.2 = (bf16[2,2,512,512]{3,2,1,0:T(8,128)(2,1)}, bf16[2,2,512,512]{3,2,1,0:T(8,128)(2,1)}, u32[]{:S(2)}, u32[]{:S(2)}) collective-permute-start(bf16[2,2,512,512]{3,2,1,0:T(8,128)(2,1)} %param.6), channel_id=1, source_target_pairs={{0,16},{16,0},{1,17},{17,1},{2,18},{18,2},{3,19},{19,3},{4,20},{20... | collective-permute-start | bytes 6291464 | tf_op jit(solution)/shard_map/ppermute | solution.py:23
  2.1 35.0 %collective-permute-start.3 = (bf16[2,2,512,512]{3,2,1,0:T(8,128)(2,1)}, bf16[2,2,512,512]{3,2,1,0:T(8,128)(2,1)}, u32[]{:S(2)}, u32[]{:S(2)}) collective-permute-start(bf16[2,2,512,512]{3,2,1,0:T(8,128)(2,1)} %right_ref.1), channel_id=1, source_target_pairs={{0,16},{16,0},{1,17},{17,1},{2,18},{18,2},{3,19},{19,3},{4,20},{20... | collective-permute-start | bytes 6291464 | tf_op jit(solution)/shard_map/ppermute | solution.py:23
  31.9 5.1 %collective-permute-start.1 = (bf16[16,2,16,512]{3,2,1,0:T(8,128)(2,1)S(1)}, bf16[16,2,16,512]{3,2,1,0:T(8,128)(2,1)S(1)}, u32[]{:S(2)}, u32[]{:S(2)}) collective-permute-start(bf16[16,2,16,512]{3,2,1,0:T(8,128)(2,1)S(1)} %bitcast.8), channel_id=1, source_target_pairs={{0,16},{16,0},{1,17},{17,1},{2,18},{18,2},{3,19},{19,3},{4,20},{20... | collective-permute-start | bytes 1572872 | tf_op jit(solution)/shard_map/ppermute | solution.py:23
  33.9 3.2 %collective-permute-start = (s32[2,2]{1,0:T(2,128)S(1)}, s32[2,2]{1,0:T(2,128)S(1)}, u32[]{:S(2)}, u32[]{:S(2)}) collective-permute-start(s32[2,2]{1,0:T(2,128)S(1)} %copy-done.3), channel_id=1, source_target_pairs={{0,16},{16,0},{1,17},{17,1},{2,18},{18,2},{3,19},{19,3},{4,20},{20... | collective-permute-start | bytes 56 | tf_op jit(solution)/shard_map/ppermute | solution.py:23
  42.9 12.7 %copy-start.1 = (bf16[16,2,16,512]{3,2,1,0:T(8,128)(2,1)}, bf16[16,2,16,512]{3,2,1,0:T(8,128)(2,1)S(1)}, u32[]{:S(2)}) copy-start(bf16[16,2,16,512]{3,2,1,0:T(8,128)(2,1)S(1)} %get-tuple-element.7) | copy-start | bytes 1572868
  55.6 12.7 %all-to-all-start.2 = ((bf16[16,2,16,512]{3,2,1,0:T(8,128)(2,1)}), bf16[16,2,16,512]{3,2,1,0:T(8,128)(2,1)S(1)}, u32[]{:S(2)}, u32[]{:S(2)}) async-start(bf16[16,2,16,512]{3,2,1,0:T(8,128)(2,1)} %copy-done.1), calls=%async_computation.2 | async-start | bytes 1048576 | tf_op jit(solution)/shard_map/all_to_all | solution.py:15
  61.2 14.2 %collective-permute-start.4 = (bf16[4,2,16,512]{3,2,1,0:T(8,128)(2,1)S(1)}, bf16[4,2,16,512]{3,2,1,0:T(8,128)(2,1)S(1)}, u32[]{:S(2)}, u32[]{:S(2)}) collective-permute-start(bf16[4,2,16,512]{3,2,1,0:T(8,128)(2,1)S(1)} %reduce_sum.31), channel_id=1, source_target_pairs={{0,1},{1,2},{2,3},{3,4},{4,5},{5,6},{6,7},{7,8},{8,9},{9,10},{10,1... | collective-permute-start | bytes 393224 | tf_op jit(solution)/shard_map/ppermute | solution.py:28
  76.1 12.0 %all-to-all-start.4 = ((bf16[4,2,16,512]{3,2,1,0:T(8,128)(2,1)}), bf16[4,2,16,512]{3,2,1,0:T(8,128)(2,1)S(1)}, u32[]{:S(2)}, u32[]{:S(2)}) async-start(bf16[4,2,16,512]{3,2,1,0:T(8,128)(2,1)} %add_convert_fusion), calls=%async_computation.4 | async-start | bytes 262144 | tf_op jit(solution)/shard_map/all_to_all | solution.py:15

commit v3 on v2

v3 whole, which is shorter than its diff:
```python
import jax
import jax.numpy as jnp
from jax import lax
from jax.experimental import pallas as pl
from jax.experimental.pallas import tpu as pltpu
from jax.sharding import Mesh
from jax.sharding import PartitionSpec as P

OP = ("x", "y", "c")
F32 = jnp.float32
BF16 = jnp.bfloat16


def exchanged(x, axis):
    return lax.all_to_all(x, axis, split_axis=0, concat_axis=0, tiled=True)


def shared(x, axis):
    return exchanged(jnp.broadcast_to(x[None], (lax.axis_size(axis),) + x.shape), axis)


def from_partner(x):
    return lax.ppermute(x, "c", [(0, 1), (1, 0)])


def from_behind(x):
    n = lax.axis_size("sec")
    return lax.ppermute(x, "sec", [(i, (i + 1) % n) for i in range(n)])


def in_vmem(x):
    return pltpu.with_memory_space_constraint(x, pltpu.VMEM)


def in_hbm(x):
    return pltpu.with_memory_space_constraint(x, pltpu.HBM)


def fetch_kernel(where_ref, left_ref, right_ref, rows_ref, rights_ref, sems):
    core = where_ref[1]
    fetches = []
    for k in range(right_ref.shape[0]):
        fetches.append(pltpu.make_async_copy(left_ref.at[k, 0, :, core], rows_ref.at[k], sems.at[0, k]))
        fetches.append(pltpu.make_async_copy(right_ref.at[k, 0], rights_ref.at[k], sems.at[1, k]))
    for fetch in fetches:
        fetch.start()
    for fetch in fetches:
        fetch.wait()


def fetched(where, left, right):
    kdev, _, chips, _, tall, width = left.shape
    hbm = pl.BlockSpec(memory_space=pltpu.HBM)
    return pl.pallas_call(
        fetch_kernel,
        in_specs=[pl.BlockSpec(memory_space=pltpu.SMEM), hbm, hbm],
        out_specs=[pl.BlockSpec(memory_space=pltpu.VMEM)] * 2,
        out_shape=[
            pltpu.VMEM((kdev, chips, tall, width), BF16),
            pltpu.VMEM((kdev, width, width), BF16),
        ],
        scratch_shapes=[pltpu.SemaphoreType.DMA((2, kdev))],
        compiler_params=pltpu.CompilerParams(vmem_limit_bytes=2**20),
        name="fetch",
    )(where, in_hbm(left), in_hbm(right))


def sums_kernel(where_ref, conn_ref, conn2_ref, dims_ref, near_ref, far_ref, rows0_ref, right0_ref, left_ref, right_ref, left2_ref, right2_ref, own_ref, onward_ref, psi_ref, rows_ref, rights_ref, half_ref, sum_ref, sems):
    kdev, sdev, width, _ = right_ref.shape
    chips, _, tall, _ = near_ref.shape
    group = where_ref[0]
    core = where_ref[1]
    many = chips * tall
    steps = [(0, 0, rows0_ref, right0_ref, ())]
    for whose, s in ((0, 1), (1, 0), (1, 1)):
        n = len(steps) - 1
        left, right = ((left_ref, right_ref), (left2_ref, right2_ref))[whose]
        fetches = []
        for k in range(kdev):
            fetches.append(pltpu.make_async_copy(left.at[k, s, :, core], rows_ref.at[n, k], sems.at[0, n, k]))
            fetches.append(pltpu.make_async_copy(right.at[k, s], rights_ref.at[n, k], sems.at[1, n, k]))
        for fetch in fetches:
            fetch.start()
        steps.append((whose, s, rows_ref.at[n], rights_ref.at[n], fetches))
    cols = lax.broadcasted_iota(jnp.int32, (tall, width), 1)
    row = lax.broadcasted_iota(jnp.int32, (tall, width), 0)
    for s in range(sdev):
        size = dims_ref[s]
        inside = cols < size
        for chip in range(chips):
            for ref, seat in ((near_ref, core), (far_ref, 1 - core)):
                start = pl.multiple_of((chip * 2 + seat) * tall, tall)
                kept = jnp.where(inside & (row + start < size), ref[chip, s].astype(F32), 0.0)
                psi_ref[s, pl.ds(start, tall), :] = kept.astype(BF16)
    sum_ref[...] = jnp.zeros_like(sum_ref)
    for whose, s, rows, rights, fetches in steps:
        for fetch in fetches:
            fetch.wait()
        left = rows[...].reshape(kdev * many, width)
        half_ref[...] = jnp.dot(left, psi_ref[s], preferred_element_type=F32).astype(BF16)
        for k in range(kdev):
            target = (conn_ref, conn2_ref)[whose][k, s]
            place = target % sdev + jnp.where(target // sdev != group, sdev, 0)
            sum_ref[place] += lax.dot_general(
                half_ref[k * many : (k + 1) * many, :],
                rights[k],
                (((1,), (1,)), ((), ())),
                preferred_element_type=F32,
            )
    for t in range(2 * sdev):
        out_ref = (own_ref, onward_ref)[t // sdev]
        for chip in range(chips):
            out_ref[chip, t % sdev] = sum_ref[t, chip * tall : (chip + 1) * tall, :].astype(BF16)


def slot_sums(where, conn, conn2, dims, near, far, rows0, right0, left, right, left2, right2):
    kdev, sdev, chips, _, tall, width = left.shape
    assert sdev == 2
    rest = 2 * sdev - 1
    smem = pl.BlockSpec(memory_space=pltpu.SMEM)
    vmem = pl.BlockSpec(memory_space=pltpu.VMEM)
    hbm = pl.BlockSpec(memory_space=pltpu.HBM)
    many = chips * tall
    return pl.pallas_call(
        sums_kernel,
        in_specs=[smem] * 4 + [vmem] * 4 + [hbm] * 4,
        out_specs=[vmem] * 2,
        out_shape=[pltpu.VMEM((chips, sdev, tall, width), BF16)] * 2,
        scratch_shapes=[
            pltpu.VMEM((sdev, width, width), BF16),
            pltpu.VMEM((rest, kdev, chips, tall, width), BF16),
            pltpu.VMEM((rest, kdev, width, width), BF16),
            pltpu.VMEM((kdev * many, width), BF16),
            pltpu.VMEM((2 * sdev, many, width), F32),
            pltpu.SemaphoreType.DMA((2, rest, kdev)),
        ],
        compiler_params=pltpu.CompilerParams(vmem_limit_bytes=24 * 2**20),
        name="slot_sums",
    )(where, conn, conn2, dims, *(in_vmem(x) for x in (near, far, rows0, right0)), *(in_hbm(x) for x in (left, right, left2, right2)))


def last_kernel(where_ref, dims_ref, parts_ref, out_ref):
    count, sdev, tall, width = parts_ref.shape
    cols = lax.broadcasted_iota(jnp.int32, (tall, width), 1)
    row = lax.broadcasted_iota(jnp.int32, (tall, width), 0) + where_ref[2]
    for s in range(sdev):
        total = parts_ref[0, s].astype(F32)
        for part in range(1, count):
            total = total + parts_ref[part, s].astype(F32)
        size = dims_ref[s]
        out_ref[s] = jnp.where((cols < size) & (row < size), total, 0.0).astype(BF16)


def last_sum(where, dims, parts):
    smem = pl.BlockSpec(memory_space=pltpu.SMEM)
    vmem = pl.BlockSpec(memory_space=pltpu.VMEM)
    return pl.pallas_call(
        last_kernel,
        in_specs=[smem, smem, vmem],
        out_specs=vmem,
        out_shape=jax.ShapeDtypeStruct(parts.shape[1:], BF16),
        compiler_params=pltpu.CompilerParams(vmem_limit_bytes=4 * 2**20),
        name="last_sum",
    )(where, dims, in_vmem(parts))


def sigma_rows(psi, left_ops, right_ops, conn, dims):
    sdev, tall, width = psi.shape
    nx, ny = lax.axis_size("x"), lax.axis_size("y")
    places = (lax.axis_index("sec"), lax.axis_index("c"), lax.axis_index(OP) * tall)
    where = jnp.stack(places).astype(jnp.int32)
    by_row = left_ops.shape[:2] + (nx * ny, 2, tall, width)
    left2 = from_partner(left_ops).reshape(by_row)
    right2 = from_partner(right_ops)
    conn2 = from_partner(conn)
    left = left_ops.reshape(by_row)
    rows0, right0 = fetched(where, left, right_ops)
    by_y = shared(psi, "y").reshape(ny, sdev, tall, width)
    by_x = shared(by_y, "x").reshape(nx * ny, sdev, tall, width)
    other = from_partner(by_x)
    own, onward = slot_sums(where, conn, conn2, dims, by_x, other, rows0, right0, left, right_ops, left2, right2)
    by_chip = (nx, ny, sdev, tall, width)
    onward = exchanged(onward, "x").reshape(by_chip).astype(F32).sum(axis=0).astype(BF16)
    onward = from_behind(onward)
    own = exchanged(own, "x").reshape(by_chip).astype(F32).sum(axis=0)
    parts = exchanged((own + onward.astype(F32)).astype(BF16), "y")
    return last_sum(where, dims, parts)


def solution(mesh):
    finer = Mesh(mesh.devices.reshape(4, 4, 2, mesh.shape["sec"]), OP + ("sec",))
    in_specs = (
        P("sec", OP, None),
        P(OP, "sec", None, None),
        P(OP, "sec", None, None),
        P(OP, "sec"),
        P("sec"),
    )
    out_specs = P("sec", OP, None)
    return jax.shard_map(sigma_rows, mesh=finer, in_specs=in_specs, out_specs=out_specs, check_vma=False)
```

time: 89.5 us -> 90.8 us (1.015)
  blocking collectives: 39.3 us -> 50.1 us
  waiting for transfers between devices: 20.7 us -> 11.3 us
  Pallas kernels: 5.77 us -> 9.23 us
  starting transfers between devices: 20.4 us -> 17.1 us
  other arithmetic: 1.77 us -> 0.26 us
  local copies, waits for them, and re-layouts: 0.83 us -> 2.12 us
    all_to_all x3 -> x4, blocking collectives: 39.3 us -> 50.1 us  [exchanged(): return lax.all_to_all(x, axis, split_axis=0, concat_axis=0, tiled=True)]
    all_to_all x2 -> x1, waiting for transfers between devices: 12.9 us -> 4.13 us  [exchanged(): return lax.all_to_all(x, axis, split_axis=0, concat_axis=0, tiled=True)]
    pallas_call x1 -> x3, Pallas kernels: 5.77 us -> 9.23 us  [the longest x1 6.11 us: slot_sums(): pl.pallas_call(sums_kernel, in_specs=[smem] * 4 + [vmem] * 4 + [hbm] * 4,...]
    all_to_all x2 -> x1, starting transfers between devices: 8.83 us -> 5.51 us  [exchanged(): return lax.all_to_all(x, axis, split_axis=0, concat_axis=0, tiled=True)]
    convert_element_type x2 -> x1, other arithmetic: 1.37 us -> 0.03 us  [sigma_rows(): parts = exchanged((own + onward.astype(F32)).astype(BF16), 'y')]
    unnamed x8 -> x6, local copies, waits for them, and re-layouts: 0.02 us -> 1.3 us
  transfers between devices with their start and end apart: 7 -> 6, of which waited for: 4 -> 2; matrix products, arithmetic and copies ran while one was open for 1% -> 1% of each run, Pallas kernels for 0% -> 2%
where the time goes in v3:
time: 90.8 us; the launch traced here: 90.2 us
  blocking collectives  50.1 us (55%)
  starting transfers between devices  17.1 us (19%)
  waiting for transfers between devices  11.3 us (12%)
  Pallas kernels  9.23 us (10%)
  local copies, waits for them, and re-layouts  2.12 us (2%)
    all_to_all x4, blocking collectives, exchanged(): return lax.all_to_all(x, axis, split_axis=0, concat_axis=0, tiled=True)  50.1 us
    ppermute x4, starting transfers between devices, from_partner(): return lax.ppermute(x, 'c', [(0, 1), (1, 0)])  8.77 us
    ppermute x1, waiting for transfers between devices, from_behind(): return lax.ppermute(x, 'sec', [(i, (i + 1) % n) for i in range(n)])  7.2 us
    pallas_call x1, Pallas kernels, slot_sums(): pl.pallas_call(sums_kernel, in_specs=[smem] * 4 + [vmem] * 4 + [hbm] * 4,...  6.11 us
    all_to_all x1, starting transfers between devices, exchanged(): return lax.all_to_all(x, axis, split_axis=0, concat_axis=0, tiled=True)  5.51 us
    all_to_all x1, waiting for transfers between devices, exchanged(): return lax.all_to_all(x, axis, split_axis=0, concat_axis=0, tiled=True)  4.13 us
    ppermute x1, starting transfers between devices, from_behind(): return lax.ppermute(x, 'sec', [(i, (i + 1) % n) for i in range(n)])  2.78 us
    pallas_call x1, Pallas kernels, fetched(): pl.pallas_call(fetch_kernel, in_specs=[pl.BlockSpec(memory_space=pltpu.SM...  1.94 us
  transfers between devices with their start and end apart: 6, of which 2 were waited for; matrix products, arithmetic and copies ran while one was open for 1% of the time, Pallas kernels for 2%

profile of v3, /device:TPU:6, one launch (start us, length us, event | category | flops | bytes accessed | tf_op | source)
XLA Modules:
  0.0 90.2 jit_solution(14689230680955389507)
XLA Ops:
  0.0 0.0 copy-start.1
  0.0 2.0 %collective-permute-start.2 = (bf16[2,2,512,512]{3,2,1,0:T(8,128)(2,1)}, bf16[2,2,512,512]{3,2,1,0:T(8,128)(2,1)S(1)}, u32[]{:S(2)}, u32[]{:S(2)}) collective-permute-start(bf16[2,2,512,512]{3,2,1,0:T(8,128)(2,1)} %param.6), channel_id=1, source_target_pairs={{0,16},{16,0},{1,17},{17,1},{2,18},{18,2},{3,19},{19,3},{4,20},{20... | collective-permute-start | bytes 6291464 | tf_op jit(solution)/shard_map/ppermute | solution.py:23
  2.1 2.4 %collective-permute-start.3 = (bf16[2,2,512,512]{3,2,1,0:T(8,128)(2,1)}, bf16[2,2,512,512]{3,2,1,0:T(8,128)(2,1)}, u32[]{:S(2)}, u32[]{:S(2)}) collective-permute-start(bf16[2,2,512,512]{3,2,1,0:T(8,128)(2,1)} %right_ref.3), channel_id=1, source_target_pairs={{0,16},{16,0},{1,17},{17,1},{2,18},{18,2},{3,19},{19,3},{4,20},{20... | collective-permute-start | bytes 6291464 | tf_op jit(solution)/shard_map/ppermute | solution.py:23
  4.5 0.8 broadcast_in_dim.4
  5.2 16.0 %all_to_all.25 = bf16[4,2,16,512]{3,2,1,0:T(8,128)(2,1)S(1)} all-to-all(bf16[4,2,16,512]{3,2,1,0:T(8,128)(2,1)S(1)} %broadcast_in_dim.4), channel_id=1, replica_groups=mesh['x'=4,'y'=4,'c'=2,'sec'=16] {'y'}, dimensions={0} | all-to-all | bytes 262144 | tf_op jit(solution)/shard_map/all_to_all | solution.py:15
  21.3 0.1 broadcast_in_dim.5
  21.3 10.6 %all_to_all.26 = bf16[4,4,2,16,512]{4,3,2,1,0:T(8,128)(2,1)S(1)} all-to-all(bf16[4,4,2,16,512]{4,3,2,1,0:T(8,128)(2,1)S(1)} %broadcast_in_dim.5), channel_id=1, replica_groups=mesh['x'=4,'y'=4,'c'=2,'sec'=16] {'x'}, dimensions={0} | all-to-all | bytes 1048576 | tf_op jit(solution)/shard_map/all_to_all | solution.py:15
  31.9 1.9 %collective-permute-start.1 = (bf16[16,2,16,512]{3,2,1,0:T(8,128)(2,1)S(1)}, bf16[16,2,16,512]{3,2,1,0:T(8,128)(2,1)S(1)}, u32[]{:S(2)}, u32[]{:S(2)}) collective-permute-start(bf16[16,2,16,512]{3,2,1,0:T(8,128)(2,1)S(1)} %bitcast.9), channel_id=1, source_target_pairs={{0,16},{16,0},{1,17},{17,1},{2,18},{18,2},{3,19},{19,3},{4,20},{20... | collective-permute-start | bytes 1572872 | tf_op jit(solution)/shard_map/ppermute | solution.py:23
  33.8 0.0 copy-done.1
  33.9 2.4 %collective-permute-start = (s32[2,2]{1,0:T(2,128)S(1)}, s32[2,2]{1,0:T(2,128)S(1)}, u32[]{:S(2)}, u32[]{:S(2)}) collective-permute-start(s32[2,2]{1,0:T(2,128)S(1)} %copy-done.1), channel_id=1, source_target_pairs={{0,16},{16,0},{1,17},{17,1},{2,18},{18,2},{3,19},{19,3},{4,20},{20... | collective-permute-start | bytes 56 | tf_op jit(solution)/shard_map/ppermute | solution.py:23
  36.3 0.1 pad_add_fusion.where_ref
  36.4 0.0 copy-start
  36.4 1.9 %fetch.1 = (bf16[2,16,16,512]{3,2,1,0:T(8,128)(2,1)S(1)}, bf16[2,512,512]{2,1,0:T(8,128)(2,1)S(1)}) custom-call(s32[3]{0:T(128)S(1)} %pad_add_fusion.where_ref, bf16[2,2,16,2,16,512]{5,4,3,2,1,0:T(8,128)(2,1)} %bitcast.11, bf16[2,2,512,512]{3,2,1,0:T(8,128)(2,1)} %right_ref.3), custom_call_target="tpu_custom_call" | custom-call | tf_op jit(solution)/shard_map/fetch/pallas_call | solution.py:54
  38.3 0.0 collective-permute-done.conn2_ref
  38.3 0.0 collective-permute-done.1.far_ref
  38.3 0.0 collective-permute-done.2
  38.3 0.0 copy-start.2
  38.3 0.0 collective-permute-done.3.right2_ref
  38.4 1.3 %copy-done.2 = bf16[2,2,512,512]{3,2,1,0:T(8,128)(2,1)} copy-done((bf16[2,2,512,512]{3,2,1,0:T(8,128)(2,1)}, bf16[2,2,512,512]{3,2,1,0:T(8,128)(2,1)S(1)}, u32[]{:S(2)}) %copy-start.2) | copy-done | bytes 2097176
  39.6 0.0 copy-done
  39.6 6.1 %slot_sums.1 = (bf16[16,2,16,512]{3,2,1,0:T(8,128)(2,1)}, bf16[16,2,16,512]{3,2,1,0:T(8,128)(2,1)S(1)}) custom-call(s32[3]{0:T(128)S(1)} %pad_add_fusion.where_ref, s32[2,2]{1,0:T(2,128)S(1)} %copy-done.1, s32[2,2]{1,0:T(2,128)S(1)} %collective-permute-done.conn2_ref, s32[2]{0:T(128)S(1)} %copy-done, bf16[16,2,16,512]{3,2,1,0:T(8,128)(2,1)S(1)} %bitcast.10, ...), custom_call_target="tpu_custom_call" | custom-call | tf_op jit(solution)/shard_map/slot_sums/pallas_call | solution.py:124
  45.8 12.3 %all_to_all.27 = bf16[16,2,16,512]{3,2,1,0:T(8,128)(2,1)S(1)} all-to-all(bf16[16,2,16,512]{3,2,1,0:T(8,128)(2,1)S(1)} %get-tuple-element.12), channel_id=1, replica_groups=mesh['x'=4,'y'=4,'c'=2,'sec'=16] {'x'}, dimensions={0} | all-to-all | bytes 1048576 | tf_op jit(solution)/shard_map/all_to_all | solution.py:15
  58.1 5.5 %all-to-all-start.2 = ((bf16[16,2,16,512]{3,2,1,0:T(8,128)(2,1)}), bf16[16,2,16,512]{3,2,1,0:T(8,128)(2,1)S(1)}, u32[]{:S(2)}, u32[]{:S(2)}) async-start(bf16[16,2,16,512]{3,2,1,0:T(8,128)(2,1)} %get-tuple-element.11), calls=%async_computation.2 | async-start | bytes 1048576 | tf_op jit(solution)/shard_map/all_to_all | solution.py:15
  63.6 0.1 reduce_sum.22
  63.7 2.8 %collective-permute-start.4 = (bf16[4,2,16,512]{3,2,1,0:T(8,128)(2,1)S(1)}, bf16[4,2,16,512]{3,2,1,0:T(8,128)(2,1)S(1)}, u32[]{:S(2)}, u32[]{:S(2)}) collective-permute-start(bf16[4,2,16,512]{3,2,1,0:T(8,128)(2,1)S(1)} %reduce_sum.22), channel_id=1, source_target_pairs={{0,1},{1,2},{2,3},{3,4},{4,5},{5,6},{6,7},{7,8},{8,9},{9,10},{10,1... | collective-permute-start | bytes 393224 | tf_op jit(solution)/shard_map/ppermute | solution.py:28
  66.5 4.1 %all-to-all-done.2 = bf16[16,2,16,512]{3,2,1,0:T(8,128)(2,1)S(1)} async-done(((bf16[16,2,16,512]{3,2,1,0:T(8,128)(2,1)}), bf16[16,2,16,512]{3,2,1,0:T(8,128)(2,1)S(1)}, u32[]{:S(2)}, u32[]{:S(2)}) %all-to-all-start.2) | async-done | bytes 524320 | tf_op jit(solution)/shard_map/all_to_all | solution.py:15
  70.6 0.1 convert_reduce_fusion
  70.7 7.2 %collective-permute-done.4 = bf16[4,2,16,512]{3,2,1,0:T(8,128)(2,1)S(1)} collective-permute-done((bf16[4,2,16,512]{3,2,1,0:T(8,128)(2,1)S(1)}, bf16[4,2,16,512]{3,2,1,0:T(8,128)(2,1)S(1)}, u32[]{:S(2)}, u32[]{:S(2)}) %collective-permute-start.4) | collective-permute-done | bytes 131104 | tf_op jit(solution)/shard_map/ppermute | solution.py:28
  77.9 11.1 %all_to_all.28.parts_ref = bf16[4,2,16,512]{3,2,1,0:T(8,128)(2,1)S(1)} all-to-all(bf16[4,2,16,512]{3,2,1,0:T(8,128)(2,1)S(1)} %add_convert_fusion), channel_id=1, replica_groups=mesh['x'=4,'y'=4,'c'=2,'sec'=16] {'y'}, dimensions={0} | all-to-all | bytes 262144 | tf_op jit(solution)/shard_map/all_to_all | solution.py:15
  89.0 1.2 %last_sum.1 = bf16[2,16,512]{2,1,0:T(8,128)(2,1)} custom-call(s32[3]{0:T(128)S(1)} %pad_add_fusion.where_ref, s32[2]{0:T(128)S(1)} %copy-done, bf16[4,2,16,512]{3,2,1,0:T(8,128)(2,1)S(1)} %all_to_all.28.parts_ref), custom_call_target="tpu_custom_call" | custom-call | tf_op jit(solution)/shard_map/last_sum/pallas_call | solution.py:157
  (1 shorter events, 0.0 us)
Async XLA Ops:
  0.0 33.8 %copy-start.1 = (s32[2,2]{1,0:T(2,128)S(1)}, s32[2,2]{1,0:T(2,128)}, u32[]{:S(2)}) copy-start(s32[2,2]{1,0:T(2,128)} %conn_ref.1) | copy-start | bytes 52
  0.0 38.3 %collective-permute-start.2 = (bf16[2,2,512,512]{3,2,1,0:T(8,128)(2,1)}, bf16[2,2,512,512]{3,2,1,0:T(8,128)(2,1)S(1)}, u32[]{:S(2)}, u32[]{:S(2)}) collective-permute-start(bf16[2,2,512,512]{3,2,1,0:T(8,128)(2,1)} %param.6), channel_id=1, source_target_pairs={{0,16},{16,0},{1,17},{17,1},{2,18},{18,2},{3,19},{19,3},{4,20},{20... | collective-permute-start | bytes 6291464 | tf_op jit(solution)/shard_map/ppermute | solution.py:23
  2.1 36.3 %collective-permute-start.3 = (bf16[2,2,512,512]{3,2,1,0:T(8,128)(2,1)}, bf16[2,2,512,512]{3,2,1,0:T(8,128)(2,1)}, u32[]{:S(2)}, u32[]{:S(2)}) collective-permute-start(bf16[2,2,512,512]{3,2,1,0:T(8,128)(2,1)} %right_ref.3), channel_id=1, source_target_pairs={{0,16},{16,0},{1,17},{17,1},{2,18},{18,2},{3,19},{19,3},{4,20},{20... | collective-permute-start | bytes 6291464 | tf_op jit(solution)/shard_map/ppermute | solution.py:23
  31.9 6.4 %collective-permute-start.1 = (bf16[16,2,16,512]{3,2,1,0:T(8,128)(2,1)S(1)}, bf16[16,2,16,512]{3,2,1,0:T(8,128)(2,1)S(1)}, u32[]{:S(2)}, u32[]{:S(2)}) collective-permute-start(bf16[16,2,16,512]{3,2,1,0:T(8,128)(2,1)S(1)} %bitcast.9), channel_id=1, source_target_pairs={{0,16},{16,0},{1,17},{17,1},{2,18},{18,2},{3,19},{19,3},{4,20},{20... | collective-permute-start | bytes 1572872 | tf_op jit(solution)/shard_map/ppermute | solution.py:23
  33.9 4.5 %collective-permute-start = (s32[2,2]{1,0:T(2,128)S(1)}, s32[2,2]{1,0:T(2,128)S(1)}, u32[]{:S(2)}, u32[]{:S(2)}) collective-permute-start(s32[2,2]{1,0:T(2,128)S(1)} %copy-done.1), channel_id=1, source_target_pairs={{0,16},{16,0},{1,17},{17,1},{2,18},{18,2},{3,19},{19,3},{4,20},{20... | collective-permute-start | bytes 56 | tf_op jit(solution)/shard_map/ppermute | solution.py:23
  36.4 3.3 %copy-start = (s32[2]{0:T(128)S(1)}, s32[2]{0:T(128)}, u32[]{:S(2)}) copy-start(s32[2]{0:T(128)} %dims_ref.3) | copy-start | bytes 28
  38.3 1.3 %copy-start.2 = (bf16[2,2,512,512]{3,2,1,0:T(8,128)(2,1)}, bf16[2,2,512,512]{3,2,1,0:T(8,128)(2,1)S(1)}, u32[]{:S(2)}) copy-start(bf16[2,2,512,512]{3,2,1,0:T(8,128)(2,1)S(1)} %collective-permute-done.2) | copy-start | bytes 6291460
  58.1 12.5 %all-to-all-start.2 = ((bf16[16,2,16,512]{3,2,1,0:T(8,128)(2,1)}), bf16[16,2,16,512]{3,2,1,0:T(8,128)(2,1)S(1)}, u32[]{:S(2)}, u32[]{:S(2)}) async-start(bf16[16,2,16,512]{3,2,1,0:T(8,128)(2,1)} %get-tuple-element.11), calls=%async_computation.2 | async-start | bytes 1048576 | tf_op jit(solution)/shard_map/all_to_all | solution.py:15
  63.7 14.2 %collective-permute-start.4 = (bf16[4,2,16,512]{3,2,1,0:T(8,128)(2,1)S(1)}, bf16[4,2,16,512]{3,2,1,0:T(8,128)(2,1)S(1)}, u32[]{:S(2)}, u32[]{:S(2)}) collective-permute-start(bf16[4,2,16,512]{3,2,1,0:T(8,128)(2,1)S(1)} %reduce_sum.22), channel_id=1, source_target_pairs={{0,1},{1,2},{2,3},{3,4},{4,5},{5,6},{6,7},{7,8},{8,9},{9,10},{10,1... | collective-permute-start | bytes 393224 | tf_op jit(solution)/shard_map/ppermute | solution.py:28

commit v4 on v3

--- a/solution.py
+++ b/solution.py
@@ -79,19 +79,21 @@
         for k in range(kdev):
             fetches.append(pltpu.make_async_copy(left.at[k, s, :, core], rows_ref.at[n, k], sems.at[0, n, k]))
             fetches.append(pltpu.make_async_copy(right.at[k, s], rights_ref.at[n, k], sems.at[1, n, k]))
+        steps.append((whose, s, rows_ref.at[n], rights_ref.at[n], fetches))
         for fetch in fetches:
             fetch.start()
-        steps.append((whose, s, rows_ref.at[n], rights_ref.at[n], fetches))
     cols = lax.broadcasted_iota(jnp.int32, (tall, width), 1)
     row = lax.broadcasted_iota(jnp.int32, (tall, width), 0)
-    for s in range(sdev):
-        size = dims_ref[s]
-        inside = cols < size
-        for chip in range(chips):
+
+    @pl.loop(0, chips)
+    def _(chip):
+        for s in range(sdev):
+            size = dims_ref[s]
             for ref, seat in ((near_ref, core), (far_ref, 1 - core)):
                 start = pl.multiple_of((chip * 2 + seat) * tall, tall)
-                kept = jnp.where(inside & (row + start < size), ref[chip, s].astype(F32), 0.0)
-                psi_ref[s, pl.ds(start, tall), :] = kept.astype(BF16)
+                kept = (cols < size) & (row + start < size)
+                psi_ref[s, pl.ds(start, tall), :] = jnp.where(kept, ref[chip, s].astype(F32), 0.0).astype(BF16)
+
     sum_ref[...] = jnp.zeros_like(sum_ref)
     for whose, s, rows, rights, fetches in steps:
         for fetch in fetches:
@@ -139,29 +141,12 @@
     )(where, conn, conn2, dims, *(in_vmem(x) for x in (near, far, rows0, right0)), *(in_hbm(x) for x in (left, right, left2, right2)))
 
 
-def last_kernel(where_ref, dims_ref, parts_ref, out_ref):
-    count, sdev, tall, width = parts_ref.shape
-    cols = lax.broadcasted_iota(jnp.int32, (tall, width), 1)
-    row = lax.broadcasted_iota(jnp.int32, (tall, width), 0) + where_ref[2]
-    for s in range(sdev):
-        total = parts_ref[0, s].astype(F32)
-        for part in range(1, count):
-            total = total + parts_ref[part, s].astype(F32)
-        size = dims_ref[s]
-        out_ref[s] = jnp.where((cols < size) & (row < size), total, 0.0).astype(BF16)
-
-
-def last_sum(where, dims, parts):
-    smem = pl.BlockSpec(memory_space=pltpu.SMEM)
-    vmem = pl.BlockSpec(memory_space=pltpu.VMEM)
-    return pl.pallas_call(
-        last_kernel,
-        in_specs=[smem, smem, vmem],
-        out_specs=vmem,
-        out_shape=jax.ShapeDtypeStruct(parts.shape[1:], BF16),
-        compiler_params=pltpu.CompilerParams(vmem_limit_bytes=4 * 2**20),
-        name="last_sum",
-    )(where, dims, in_vmem(parts))
+def kept_entries(dims, row_start, rows, width):
+    row_ids = row_start + jnp.arange(rows, dtype=jnp.int32)
+    col_ids = jnp.arange(width, dtype=jnp.int32)
+    return (row_ids[None, :, None] < dims[:, None, None]) & (
+        col_ids[None, None, :] < dims[:, None, None]
+    )
 
 
 def sigma_rows(psi, left_ops, right_ops, conn, dims):
@@ -177,14 +162,16 @@
     rows0, right0 = fetched(where, left, right_ops)
     by_y = shared(psi, "y").reshape(ny, sdev, tall, width)
     by_x = shared(by_y, "x").reshape(nx * ny, sdev, tall, width)
+    kept = kept_entries(dims, places[2], tall, width)
+    by_x, kept = lax.optimization_barrier((by_x, kept))
     other = from_partner(by_x)
     own, onward = slot_sums(where, conn, conn2, dims, by_x, other, rows0, right0, left, right_ops, left2, right2)
     by_chip = (nx, ny, sdev, tall, width)
     onward = exchanged(onward, "x").reshape(by_chip).astype(F32).sum(axis=0).astype(BF16)
     onward = from_behind(onward)
     own = exchanged(own, "x").reshape(by_chip).astype(F32).sum(axis=0)
-    parts = exchanged((own + onward.astype(F32)).astype(BF16), "y")
-    return last_sum(where, dims, parts)
+    summed = exchanged((own + onward.astype(F32)).astype(BF16), "y").astype(F32).sum(axis=0)
+    return jnp.where(kept, summed, jnp.zeros_like(summed)).astype(BF16)
 
 
 def solution(mesh):

time: 90.8 us -> 91.3 us (level)
  blocking collectives: 50.1 us -> 23.4 us
  waiting for transfers between devices: 11.3 us -> 26.2 us
  starting transfers between devices: 17.1 us -> 28.3 us
  Pallas kernels: 9.23 us -> 7.15 us
  other arithmetic: 0.26 us -> 1.8 us
  local copies, waits for them, and re-layouts: 2.12 us -> 3.57 us
    all_to_all x4 -> x2, blocking collectives: 50.1 us -> 23.4 us  [exchanged(): return lax.all_to_all(x, axis, split_axis=0, concat_axis=0, tiled=True)]
    all_to_all x1 -> x3, waiting for transfers between devices: 4.13 us -> 19.6 us  [exchanged(): return lax.all_to_all(x, axis, split_axis=0, concat_axis=0, tiled=True)]
    all_to_all x1 -> x3, starting transfers between devices: 5.51 us -> 17.4 us  [exchanged(): return lax.all_to_all(x, axis, split_axis=0, concat_axis=0, tiled=True)]
    broadcast_in_dim x2, local copies, waits for them, and re-layouts: 0.82 us -> 2.27 us  [shared(): jnp.broadcast_to(x[None], (lax.axis_size(axis),) + x.shape)]
    pallas_call x1 -> x0, Pallas kernels: 1.18 us -> none  [last_sum(): pl.pallas_call(last_kernel, in_specs=[smem, smem, vmem], out_specs=vmem,...]
  transfers between devices with their start and end apart: 6 -> 8, of which waited for: 2 -> 4; matrix products, arithmetic and copies ran while one was open for 1% -> 4% of each run, Pallas kernels for 2% -> 2%
where the time goes in v4:
time: 91.3 us; the launch traced here: 90.6 us
  starting transfers between devices  28.3 us (31%)
  waiting for transfers between devices  26.2 us (29%)
  blocking collectives  23.4 us (26%)
  Pallas kernels  7.15 us (8%)
  local copies, waits for them, and re-layouts  3.57 us (4%)
  other arithmetic  1.8 us (2%)
    all_to_all x2, blocking collectives, exchanged(): return lax.all_to_all(x, axis, split_axis=0, concat_axis=0, tiled=True)  23.4 us
    all_to_all x3, waiting for transfers between devices, exchanged(): return lax.all_to_all(x, axis, split_axis=0, concat_axis=0, tiled=True)  19.6 us
    all_to_all x3, starting transfers between devices, exchanged(): return lax.all_to_all(x, axis, split_axis=0, concat_axis=0, tiled=True)  17.4 us
    ppermute x4, starting transfers between devices, from_partner(): return lax.ppermute(x, 'c', [(0, 1), (1, 0)])  8.77 us
    ppermute x1, waiting for transfers between devices, from_behind(): return lax.ppermute(x, 'sec', [(i, (i + 1) % n) for i in range(n)])  6.57 us
    pallas_call x1, Pallas kernels, slot_sums(): pl.pallas_call(sums_kernel, in_specs=[smem] * 4 + [vmem] * 4 + [hbm] * 4,...  5.21 us
    broadcast_in_dim x2, local copies, waits for them, and re-layouts, shared(): jnp.broadcast_to(x[None], (lax.axis_size(axis),) + x.shape)  2.27 us
    ppermute x1, starting transfers between devices, from_behind(): return lax.ppermute(x, 'sec', [(i, (i + 1) % n) for i in range(n)])  2.15 us
  transfers between devices with their start and end apart: 8, of which 4 were waited for; matrix products, arithmetic and copies ran while one was open for 4% of the time, Pallas kernels for 2%

profile of v4, /device:TPU:6, one launch (start us, length us, event | category | flops | bytes accessed | tf_op | source)
XLA Modules:
  0.0 90.6 jit_solution(9861887163561057437)
XLA Ops:
  0.0 0.0 copy-start
  0.0 0.0 copy-start.1
  0.0 2.0 %collective-permute-start.2 = (bf16[2,2,512,512]{3,2,1,0:T(8,128)(2,1)}, bf16[2,2,512,512]{3,2,1,0:T(8,128)(2,1)S(1)}, u32[]{:S(2)}, u32[]{:S(2)}) collective-permute-start(bf16[2,2,512,512]{3,2,1,0:T(8,128)(2,1)} %param.6), channel_id=1, source_target_pairs={{0,16},{16,0},{1,17},{17,1},{2,18},{18,2},{3,19},{19,3},{4,20},{20... | collective-permute-start | bytes 6291464 | tf_op jit(solution)/shard_map/ppermute | solution.py:23
  2.1 2.4 %collective-permute-start.3 = (bf16[2,2,512,512]{3,2,1,0:T(8,128)(2,1)}, bf16[2,2,512,512]{3,2,1,0:T(8,128)(2,1)}, u32[]{:S(2)}, u32[]{:S(2)}) collective-permute-start(bf16[2,2,512,512]{3,2,1,0:T(8,128)(2,1)} %right_ref.3), channel_id=1, source_target_pairs={{0,16},{16,0},{1,17},{17,1},{2,18},{18,2},{3,19},{19,3},{4,20},{20... | collective-permute-start | bytes 6291464 | tf_op jit(solution)/shard_map/ppermute | solution.py:23
  4.5 1.4 %broadcast_in_dim.6 = bf16[4,2,16,512]{3,2,1,0:T(8,128)(2,1)} broadcast(bf16[2,16,512]{2,1,0:T(8,128)(2,1)} %param.5), dimensions={1,2,3} | broadcast | bytes 163840 | tf_op jit(solution)/shard_map/broadcast_in_dim | solution.py:19
  5.9 7.1 %all-to-all-start = ((bf16[4,2,16,512]{3,2,1,0:T(8,128)(2,1)}), bf16[4,2,16,512]{3,2,1,0:T(8,128)(2,1)S(1)}, u32[]{:S(2)}, u32[]{:S(2)}) async-start(bf16[4,2,16,512]{3,2,1,0:T(8,128)(2,1)} %broadcast_in_dim.6), calls=%async_computation | async-start | bytes 262144 | tf_op jit(solution)/shard_map/all_to_all | solution.py:15
  13.0 0.7 iota_compare_fusion
  13.7 8.4 %all-to-all-done = bf16[4,2,16,512]{3,2,1,0:T(8,128)(2,1)S(1)} async-done(((bf16[4,2,16,512]{3,2,1,0:T(8,128)(2,1)}), bf16[4,2,16,512]{3,2,1,0:T(8,128)(2,1)S(1)}, u32[]{:S(2)}, u32[]{:S(2)}) %all-to-all-start) | async-done | bytes 131104 | tf_op jit(solution)/shard_map/all_to_all | solution.py:15
  22.1 0.9 broadcast_in_dim.7
  23.0 4.8 %all-to-all-start.1 = ((bf16[4,4,2,16,512]{4,3,2,1,0:T(8,128)(2,1)}), bf16[4,4,2,16,512]{4,3,2,1,0:T(8,128)(2,1)S(1)}, u32[]{:S(2)}, u32[]{:S(2)}) async-start(bf16[4,4,2,16,512]{4,3,2,1,0:T(8,128)(2,1)} %broadcast_in_dim.7), calls=%async_computation.1 | async-start | bytes 1048576 | tf_op jit(solution)/shard_map/all_to_all | solution.py:15
  27.8 0.0 copy-done
  27.8 0.1 broadcast_compare_fusion
  27.9 0.1 broadcast_and_fusion
  27.9 6.5 %all-to-all-done.1 = bf16[4,4,2,16,512]{4,3,2,1,0:T(8,128)(2,1)S(1)} async-done(((bf16[4,4,2,16,512]{4,3,2,1,0:T(8,128)(2,1)}), bf16[4,4,2,16,512]{4,3,2,1,0:T(8,128)(2,1)S(1)}, u32[]{:S(2)}, u32[]{:S(2)}) %all-to-all-start.1) | async-done | bytes 524320 | tf_op jit(solution)/shard_map/all_to_all | solution.py:15
  34.4 1.9 %collective-permute-start.1 = (bf16[16,2,16,512]{3,2,1,0:T(8,128)(2,1)S(1)}, bf16[16,2,16,512]{3,2,1,0:T(8,128)(2,1)S(1)}, u32[]{:S(2)}, u32[]{:S(2)}) collective-permute-start(bf16[16,2,16,512]{3,2,1,0:T(8,128)(2,1)S(1)} %bitcast.9), channel_id=1, source_target_pairs={{0,16},{16,0},{1,17},{17,1},{2,18},{18,2},{3,19},{19,3},{4,20},{20... | collective-permute-start | bytes 1572872 | tf_op jit(solution)/shard_map/ppermute | solution.py:23
  36.3 0.0 copy-done.1
  36.3 2.4 %collective-permute-start = (s32[2,2]{1,0:T(2,128)S(1)}, s32[2,2]{1,0:T(2,128)S(1)}, u32[]{:S(2)}, u32[]{:S(2)}) collective-permute-start(s32[2,2]{1,0:T(2,128)S(1)} %copy-done.1), channel_id=1, source_target_pairs={{0,16},{16,0},{1,17},{17,1},{2,18},{18,2},{3,19},{19,3},{4,20},{20... | collective-permute-start | bytes 56 | tf_op jit(solution)/shard_map/ppermute | solution.py:23
  38.7 0.1 pad_add_fusion.where_ref
  38.8 1.9 %fetch.1 = (bf16[2,16,16,512]{3,2,1,0:T(8,128)(2,1)S(1)}, bf16[2,512,512]{2,1,0:T(8,128)(2,1)S(1)}) custom-call(s32[3]{0:T(128)S(1)} %pad_add_fusion.where_ref, bf16[2,2,16,2,16,512]{5,4,3,2,1,0:T(8,128)(2,1)} %bitcast.11, bf16[2,2,512,512]{3,2,1,0:T(8,128)(2,1)} %right_ref.3), custom_call_target="tpu_custom_call" | custom-call | tf_op jit(solution)/shard_map/fetch/pallas_call | solution.py:54
  40.8 0.0 collective-permute-done.conn2_ref
  40.8 0.0 collective-permute-done.1.far_ref
  40.8 0.0 collective-permute-done.2
  40.8 0.0 copy-start.2
  40.8 0.0 collective-permute-done.3.right2_ref
  40.8 1.3 %copy-done.2 = bf16[2,2,512,512]{3,2,1,0:T(8,128)(2,1)} copy-done((bf16[2,2,512,512]{3,2,1,0:T(8,128)(2,1)}, bf16[2,2,512,512]{3,2,1,0:T(8,128)(2,1)S(1)}, u32[]{:S(2)}) %copy-start.2) | copy-done | bytes 2097176
  42.1 5.2 %slot_sums.1 = (bf16[16,2,16,512]{3,2,1,0:T(8,128)(2,1)}, bf16[16,2,16,512]{3,2,1,0:T(8,128)(2,1)S(1)}) custom-call(s32[3]{0:T(128)S(1)} %pad_add_fusion.where_ref, s32[2,2]{1,0:T(2,128)S(1)} %copy-done.1, s32[2,2]{1,0:T(2,128)S(1)} %collective-permute-done.conn2_ref, s32[2]{0:T(128)S(1)} %copy-done, bf16[16,2,16,512]{3,2,1,0:T(8,128)(2,1)S(1)} %bitcast.10, ...), custom_call_target="tpu_custom_call" | custom-call | tf_op jit(solution)/shard_map/slot_sums/pallas_call | solution.py:126
  47.3 12.3 %all_to_all.25 = bf16[16,2,16,512]{3,2,1,0:T(8,128)(2,1)S(1)} all-to-all(bf16[16,2,16,512]{3,2,1,0:T(8,128)(2,1)S(1)} %get-tuple-element.16), channel_id=1, replica_groups=mesh['x'=4,'y'=4,'c'=2,'sec'=16] {'x'}, dimensions={0} | all-to-all | bytes 1048576 | tf_op jit(solution)/shard_map/all_to_all | solution.py:15
  59.7 5.5 %all-to-all-start.2 = ((bf16[16,2,16,512]{3,2,1,0:T(8,128)(2,1)}), bf16[16,2,16,512]{3,2,1,0:T(8,128)(2,1)S(1)}, u32[]{:S(2)}, u32[]{:S(2)}) async-start(bf16[16,2,16,512]{3,2,1,0:T(8,128)(2,1)} %get-tuple-element.15), calls=%async_computation.2 | async-start | bytes 1048576 | tf_op jit(solution)/shard_map/all_to_all | solution.py:15
  65.2 0.1 reduce_sum.31
  65.3 2.2 %collective-permute-start.4 = (bf16[4,2,16,512]{3,2,1,0:T(8,128)(2,1)S(1)}, bf16[4,2,16,512]{3,2,1,0:T(8,128)(2,1)S(1)}, u32[]{:S(2)}, u32[]{:S(2)}) collective-permute-start(bf16[4,2,16,512]{3,2,1,0:T(8,128)(2,1)S(1)} %reduce_sum.31), channel_id=1, source_target_pairs={{0,1},{1,2},{2,3},{3,4},{4,5},{5,6},{6,7},{7,8},{8,9},{9,10},{10,1... | collective-permute-start | bytes 393224 | tf_op jit(solution)/shard_map/ppermute | solution.py:28
  67.4 4.8 %all-to-all-done.2 = bf16[16,2,16,512]{3,2,1,0:T(8,128)(2,1)S(1)} async-done(((bf16[16,2,16,512]{3,2,1,0:T(8,128)(2,1)}), bf16[16,2,16,512]{3,2,1,0:T(8,128)(2,1)S(1)}, u32[]{:S(2)}, u32[]{:S(2)}) %all-to-all-start.2) | async-done | bytes 524320 | tf_op jit(solution)/shard_map/all_to_all | solution.py:15
  72.2 0.1 convert_reduce_fusion
  72.3 6.6 %collective-permute-done.4 = bf16[4,2,16,512]{3,2,1,0:T(8,128)(2,1)S(1)} collective-permute-done((bf16[4,2,16,512]{3,2,1,0:T(8,128)(2,1)S(1)}, bf16[4,2,16,512]{3,2,1,0:T(8,128)(2,1)S(1)}, u32[]{:S(2)}, u32[]{:S(2)}) %collective-permute-start.4) | collective-permute-done | bytes 131104 | tf_op jit(solution)/shard_map/ppermute | solution.py:28
  78.9 11.1 %all_to_all.26 = bf16[4,2,16,512]{3,2,1,0:T(8,128)(2,1)S(1)} all-to-all(bf16[4,2,16,512]{3,2,1,0:T(8,128)(2,1)S(1)} %add_convert_fusion), channel_id=1, replica_groups=mesh['x'=4,'y'=4,'c'=2,'sec'=16] {'y'}, dimensions={0} | all-to-all | bytes 262144 | tf_op jit(solution)/shard_map/all_to_all | solution.py:15
  90.0 0.6 select_convert_fusion
  (3 shorter events, 0.1 us)
Async XLA Ops:
  0.0 27.8 %copy-start = (s32[2]{0:T(128)S(1)}, s32[2]{0:T(128)}, u32[]{:S(2)}) copy-start(s32[2]{0:T(128)} %dims_ref.1) | copy-start | bytes 28
  0.0 36.3 %copy-start.1 = (s32[2,2]{1,0:T(2,128)S(1)}, s32[2,2]{1,0:T(2,128)}, u32[]{:S(2)}) copy-start(s32[2,2]{1,0:T(2,128)} %conn_ref.1) | copy-start | bytes 52
  0.0 40.8 %collective-permute-start.2 = (bf16[2,2,512,512]{3,2,1,0:T(8,128)(2,1)}, bf16[2,2,512,512]{3,2,1,0:T(8,128)(2,1)S(1)}, u32[]{:S(2)}, u32[]{:S(2)}) collective-permute-start(bf16[2,2,512,512]{3,2,1,0:T(8,128)(2,1)} %param.6), channel_id=1, source_target_pairs={{0,16},{16,0},{1,17},{17,1},{2,18},{18,2},{3,19},{19,3},{4,20},{20... | collective-permute-start | bytes 6291464 | tf_op jit(solution)/shard_map/ppermute | solution.py:23
  2.1 38.8 %collective-permute-start.3 = (bf16[2,2,512,512]{3,2,1,0:T(8,128)(2,1)}, bf16[2,2,512,512]{3,2,1,0:T(8,128)(2,1)}, u32[]{:S(2)}, u32[]{:S(2)}) collective-permute-start(bf16[2,2,512,512]{3,2,1,0:T(8,128)(2,1)} %right_ref.3), channel_id=1, source_target_pairs={{0,16},{16,0},{1,17},{17,1},{2,18},{18,2},{3,19},{19,3},{4,20},{20... | collective-permute-start | bytes 6291464 | tf_op jit(solution)/shard_map/ppermute | solution.py:23
  5.9 16.2 %all-to-all-start = ((bf16[4,2,16,512]{3,2,1,0:T(8,128)(2,1)}), bf16[4,2,16,512]{3,2,1,0:T(8,128)(2,1)S(1)}, u32[]{:S(2)}, u32[]{:S(2)}) async-start(bf16[4,2,16,512]{3,2,1,0:T(8,128)(2,1)} %broadcast_in_dim.6), calls=%async_computation | async-start | bytes 262144 | tf_op jit(solution)/shard_map/all_to_all | solution.py:15
  23.0 11.4 %all-to-all-start.1 = ((bf16[4,4,2,16,512]{4,3,2,1,0:T(8,128)(2,1)}), bf16[4,4,2,16,512]{4,3,2,1,0:T(8,128)(2,1)S(1)}, u32[]{:S(2)}, u32[]{:S(2)}) async-start(bf16[4,4,2,16,512]{4,3,2,1,0:T(8,128)(2,1)} %broadcast_in_dim.7), calls=%async_computation.1 | async-start | bytes 1048576 | tf_op jit(solution)/shard_map/all_to_all | solution.py:15
  34.4 6.4 %collective-permute-start.1 = (bf16[16,2,16,512]{3,2,1,0:T(8,128)(2,1)S(1)}, bf16[16,2,16,512]{3,2,1,0:T(8,128)(2,1)S(1)}, u32[]{:S(2)}, u32[]{:S(2)}) collective-permute-start(bf16[16,2,16,512]{3,2,1,0:T(8,128)(2,1)S(1)} %bitcast.9), channel_id=1, source_target_pairs={{0,16},{16,0},{1,17},{17,1},{2,18},{18,2},{3,19},{19,3},{4,20},{20... | collective-permute-start | bytes 1572872 | tf_op jit(solution)/shard_map/ppermute | solution.py:23
  36.3 4.4 %collective-permute-start = (s32[2,2]{1,0:T(2,128)S(1)}, s32[2,2]{1,0:T(2,128)S(1)}, u32[]{:S(2)}, u32[]{:S(2)}) collective-permute-start(s32[2,2]{1,0:T(2,128)S(1)} %copy-done.1), channel_id=1, source_target_pairs={{0,16},{16,0},{1,17},{17,1},{2,18},{18,2},{3,19},{19,3},{4,20},{20... | collective-permute-start | bytes 56 | tf_op jit(solution)/shard_map/ppermute | solution.py:23
  40.8 1.3 %copy-start.2 = (bf16[2,2,512,512]{3,2,1,0:T(8,128)(2,1)}, bf16[2,2,512,512]{3,2,1,0:T(8,128)(2,1)S(1)}, u32[]{:S(2)}) copy-start(bf16[2,2,512,512]{3,2,1,0:T(8,128)(2,1)S(1)} %collective-permute-done.2) | copy-start | bytes 6291460
  59.7 12.5 %all-to-all-start.2 = ((bf16[16,2,16,512]{3,2,1,0:T(8,128)(2,1)}), bf16[16,2,16,512]{3,2,1,0:T(8,128)(2,1)S(1)}, u32[]{:S(2)}, u32[]{:S(2)}) async-start(bf16[16,2,16,512]{3,2,1,0:T(8,128)(2,1)} %get-tuple-element.15), calls=%async_computation.2 | async-start | bytes 1048576 | tf_op jit(solution)/shard_map/all_to_all | solution.py:15
  65.3 13.6 %collective-permute-start.4 = (bf16[4,2,16,512]{3,2,1,0:T(8,128)(2,1)S(1)}, bf16[4,2,16,512]{3,2,1,0:T(8,128)(2,1)S(1)}, u32[]{:S(2)}, u32[]{:S(2)}) collective-permute-start(bf16[4,2,16,512]{3,2,1,0:T(8,128)(2,1)S(1)} %reduce_sum.31), channel_id=1, source_target_pairs={{0,1},{1,2},{2,3},{3,4},{4,5},{5,6},{6,7},{7,8},{8,9},{9,10},{10,1... | collective-permute-start | bytes 393224 | tf_op jit(solution)/shard_map/ppermute | solution.py:28

commit v5 on v4

--- a/solution.py
+++ b/solution.py
@@ -37,11 +37,13 @@
 
 
 def fetch_kernel(where_ref, left_ref, right_ref, rows_ref, rights_ref, sems):
+    kdev, sdev = right_ref.shape[:2]
     core = where_ref[1]
     fetches = []
-    for k in range(right_ref.shape[0]):
-        fetches.append(pltpu.make_async_copy(left_ref.at[k, 0, :, core], rows_ref.at[k], sems.at[0, k]))
-        fetches.append(pltpu.make_async_copy(right_ref.at[k, 0], rights_ref.at[k], sems.at[1, k]))
+    for k in range(kdev):
+        for s in range(sdev):
+            fetches.append(pltpu.make_async_copy(left_ref.at[k, s, :, core], rows_ref.at[s, k], sems.at[s, k]))
+        fetches.append(pltpu.make_async_copy(right_ref.at[k, 0], rights_ref.at[k], sems.at[sdev, k]))
     for fetch in fetches:
         fetch.start()
     for fetch in fetches:
@@ -49,39 +51,43 @@
 
 
 def fetched(where, left, right):
-    kdev, _, chips, _, tall, width = left.shape
+    kdev, sdev, chips, _, tall, width = left.shape
     hbm = pl.BlockSpec(memory_space=pltpu.HBM)
     return pl.pallas_call(
         fetch_kernel,
         in_specs=[pl.BlockSpec(memory_space=pltpu.SMEM), hbm, hbm],
         out_specs=[pl.BlockSpec(memory_space=pltpu.VMEM)] * 2,
         out_shape=[
-            pltpu.VMEM((kdev, chips, tall, width), BF16),
+            pltpu.VMEM((sdev, kdev, chips, tall, width), BF16),
             pltpu.VMEM((kdev, width, width), BF16),
         ],
-        scratch_shapes=[pltpu.SemaphoreType.DMA((2, kdev))],
+        scratch_shapes=[pltpu.SemaphoreType.DMA((sdev + 1, kdev))],
         compiler_params=pltpu.CompilerParams(vmem_limit_bytes=2**20),
         name="fetch",
     )(where, in_hbm(left), in_hbm(right))
 
 
-def sums_kernel(where_ref, conn_ref, conn2_ref, dims_ref, near_ref, far_ref, rows0_ref, right0_ref, left_ref, right_ref, left2_ref, right2_ref, own_ref, onward_ref, psi_ref, rows_ref, rights_ref, half_ref, sum_ref, sems):
+def sums_kernel(where_ref, conn_ref, conn2_ref, dims_ref, near_ref, far_ref, rows0_ref, right0_ref, right_ref, left2_ref, right2_ref, own_ref, onward_ref, psi_ref, rows_ref, rights_ref, half_ref, sum_ref, sems):
     kdev, sdev, width, _ = right_ref.shape
     chips, _, tall, _ = near_ref.shape
     group = where_ref[0]
     core = where_ref[1]
     many = chips * tall
-    steps = [(0, 0, rows0_ref, right0_ref, ())]
+    steps = [(0, 0, rows0_ref.at[0], right0_ref, (), ())]
     for whose, s in ((0, 1), (1, 0), (1, 1)):
         n = len(steps) - 1
-        left, right = ((left_ref, right_ref), (left2_ref, right2_ref))[whose]
-        fetches = []
+        rights = (right_ref, right2_ref)[whose]
+        row_copies, right_copies = [], []
+        rows = rows0_ref.at[s]
+        if whose == 1:
+            rows = rows_ref.at[s]
+            for k in range(kdev):
+                row_copies.append(pltpu.make_async_copy(left2_ref.at[k, s, :, core], rows.at[k], sems.at[0, n, k]))
         for k in range(kdev):
-            fetches.append(pltpu.make_async_copy(left.at[k, s, :, core], rows_ref.at[n, k], sems.at[0, n, k]))
-            fetches.append(pltpu.make_async_copy(right.at[k, s], rights_ref.at[n, k], sems.at[1, n, k]))
-        steps.append((whose, s, rows_ref.at[n], rights_ref.at[n], fetches))
-        for fetch in fetches:
+            right_copies.append(pltpu.make_async_copy(rights.at[k, s], rights_ref.at[n, k], sems.at[1, n, k]))
+        for fetch in row_copies + right_copies:
             fetch.start()
+        steps.append((whose, s, rows, rights_ref.at[n], row_copies, right_copies))
     cols = lax.broadcasted_iota(jnp.int32, (tall, width), 1)
     row = lax.broadcasted_iota(jnp.int32, (tall, width), 0)
 
@@ -95,12 +101,14 @@
                 psi_ref[s, pl.ds(start, tall), :] = jnp.where(kept, ref[chip, s].astype(F32), 0.0).astype(BF16)
 
     sum_ref[...] = jnp.zeros_like(sum_ref)
-    for whose, s, rows, rights, fetches in steps:
-        for fetch in fetches:
+    for whose, s, rows, rights, row_copies, right_copies in steps:
+        for fetch in row_copies:
             fetch.wait()
         left = rows[...].reshape(kdev * many, width)
         half_ref[...] = jnp.dot(left, psi_ref[s], preferred_element_type=F32).astype(BF16)
         for k in range(kdev):
+            if right_copies:
+                right_copies[k].wait()
             target = (conn_ref, conn2_ref)[whose][k, s]
             place = target % sdev + jnp.where(target // sdev != group, sdev, 0)
             sum_ref[place] += lax.dot_general(
@@ -115,8 +123,8 @@
             out_ref[chip, t % sdev] = sum_ref[t, chip * tall : (chip + 1) * tall, :].astype(BF16)
 
 
-def slot_sums(where, conn, conn2, dims, near, far, rows0, right0, left, right, left2, right2):
-    kdev, sdev, chips, _, tall, width = left.shape
+def slot_sums(where, conn, conn2, dims, near, far, rows0, right0, right, left2, right2):
+    kdev, sdev, chips, _, tall, width = left2.shape
     assert sdev == 2
     rest = 2 * sdev - 1
     smem = pl.BlockSpec(memory_space=pltpu.SMEM)
@@ -125,12 +133,12 @@
     many = chips * tall
     return pl.pallas_call(
         sums_kernel,
-        in_specs=[smem] * 4 + [vmem] * 4 + [hbm] * 4,
+        in_specs=[smem] * 4 + [vmem] * 4 + [hbm] * 3,
         out_specs=[vmem] * 2,
         out_shape=[pltpu.VMEM((chips, sdev, tall, width), BF16)] * 2,
         scratch_shapes=[
             pltpu.VMEM((sdev, width, width), BF16),
-            pltpu.VMEM((rest, kdev, chips, tall, width), BF16),
+            pltpu.VMEM((sdev, kdev, chips, tall, width), BF16),
             pltpu.VMEM((rest, kdev, width, width), BF16),
             pltpu.VMEM((kdev * many, width), BF16),
             pltpu.VMEM((2 * sdev, many, width), F32),
@@ -138,7 +146,7 @@
         ],
         compiler_params=pltpu.CompilerParams(vmem_limit_bytes=24 * 2**20),
         name="slot_sums",
-    )(where, conn, conn2, dims, *(in_vmem(x) for x in (near, far, rows0, right0)), *(in_hbm(x) for x in (left, right, left2, right2)))
+    )(where, conn, conn2, dims, *(in_vmem(x) for x in (near, far, rows0, right0)), *(in_hbm(x) for x in (right, left2, right2)))
 
 
 def kept_entries(dims, row_start, rows, width):
@@ -161,11 +169,11 @@
     left = left_ops.reshape(by_row)
     rows0, right0 = fetched(where, left, right_ops)
     by_y = shared(psi, "y").reshape(ny, sdev, tall, width)
+    kept = kept_entries(dims, places[2], tall, width)
+    by_y, kept = lax.optimization_barrier((by_y, kept))
     by_x = shared(by_y, "x").reshape(nx * ny, sdev, tall, width)
-    kept = kept_entries(dims, places[2], tall, width)
-    by_x, kept = lax.optimization_barrier((by_x, kept))
     other = from_partner(by_x)
-    own, onward = slot_sums(where, conn, conn2, dims, by_x, other, rows0, right0, left, right_ops, left2, right2)
+    own, onward = slot_sums(where, conn, conn2, dims, by_x, other, rows0, right0, right_ops, left2, right2)
     by_chip = (nx, ny, sdev, tall, width)
     onward = exchanged(onward, "x").reshape(by_chip).astype(F32).sum(axis=0).astype(BF16)
     onward = from_behind(onward)

time: 91.3 us -> 91.3 us (level)
  blocking collectives: 23.4 us -> 34 us
  waiting for transfers between devices: 26.2 us -> 18.9 us
  starting transfers between devices: 28.3 us -> 24.2 us
  Pallas kernels: 7.15 us -> 8.19 us
    all_to_all x2 -> x3, blocking collectives: 23.4 us -> 34 us  [exchanged(): return lax.all_to_all(x, axis, split_axis=0, concat_axis=0, tiled=True)]
    all_to_all x3 -> x2, waiting for transfers between devices: 19.6 us -> 11.7 us  [exchanged(): return lax.all_to_all(x, axis, split_axis=0, concat_axis=0, tiled=True)]
    all_to_all x3 -> x2, starting transfers between devices: 17.4 us -> 12.6 us  [exchanged(): return lax.all_to_all(x, axis, split_axis=0, concat_axis=0, tiled=True)]
  transfers between devices with their start and end apart: 8 -> 7, of which waited for: 4 -> 3; matrix products, arithmetic and copies ran while one was open for 4% -> 4% of each run, Pallas kernels for 2% -> 2%
where the time goes in v5:
time: 91.3 us; the launch traced here: 90.7 us
  blocking collectives  34 us (37%)
  starting transfers between devices  24.2 us (27%)
  waiting for transfers between devices  18.9 us (21%)
  Pallas kernels  8.19 us (9%)
  local copies, waits for them, and re-layouts  2.76 us (3%)
  other arithmetic  2.45 us (3%)
    all_to_all x3, blocking collectives, exchanged(): return lax.all_to_all(x, axis, split_axis=0, concat_axis=0, tiled=True)  34 us
    all_to_all x2, starting transfers between devices, exchanged(): return lax.all_to_all(x, axis, split_axis=0, concat_axis=0, tiled=True)  12.6 us
    all_to_all x2, waiting for transfers between devices, exchanged(): return lax.all_to_all(x, axis, split_axis=0, concat_axis=0, tiled=True)  11.7 us
    ppermute x4, starting transfers between devices, from_partner(): return lax.ppermute(x, 'c', [(0, 1), (1, 0)])  8.77 us
    ppermute x1, waiting for transfers between devices, from_behind(): return lax.ppermute(x, 'sec', [(i, (i + 1) % n) for i in range(n)])  7.21 us
    pallas_call x1, Pallas kernels, slot_sums(): pl.pallas_call(sums_kernel, in_specs=[smem] * 4 + [vmem] * 4 + [hbm] * 3,...  6.07 us
    ppermute x1, starting transfers between devices, from_behind(): return lax.ppermute(x, 'sec', [(i, (i + 1) % n) for i in range(n)])  2.79 us
    pallas_call x1, Pallas kernels, fetched(): pl.pallas_call(fetch_kernel, in_specs=[pl.BlockSpec(memory_space=pltpu.SM...  2.11 us
  transfers between devices with their start and end apart: 7, of which 3 were waited for; matrix products, arithmetic and copies ran while one was open for 4% of the time, Pallas kernels for 2%

profile of v5, /device:TPU:6, one launch (start us, length us, event | category | flops | bytes accessed | tf_op | source)
XLA Modules:
  0.0 90.7 jit_solution(9387811780191738771)
XLA Ops:
  0.0 0.0 copy-start.1
  0.0 2.0 %collective-permute-start.2 = (bf16[2,2,512,512]{3,2,1,0:T(8,128)(2,1)}, bf16[2,2,512,512]{3,2,1,0:T(8,128)(2,1)S(1)}, u32[]{:S(2)}, u32[]{:S(2)}) collective-permute-start(bf16[2,2,512,512]{3,2,1,0:T(8,128)(2,1)} %param.6), channel_id=1, source_target_pairs={{0,16},{16,0},{1,17},{17,1},{2,18},{18,2},{3,19},{19,3},{4,20},{20... | collective-permute-start | bytes 6291464 | tf_op jit(solution)/shard_map/ppermute | solution.py:23
  2.1 2.4 %collective-permute-start.3 = (bf16[2,2,512,512]{3,2,1,0:T(8,128)(2,1)}, bf16[2,2,512,512]{3,2,1,0:T(8,128)(2,1)}, u32[]{:S(2)}, u32[]{:S(2)}) collective-permute-start(bf16[2,2,512,512]{3,2,1,0:T(8,128)(2,1)} %right_ref.3), channel_id=1, source_target_pairs={{0,16},{16,0},{1,17},{17,1},{2,18},{18,2},{3,19},{19,3},{4,20},{20... | collective-permute-start | bytes 6291464 | tf_op jit(solution)/shard_map/ppermute | solution.py:23
  4.5 1.4 %broadcast_in_dim.6 = bf16[4,2,16,512]{3,2,1,0:T(8,128)(2,1)} broadcast(bf16[2,16,512]{2,1,0:T(8,128)(2,1)} %param.5), dimensions={1,2,3} | broadcast | bytes 163840 | tf_op jit(solution)/shard_map/broadcast_in_dim | solution.py:19
  5.9 7.1 %all-to-all-start = ((bf16[4,2,16,512]{3,2,1,0:T(8,128)(2,1)}), bf16[4,2,16,512]{3,2,1,0:T(8,128)(2,1)S(1)}, u32[]{:S(2)}, u32[]{:S(2)}) async-start(bf16[4,2,16,512]{3,2,1,0:T(8,128)(2,1)} %broadcast_in_dim.6), calls=%async_computation | async-start | bytes 262144 | tf_op jit(solution)/shard_map/all_to_all | solution.py:15
  13.0 0.7 broadcast_compare_fusion
  13.7 0.7 iota_compare_fusion
  14.4 0.1 broadcast_and_fusion
  14.5 7.6 %all-to-all-done = bf16[4,2,16,512]{3,2,1,0:T(8,128)(2,1)S(1)} async-done(((bf16[4,2,16,512]{3,2,1,0:T(8,128)(2,1)}), bf16[4,2,16,512]{3,2,1,0:T(8,128)(2,1)S(1)}, u32[]{:S(2)}, u32[]{:S(2)}) %all-to-all-start) | async-done | bytes 131104 | tf_op jit(solution)/shard_map/all_to_all | solution.py:15
  22.2 10.6 %all_to_all.25 = bf16[4,4,2,16,512]{4,3,2,1,0:T(8,128)(2,1)S(1)} all-to-all(bf16[4,4,2,16,512]{4,3,2,1,0:T(8,128)(2,1)S(1)} %broadcast_in_dim.7), channel_id=1, replica_groups=mesh['x'=4,'y'=4,'c'=2,'sec'=16] {'x'}, dimensions={0} | all-to-all | bytes 1048576 | tf_op jit(solution)/shard_map/all_to_all | solution.py:15
  32.8 1.9 %collective-permute-start.1 = (bf16[16,2,16,512]{3,2,1,0:T(8,128)(2,1)S(1)}, bf16[16,2,16,512]{3,2,1,0:T(8,128)(2,1)S(1)}, u32[]{:S(2)}, u32[]{:S(2)}) collective-permute-start(bf16[16,2,16,512]{3,2,1,0:T(8,128)(2,1)S(1)} %bitcast.9), channel_id=1, source_target_pairs={{0,16},{16,0},{1,17},{17,1},{2,18},{18,2},{3,19},{19,3},{4,20},{20... | collective-permute-start | bytes 1572872 | tf_op jit(solution)/shard_map/ppermute | solution.py:23
  34.7 0.0 copy-done.1
  34.7 2.4 %collective-permute-start = (s32[2,2]{1,0:T(2,128)S(1)}, s32[2,2]{1,0:T(2,128)S(1)}, u32[]{:S(2)}, u32[]{:S(2)}) collective-permute-start(s32[2,2]{1,0:T(2,128)S(1)} %copy-done.1), channel_id=1, source_target_pairs={{0,16},{16,0},{1,17},{17,1},{2,18},{18,2},{3,19},{19,3},{4,20},{20... | collective-permute-start | bytes 56 | tf_op jit(solution)/shard_map/ppermute | solution.py:23
  37.1 0.1 pad_add_fusion.where_ref
  37.2 0.0 copy-start
  37.2 2.1 %fetch.1 = (bf16[2,2,16,16,512]{4,3,2,1,0:T(8,128)(2,1)S(1)}, bf16[2,512,512]{2,1,0:T(8,128)(2,1)S(1)}) custom-call(s32[3]{0:T(128)S(1)} %pad_add_fusion.where_ref, bf16[2,2,16,2,16,512]{5,4,3,2,1,0:T(8,128)(2,1)} %bitcast.11, bf16[2,2,512,512]{3,2,1,0:T(8,128)(2,1)} %right_ref.3), custom_call_target="tpu_custom_call" | custom-call | tf_op jit(solution)/shard_map/fetch/pallas_call | solution.py:56
  39.3 0.0 collective-permute-done.conn2_ref
  39.3 0.0 collective-permute-done.1.far_ref
  39.3 0.0 collective-permute-done.2
  39.4 0.0 copy-start.2
  39.4 0.0 collective-permute-done.3.right2_ref
  39.4 1.3 %copy-done.2 = bf16[2,2,512,512]{3,2,1,0:T(8,128)(2,1)} copy-done((bf16[2,2,512,512]{3,2,1,0:T(8,128)(2,1)}, bf16[2,2,512,512]{3,2,1,0:T(8,128)(2,1)S(1)}, u32[]{:S(2)}) %copy-start.2) | copy-done | bytes 2097176
  40.7 0.0 copy-done
  40.7 6.1 %slot_sums.1 = (bf16[16,2,16,512]{3,2,1,0:T(8,128)(2,1)}, bf16[16,2,16,512]{3,2,1,0:T(8,128)(2,1)S(1)}) custom-call(s32[3]{0:T(128)S(1)} %pad_add_fusion.where_ref, s32[2,2]{1,0:T(2,128)S(1)} %copy-done.1, s32[2,2]{1,0:T(2,128)S(1)} %collective-permute-done.conn2_ref, s32[2]{0:T(128)S(1)} %copy-done, bf16[16,2,16,512]{3,2,1,0:T(8,128)(2,1)S(1)} %bitcast.10, ...), custom_call_target="tpu_custom_call" | custom-call | tf_op jit(solution)/shard_map/slot_sums/pallas_call | solution.py:134
  46.7 12.3 %all_to_all.26 = bf16[16,2,16,512]{3,2,1,0:T(8,128)(2,1)S(1)} all-to-all(bf16[16,2,16,512]{3,2,1,0:T(8,128)(2,1)S(1)} %get-tuple-element.16), channel_id=1, replica_groups=mesh['x'=4,'y'=4,'c'=2,'sec'=16] {'x'}, dimensions={0} | all-to-all | bytes 1048576 | tf_op jit(solution)/shard_map/all_to_all | solution.py:15
  59.1 5.5 %all-to-all-start.2 = ((bf16[16,2,16,512]{3,2,1,0:T(8,128)(2,1)}), bf16[16,2,16,512]{3,2,1,0:T(8,128)(2,1)S(1)}, u32[]{:S(2)}, u32[]{:S(2)}) async-start(bf16[16,2,16,512]{3,2,1,0:T(8,128)(2,1)} %get-tuple-element.15), calls=%async_computation.2 | async-start | bytes 1048576 | tf_op jit(solution)/shard_map/all_to_all | solution.py:15
  64.6 0.1 reduce_sum.31
  64.7 2.8 %collective-permute-start.4 = (bf16[4,2,16,512]{3,2,1,0:T(8,128)(2,1)S(1)}, bf16[4,2,16,512]{3,2,1,0:T(8,128)(2,1)S(1)}, u32[]{:S(2)}, u32[]{:S(2)}) collective-permute-start(bf16[4,2,16,512]{3,2,1,0:T(8,128)(2,1)S(1)} %reduce_sum.31), channel_id=1, source_target_pairs={{0,1},{1,2},{2,3},{3,4},{4,5},{5,6},{6,7},{7,8},{8,9},{9,10},{10,1... | collective-permute-start | bytes 393224 | tf_op jit(solution)/shard_map/ppermute | solution.py:28
  67.5 4.1 %all-to-all-done.2 = bf16[16,2,16,512]{3,2,1,0:T(8,128)(2,1)S(1)} async-done(((bf16[16,2,16,512]{3,2,1,0:T(8,128)(2,1)}), bf16[16,2,16,512]{3,2,1,0:T(8,128)(2,1)S(1)}, u32[]{:S(2)}, u32[]{:S(2)}) %all-to-all-start.2) | async-done | bytes 524320 | tf_op jit(solution)/shard_map/all_to_all | solution.py:15
  71.6 0.1 convert_reduce_fusion
  71.7 7.2 %collective-permute-done.4 = bf16[4,2,16,512]{3,2,1,0:T(8,128)(2,1)S(1)} collective-permute-done((bf16[4,2,16,512]{3,2,1,0:T(8,128)(2,1)S(1)}, bf16[4,2,16,512]{3,2,1,0:T(8,128)(2,1)S(1)}, u32[]{:S(2)}, u32[]{:S(2)}) %collective-permute-start.4) | collective-permute-done | bytes 131104 | tf_op jit(solution)/shard_map/ppermute | solution.py:28
  78.9 11.1 %all_to_all.27 = bf16[4,2,16,512]{3,2,1,0:T(8,128)(2,1)S(1)} all-to-all(bf16[4,2,16,512]{3,2,1,0:T(8,128)(2,1)S(1)} %add_convert_fusion), channel_id=1, replica_groups=mesh['x'=4,'y'=4,'c'=2,'sec'=16] {'y'}, dimensions={0} | all-to-all | bytes 262144 | tf_op jit(solution)/shard_map/all_to_all | solution.py:15
  90.0 0.6 select_convert_fusion
  (4 shorter events, 0.1 us)
Async XLA Ops:
  0.0 34.7 %copy-start.1 = (s32[2,2]{1,0:T(2,128)S(1)}, s32[2,2]{1,0:T(2,128)}, u32[]{:S(2)}) copy-start(s32[2,2]{1,0:T(2,128)} %conn_ref.1) | copy-start | bytes 52
  0.0 39.3 %collective-permute-start.2 = (bf16[2,2,512,512]{3,2,1,0:T(8,128)(2,1)}, bf16[2,2,512,512]{3,2,1,0:T(8,128)(2,1)S(1)}, u32[]{:S(2)}, u32[]{:S(2)}) collective-permute-start(bf16[2,2,512,512]{3,2,1,0:T(8,128)(2,1)} %param.6), channel_id=1, source_target_pairs={{0,16},{16,0},{1,17},{17,1},{2,18},{18,2},{3,19},{19,3},{4,20},{20... | collective-permute-start | bytes 6291464 | tf_op jit(solution)/shard_map/ppermute | solution.py:23
  2.1 37.3 %collective-permute-start.3 = (bf16[2,2,512,512]{3,2,1,0:T(8,128)(2,1)}, bf16[2,2,512,512]{3,2,1,0:T(8,128)(2,1)}, u32[]{:S(2)}, u32[]{:S(2)}) collective-permute-start(bf16[2,2,512,512]{3,2,1,0:T(8,128)(2,1)} %right_ref.3), channel_id=1, source_target_pairs={{0,16},{16,0},{1,17},{17,1},{2,18},{18,2},{3,19},{19,3},{4,20},{20... | collective-permute-start | bytes 6291464 | tf_op jit(solution)/shard_map/ppermute | solution.py:23
  5.9 16.2 %all-to-all-start = ((bf16[4,2,16,512]{3,2,1,0:T(8,128)(2,1)}), bf16[4,2,16,512]{3,2,1,0:T(8,128)(2,1)S(1)}, u32[]{:S(2)}, u32[]{:S(2)}) async-start(bf16[4,2,16,512]{3,2,1,0:T(8,128)(2,1)} %broadcast_in_dim.6), calls=%async_computation | async-start | bytes 262144 | tf_op jit(solution)/shard_map/all_to_all | solution.py:15
  32.8 6.6 %collective-permute-start.1 = (bf16[16,2,16,512]{3,2,1,0:T(8,128)(2,1)S(1)}, bf16[16,2,16,512]{3,2,1,0:T(8,128)(2,1)S(1)}, u32[]{:S(2)}, u32[]{:S(2)}) collective-permute-start(bf16[16,2,16,512]{3,2,1,0:T(8,128)(2,1)S(1)} %bitcast.9), channel_id=1, source_target_pairs={{0,16},{16,0},{1,17},{17,1},{2,18},{18,2},{3,19},{19,3},{4,20},{20... | collective-permute-start | bytes 1572872 | tf_op jit(solution)/shard_map/ppermute | solution.py:23
  34.7 4.6 %collective-permute-start = (s32[2,2]{1,0:T(2,128)S(1)}, s32[2,2]{1,0:T(2,128)S(1)}, u32[]{:S(2)}, u32[]{:S(2)}) collective-permute-start(s32[2,2]{1,0:T(2,128)S(1)} %copy-done.1), channel_id=1, source_target_pairs={{0,16},{16,0},{1,17},{17,1},{2,18},{18,2},{3,19},{19,3},{4,20},{20... | collective-permute-start | bytes 56 | tf_op jit(solution)/shard_map/ppermute | solution.py:23
  37.2 3.5 %copy-start = (s32[2]{0:T(128)S(1)}, s32[2]{0:T(128)}, u32[]{:S(2)}) copy-start(s32[2]{0:T(128)} %dims_ref.1) | copy-start | bytes 28
  39.4 1.3 %copy-start.2 = (bf16[2,2,512,512]{3,2,1,0:T(8,128)(2,1)}, bf16[2,2,512,512]{3,2,1,0:T(8,128)(2,1)S(1)}, u32[]{:S(2)}) copy-start(bf16[2,2,512,512]{3,2,1,0:T(8,128)(2,1)S(1)} %collective-permute-done.2) | copy-start | bytes 6291460
  59.1 12.5 %all-to-all-start.2 = ((bf16[16,2,16,512]{3,2,1,0:T(8,128)(2,1)}), bf16[16,2,16,512]{3,2,1,0:T(8,128)(2,1)S(1)}, u32[]{:S(2)}, u32[]{:S(2)}) async-start(bf16[16,2,16,512]{3,2,1,0:T(8,128)(2,1)} %get-tuple-element.15), calls=%async_computation.2 | async-start | bytes 1048576 | tf_op jit(solution)/shard_map/all_to_all | solution.py:15
  64.7 14.2 %collective-permute-start.4 = (bf16[4,2,16,512]{3,2,1,0:T(8,128)(2,1)S(1)}, bf16[4,2,16,512]{3,2,1,0:T(8,128)(2,1)S(1)}, u32[]{:S(2)}, u32[]{:S(2)}) collective-permute-start(bf16[4,2,16,512]{3,2,1,0:T(8,128)(2,1)S(1)} %reduce_sum.31), channel_id=1, source_target_pairs={{0,1},{1,2},{2,3},{3,4},{4,5},{5,6},{6,7},{7,8},{8,9},{9,10},{10,1... | collective-permute-start | bytes 393224 | tf_op jit(solution)/shard_map/ppermute | solution.py:28

commit v6 on v5

--- a/solution.py
+++ b/solution.py
@@ -23,9 +23,14 @@
     return lax.ppermute(x, "c", [(0, 1), (1, 0)])
 
 
-def from_behind(x):
+def around(x):
     n = lax.axis_size("sec")
-    return lax.ppermute(x, "sec", [(i, (i + 1) % n) for i in range(n)])
+    return lax.ppermute(x, "sec", [(n - 1, 0)])
+
+
+def ahead(x):
+    n = lax.axis_size("sec")
+    return lax.ppermute(x, "sec", [(i, i + 1) for i in range(n - 1)])
 
 
 def in_vmem(x):
@@ -67,27 +72,26 @@
     )(where, in_hbm(left), in_hbm(right))
 
 
-def sums_kernel(where_ref, conn_ref, conn2_ref, dims_ref, near_ref, far_ref, rows0_ref, right0_ref, right_ref, left2_ref, right2_ref, own_ref, onward_ref, psi_ref, rows_ref, rights_ref, half_ref, sum_ref, sems):
+def sums_kernel(where_ref, conn_ref, conn2_ref, dims_ref, near_ref, far_ref, rows0_ref, right0_ref, right_ref, left2_ref, right2_ref, own_ref, onward_ref, psi_ref, rows_ref, rights_ref, half_ref, sum_ref, staged_ref, sems, out_sem):
     kdev, sdev, width, _ = right_ref.shape
     chips, _, tall, _ = near_ref.shape
     group = where_ref[0]
     core = where_ref[1]
     many = chips * tall
-    steps = [(0, 0, rows0_ref.at[0], right0_ref, (), ())]
+    steps = [(0, 0, rows0_ref.at[0], right0_ref, ())]
     for whose, s in ((0, 1), (1, 0), (1, 1)):
         n = len(steps) - 1
         rights = (right_ref, right2_ref)[whose]
-        row_copies, right_copies = [], []
+        fetches = []
         rows = rows0_ref.at[s]
-        if whose == 1:
-            rows = rows_ref.at[s]
-            for k in range(kdev):
-                row_copies.append(pltpu.make_async_copy(left2_ref.at[k, s, :, core], rows.at[k], sems.at[0, n, k]))
         for k in range(kdev):
-            right_copies.append(pltpu.make_async_copy(rights.at[k, s], rights_ref.at[n, k], sems.at[1, n, k]))
-        for fetch in row_copies + right_copies:
+            if whose == 1:
+                rows = rows_ref.at[s]
+                fetches.append(pltpu.make_async_copy(left2_ref.at[k, s, :, core], rows.at[k], sems.at[0, n, k]))
+            fetches.append(pltpu.make_async_copy(rights.at[k, s], rights_ref.at[n, k], sems.at[1, n, k]))
+        for fetch in fetches:
             fetch.start()
-        steps.append((whose, s, rows, rights_ref.at[n], row_copies, right_copies))
+        steps.append((whose, s, rows, rights_ref.at[n], fetches))
     cols = lax.broadcasted_iota(jnp.int32, (tall, width), 1)
     row = lax.broadcasted_iota(jnp.int32, (tall, width), 0)
 
@@ -101,14 +105,12 @@
                 psi_ref[s, pl.ds(start, tall), :] = jnp.where(kept, ref[chip, s].astype(F32), 0.0).astype(BF16)
 
     sum_ref[...] = jnp.zeros_like(sum_ref)
-    for whose, s, rows, rights, row_copies, right_copies in steps:
-        for fetch in row_copies:
+    for whose, s, rows, rights, fetches in steps:
+        for fetch in fetches:
             fetch.wait()
         left = rows[...].reshape(kdev * many, width)
         half_ref[...] = jnp.dot(left, psi_ref[s], preferred_element_type=F32).astype(BF16)
         for k in range(kdev):
-            if right_copies:
-                right_copies[k].wait()
             target = (conn_ref, conn2_ref)[whose][k, s]
             place = target % sdev + jnp.where(target // sdev != group, sdev, 0)
             sum_ref[place] += lax.dot_general(
@@ -117,16 +119,26 @@
                 (((1,), (1,)), ((), ())),
                 preferred_element_type=F32,
             )
-    for t in range(2 * sdev):
-        out_ref = (own_ref, onward_ref)[t // sdev]
-        for chip in range(chips):
-            out_ref[chip, t % sdev] = sum_ref[t, chip * tall : (chip + 1) * tall, :].astype(BF16)
+    for chip in range(chips):
+        for t in range(sdev):
+            staged_ref[chip, t] = sum_ref[t, chip * tall : (chip + 1) * tall, :].astype(BF16)
+    leave = pltpu.make_async_copy(staged_ref, own_ref, out_sem)
+    leave.start()
+
+    @pl.loop(0, chips)
+    def _(chip):
+        start = pl.multiple_of(chip * tall, tall)
+        for t in range(sdev):
+            onward_ref[chip, t] = sum_ref[sdev + t, pl.ds(start, tall), :].astype(BF16)
+
+    leave.wait()
 
 
 def slot_sums(where, conn, conn2, dims, near, far, rows0, right0, right, left2, right2):
     kdev, sdev, chips, _, tall, width = left2.shape
     assert sdev == 2
     rest = 2 * sdev - 1
+    block = (chips, sdev, tall, width)
     smem = pl.BlockSpec(memory_space=pltpu.SMEM)
     vmem = pl.BlockSpec(memory_space=pltpu.VMEM)
     hbm = pl.BlockSpec(memory_space=pltpu.HBM)
@@ -134,15 +146,17 @@
     return pl.pallas_call(
         sums_kernel,
         in_specs=[smem] * 4 + [vmem] * 4 + [hbm] * 3,
-        out_specs=[vmem] * 2,
-        out_shape=[pltpu.VMEM((chips, sdev, tall, width), BF16)] * 2,
+        out_specs=[hbm, vmem],
+        out_shape=[pltpu.HBM(block, BF16), pltpu.VMEM(block, BF16)],
         scratch_shapes=[
             pltpu.VMEM((sdev, width, width), BF16),
             pltpu.VMEM((sdev, kdev, chips, tall, width), BF16),
             pltpu.VMEM((rest, kdev, width, width), BF16),
             pltpu.VMEM((kdev * many, width), BF16),
             pltpu.VMEM((2 * sdev, many, width), F32),
+            pltpu.VMEM(block, BF16),
             pltpu.SemaphoreType.DMA((2, rest, kdev)),
+            pltpu.SemaphoreType.DMA,
         ],
         compiler_params=pltpu.CompilerParams(vmem_limit_bytes=24 * 2**20),
         name="slot_sums",
@@ -169,16 +183,17 @@
     left = left_ops.reshape(by_row)
     rows0, right0 = fetched(where, left, right_ops)
     by_y = shared(psi, "y").reshape(ny, sdev, tall, width)
+    by_x = shared(by_y, "x").reshape(nx * ny, sdev, tall, width)
     kept = kept_entries(dims, places[2], tall, width)
-    by_y, kept = lax.optimization_barrier((by_y, kept))
-    by_x = shared(by_y, "x").reshape(nx * ny, sdev, tall, width)
+    by_x, kept = lax.optimization_barrier((by_x, kept))
     other = from_partner(by_x)
     own, onward = slot_sums(where, conn, conn2, dims, by_x, other, rows0, right0, right_ops, left2, right2)
     by_chip = (nx, ny, sdev, tall, width)
     onward = exchanged(onward, "x").reshape(by_chip).astype(F32).sum(axis=0).astype(BF16)
-    onward = from_behind(onward)
+    far = around(onward)
+    near = ahead(onward)
     own = exchanged(own, "x").reshape(by_chip).astype(F32).sum(axis=0)
-    summed = exchanged((own + onward.astype(F32)).astype(BF16), "y").astype(F32).sum(axis=0)
+    summed = exchanged((own + far.astype(F32) + near.astype(F32)).astype(BF16), "y").astype(F32).sum(axis=0)
     return jnp.where(kept, summed, jnp.zeros_like(summed)).astype(BF16)
 
 

time: 91.3 us -> 92 us (level)
  blocking collectives: 34 us -> 23.4 us
  waiting for transfers between devices: 18.9 us -> 25.6 us
  starting transfers between devices: 24.2 us -> 29.6 us
  Pallas kernels: 8.19 us -> 7.16 us
    all_to_all x3 -> x2, blocking collectives: 34 us -> 23.4 us  [exchanged(): return lax.all_to_all(x, axis, split_axis=0, concat_axis=0, tiled=True)]
    all_to_all x2 -> x3, waiting for transfers between devices: 11.7 us -> 18.3 us  [exchanged(): return lax.all_to_all(x, axis, split_axis=0, concat_axis=0, tiled=True)]
    all_to_all x2 -> x3, starting transfers between devices: 12.6 us -> 17.4 us  [exchanged(): return lax.all_to_all(x, axis, split_axis=0, concat_axis=0, tiled=True)]
    pallas_call x1, Pallas kernels: 6.07 us -> 5.05 us  [slot_sums(): pl.pallas_call(sums_kernel, in_specs=[smem] * 4 + [vmem] * 4 + [hbm] * 3,...]
    ppermute x1 -> x2, starting transfers between devices: 2.79 us -> 3.45 us  [the longest x1 2.15 us: ahead(): return lax.ppermute(x, 'sec', [(i, i + 1) for i in range(n - 1)])]
    ppermute x1 -> x2, waiting for transfers between devices: 7.21 us -> 7.23 us  [the longest x1 7.23 us: around(): return lax.ppermute(x, 'sec', [(n - 1, 0)])]
  transfers between devices with their start and end apart: 7 -> 9, of which waited for: 3 -> 4; matrix products, arithmetic and copies ran while one was open for 4% -> 4% of each run, Pallas kernels for 2% -> 2%
where the time goes in v6:
time: 92 us; the launch traced here: 91.3 us
  starting transfers between devices  29.6 us (32%)
  waiting for transfers between devices  25.6 us (28%)
  blocking collectives  23.4 us (25%)
  Pallas kernels  7.16 us (8%)
  local copies, waits for them, and re-layouts  3.58 us (4%)
  other arithmetic  1.82 us (2%)
    all_to_all x2, blocking collectives, exchanged(): return lax.all_to_all(x, axis, split_axis=0, concat_axis=0, tiled=True)  23.4 us
    all_to_all x3, waiting for transfers between devices, exchanged(): return lax.all_to_all(x, axis, split_axis=0, concat_axis=0, tiled=True)  18.3 us
    all_to_all x3, starting transfers between devices, exchanged(): return lax.all_to_all(x, axis, split_axis=0, concat_axis=0, tiled=True)  17.4 us
    ppermute x4, starting transfers between devices, from_partner(): return lax.ppermute(x, 'c', [(0, 1), (1, 0)])  8.77 us
    ppermute x1, waiting for transfers between devices, around(): return lax.ppermute(x, 'sec', [(n - 1, 0)])  7.23 us
    pallas_call x1, Pallas kernels, slot_sums(): pl.pallas_call(sums_kernel, in_specs=[smem] * 4 + [vmem] * 4 + [hbm] * 3,...  5.05 us
    broadcast_in_dim x2, local copies, waits for them, and re-layouts, shared(): jnp.broadcast_to(x[None], (lax.axis_size(axis),) + x.shape)  2.29 us
    ppermute x1, starting transfers between devices, ahead(): return lax.ppermute(x, 'sec', [(i, i + 1) for i in range(n - 1)])  2.15 us
  transfers between devices with their start and end apart: 9, of which 4 were waited for; matrix products, arithmetic and copies ran while one was open for 4% of the time, Pallas kernels for 2%

profile of v6, /device:TPU:6, one launch (start us, length us, event | category | flops | bytes accessed | tf_op | source)
XLA Modules:
  0.0 91.3 jit_solution(10094788872080940954)
XLA Ops:
  0.0 0.0 copy-start
  0.0 0.0 copy-start.1
  0.0 2.0 %collective-permute-start.2 = (bf16[2,2,512,512]{3,2,1,0:T(8,128)(2,1)}, bf16[2,2,512,512]{3,2,1,0:T(8,128)(2,1)S(1)}, u32[]{:S(2)}, u32[]{:S(2)}) collective-permute-start(bf16[2,2,512,512]{3,2,1,0:T(8,128)(2,1)} %param.6), channel_id=1, source_target_pairs={{0,16},{16,0},{1,17},{17,1},{2,18},{18,2},{3,19},{19,3},{4,20},{20... | collective-permute-start | bytes 6291464 | tf_op jit(solution)/shard_map/ppermute | solution.py:23
  2.1 2.4 %collective-permute-start.3 = (bf16[2,2,512,512]{3,2,1,0:T(8,128)(2,1)}, bf16[2,2,512,512]{3,2,1,0:T(8,128)(2,1)}, u32[]{:S(2)}, u32[]{:S(2)}) collective-permute-start(bf16[2,2,512,512]{3,2,1,0:T(8,128)(2,1)} %right_ref.3), channel_id=1, source_target_pairs={{0,16},{16,0},{1,17},{17,1},{2,18},{18,2},{3,19},{19,3},{4,20},{20... | collective-permute-start | bytes 6291464 | tf_op jit(solution)/shard_map/ppermute | solution.py:23
  4.5 1.4 %broadcast_in_dim.6 = bf16[4,2,16,512]{3,2,1,0:T(8,128)(2,1)} broadcast(bf16[2,16,512]{2,1,0:T(8,128)(2,1)} %param.5), dimensions={1,2,3} | broadcast | bytes 163840 | tf_op jit(solution)/shard_map/broadcast_in_dim | solution.py:19
  5.9 7.1 %all-to-all-start = ((bf16[4,2,16,512]{3,2,1,0:T(8,128)(2,1)}), bf16[4,2,16,512]{3,2,1,0:T(8,128)(2,1)S(1)}, u32[]{:S(2)}, u32[]{:S(2)}) async-start(bf16[4,2,16,512]{3,2,1,0:T(8,128)(2,1)} %broadcast_in_dim.6), calls=%async_computation | async-start | bytes 262144 | tf_op jit(solution)/shard_map/all_to_all | solution.py:15
  13.0 0.7 iota_compare_fusion
  13.7 8.4 %all-to-all-done = bf16[4,2,16,512]{3,2,1,0:T(8,128)(2,1)S(1)} async-done(((bf16[4,2,16,512]{3,2,1,0:T(8,128)(2,1)}), bf16[4,2,16,512]{3,2,1,0:T(8,128)(2,1)S(1)}, u32[]{:S(2)}, u32[]{:S(2)}) %all-to-all-start) | async-done | bytes 131104 | tf_op jit(solution)/shard_map/all_to_all | solution.py:15
  22.1 0.9 broadcast_in_dim.7
  23.0 4.8 %all-to-all-start.1 = ((bf16[4,4,2,16,512]{4,3,2,1,0:T(8,128)(2,1)}), bf16[4,4,2,16,512]{4,3,2,1,0:T(8,128)(2,1)S(1)}, u32[]{:S(2)}, u32[]{:S(2)}) async-start(bf16[4,4,2,16,512]{4,3,2,1,0:T(8,128)(2,1)} %broadcast_in_dim.7), calls=%async_computation.1 | async-start | bytes 1048576 | tf_op jit(solution)/shard_map/all_to_all | solution.py:15
  27.8 0.0 copy-done
  27.8 0.1 broadcast_compare_fusion
  27.9 0.1 broadcast_and_fusion
  28.0 6.5 %all-to-all-done.1 = bf16[4,4,2,16,512]{4,3,2,1,0:T(8,128)(2,1)S(1)} async-done(((bf16[4,4,2,16,512]{4,3,2,1,0:T(8,128)(2,1)}), bf16[4,4,2,16,512]{4,3,2,1,0:T(8,128)(2,1)S(1)}, u32[]{:S(2)}, u32[]{:S(2)}) %all-to-all-start.1) | async-done | bytes 524320 | tf_op jit(solution)/shard_map/all_to_all | solution.py:15
  34.4 1.9 %collective-permute-start.1 = (bf16[16,2,16,512]{3,2,1,0:T(8,128)(2,1)S(1)}, bf16[16,2,16,512]{3,2,1,0:T(8,128)(2,1)S(1)}, u32[]{:S(2)}, u32[]{:S(2)}) collective-permute-start(bf16[16,2,16,512]{3,2,1,0:T(8,128)(2,1)S(1)} %bitcast.9), channel_id=1, source_target_pairs={{0,16},{16,0},{1,17},{17,1},{2,18},{18,2},{3,19},{19,3},{4,20},{20... | collective-permute-start | bytes 1572872 | tf_op jit(solution)/shard_map/ppermute | solution.py:23
  36.3 0.0 copy-done.1
  36.3 2.4 %collective-permute-start = (s32[2,2]{1,0:T(2,128)S(1)}, s32[2,2]{1,0:T(2,128)S(1)}, u32[]{:S(2)}, u32[]{:S(2)}) collective-permute-start(s32[2,2]{1,0:T(2,128)S(1)} %copy-done.1), channel_id=1, source_target_pairs={{0,16},{16,0},{1,17},{17,1},{2,18},{18,2},{3,19},{19,3},{4,20},{20... | collective-permute-start | bytes 56 | tf_op jit(solution)/shard_map/ppermute | solution.py:23
  38.8 0.1 pad_add_fusion.where_ref
  38.8 2.1 %fetch.1 = (bf16[2,2,16,16,512]{4,3,2,1,0:T(8,128)(2,1)S(1)}, bf16[2,512,512]{2,1,0:T(8,128)(2,1)S(1)}) custom-call(s32[3]{0:T(128)S(1)} %pad_add_fusion.where_ref, bf16[2,2,16,2,16,512]{5,4,3,2,1,0:T(8,128)(2,1)} %bitcast.11, bf16[2,2,512,512]{3,2,1,0:T(8,128)(2,1)} %right_ref.3), custom_call_target="tpu_custom_call" | custom-call | tf_op jit(solution)/shard_map/fetch/pallas_call | solution.py:61
  41.0 0.0 collective-permute-done.conn2_ref
  41.0 0.0 collective-permute-done.1.far_ref
  41.0 0.0 collective-permute-done.2
  41.0 0.0 copy-start.2
  41.0 0.0 collective-permute-done.3.right2_ref
  41.0 1.3 %copy-done.2 = bf16[2,2,512,512]{3,2,1,0:T(8,128)(2,1)} copy-done((bf16[2,2,512,512]{3,2,1,0:T(8,128)(2,1)}, bf16[2,2,512,512]{3,2,1,0:T(8,128)(2,1)S(1)}, u32[]{:S(2)}) %copy-start.2) | copy-done | bytes 2097176
  42.3 5.0 %slot_sums.1 = (bf16[16,2,16,512]{3,2,1,0:T(8,128)(2,1)}, bf16[16,2,16,512]{3,2,1,0:T(8,128)(2,1)S(1)}) custom-call(s32[3]{0:T(128)S(1)} %pad_add_fusion.where_ref, s32[2,2]{1,0:T(2,128)S(1)} %copy-done.1, s32[2,2]{1,0:T(2,128)S(1)} %collective-permute-done.conn2_ref, s32[2]{0:T(128)S(1)} %copy-done, bf16[16,2,16,512]{3,2,1,0:T(8,128)(2,1)S(1)} %bitcast.10, ...), custom_call_target="tpu_custom_call" | custom-call | tf_op jit(solution)/shard_map/slot_sums/pallas_call | solution.py:146
  47.4 12.3 %all_to_all.25 = bf16[16,2,16,512]{3,2,1,0:T(8,128)(2,1)S(1)} all-to-all(bf16[16,2,16,512]{3,2,1,0:T(8,128)(2,1)S(1)} %get-tuple-element.16), channel_id=1, replica_groups=mesh['x'=4,'y'=4,'c'=2,'sec'=16] {'x'}, dimensions={0} | all-to-all | bytes 1048576 | tf_op jit(solution)/shard_map/all_to_all | solution.py:15
  59.7 5.5 %all-to-all-start.2 = ((bf16[16,2,16,512]{3,2,1,0:T(8,128)(2,1)}), bf16[16,2,16,512]{3,2,1,0:T(8,128)(2,1)S(1)}, u32[]{:S(2)}, u32[]{:S(2)}) async-start(bf16[16,2,16,512]{3,2,1,0:T(8,128)(2,1)} %get-tuple-element.15), calls=%async_computation.2 | async-start | bytes 1048576 | tf_op jit(solution)/shard_map/all_to_all | solution.py:15
  65.2 0.1 reduce_sum.31
  65.3 2.2 %collective-permute-start.5 = (bf16[4,2,16,512]{3,2,1,0:T(8,128)(2,1)S(1)}, bf16[4,2,16,512]{3,2,1,0:T(8,128)(2,1)S(1)}, u32[]{:S(2)}, u32[]{:S(2)}) collective-permute-start(bf16[4,2,16,512]{3,2,1,0:T(8,128)(2,1)S(1)} %reduce_sum.31), channel_id=1, source_target_pairs={{0,1},{1,2},{2,3},{3,4},{4,5},{5,6},{6,7},{7,8},{8,9},{9,10},{10,1... | collective-permute-start | bytes 393224 | tf_op jit(solution)/shard_map/ppermute | solution.py:33
  67.4 1.3 %collective-permute-start.4 = (bf16[4,2,16,512]{3,2,1,0:T(8,128)(2,1)S(1)}, bf16[4,2,16,512]{3,2,1,0:T(8,128)(2,1)S(1)}, u32[]{:S(2)}, u32[]{:S(2)}) collective-permute-start(bf16[4,2,16,512]{3,2,1,0:T(8,128)(2,1)S(1)} %reduce_sum.31), channel_id=1, source_target_pairs={{15,0},{31,16},{47,32},{63,48},{79,64},{95,80},{111,96},{127,112},... | collective-permute-start | bytes 393224 | tf_op jit(solution)/shard_map/ppermute | solution.py:28
  68.7 3.5 %all-to-all-done.2 = bf16[16,2,16,512]{3,2,1,0:T(8,128)(2,1)S(1)} async-done(((bf16[16,2,16,512]{3,2,1,0:T(8,128)(2,1)}), bf16[16,2,16,512]{3,2,1,0:T(8,128)(2,1)S(1)}, u32[]{:S(2)}, u32[]{:S(2)}) %all-to-all-start.2) | async-done | bytes 524320 | tf_op jit(solution)/shard_map/all_to_all | solution.py:15
  72.2 0.1 convert_reduce_fusion
  72.3 0.0 collective-permute-done.5
  72.3 7.2 %collective-permute-done.4 = bf16[4,2,16,512]{3,2,1,0:T(8,128)(2,1)S(1)} collective-permute-done((bf16[4,2,16,512]{3,2,1,0:T(8,128)(2,1)S(1)}, bf16[4,2,16,512]{3,2,1,0:T(8,128)(2,1)S(1)}, u32[]{:S(2)}, u32[]{:S(2)}) %collective-permute-start.4) | collective-permute-done | bytes 131104 | tf_op jit(solution)/shard_map/ppermute | solution.py:28
  79.6 11.1 %all_to_all.26 = bf16[4,2,16,512]{3,2,1,0:T(8,128)(2,1)S(1)} all-to-all(bf16[4,2,16,512]{3,2,1,0:T(8,128)(2,1)S(1)} %add_convert_fusion), channel_id=1, replica_groups=mesh['x'=4,'y'=4,'c'=2,'sec'=16] {'y'}, dimensions={0} | all-to-all | bytes 262144 | tf_op jit(solution)/shard_map/all_to_all | solution.py:15
  90.7 0.6 select_convert_fusion
  (3 shorter events, 0.1 us)
Async XLA Ops:
  0.0 27.8 %copy-start = (s32[2]{0:T(128)S(1)}, s32[2]{0:T(128)}, u32[]{:S(2)}) copy-start(s32[2]{0:T(128)} %dims_ref.1) | copy-start | bytes 28
  0.0 36.3 %copy-start.1 = (s32[2,2]{1,0:T(2,128)S(1)}, s32[2,2]{1,0:T(2,128)}, u32[]{:S(2)}) copy-start(s32[2,2]{1,0:T(2,128)} %conn_ref.1) | copy-start | bytes 52
  0.0 41.0 %collective-permute-start.2 = (bf16[2,2,512,512]{3,2,1,0:T(8,128)(2,1)}, bf16[2,2,512,512]{3,2,1,0:T(8,128)(2,1)S(1)}, u32[]{:S(2)}, u32[]{:S(2)}) collective-permute-start(bf16[2,2,512,512]{3,2,1,0:T(8,128)(2,1)} %param.6), channel_id=1, source_target_pairs={{0,16},{16,0},{1,17},{17,1},{2,18},{18,2},{3,19},{19,3},{4,20},{20... | collective-permute-start | bytes 6291464 | tf_op jit(solution)/shard_map/ppermute | solution.py:23
  2.1 39.0 %collective-permute-start.3 = (bf16[2,2,512,512]{3,2,1,0:T(8,128)(2,1)}, bf16[2,2,512,512]{3,2,1,0:T(8,128)(2,1)}, u32[]{:S(2)}, u32[]{:S(2)}) collective-permute-start(bf16[2,2,512,512]{3,2,1,0:T(8,128)(2,1)} %right_ref.3), channel_id=1, source_target_pairs={{0,16},{16,0},{1,17},{17,1},{2,18},{18,2},{3,19},{19,3},{4,20},{20... | collective-permute-start | bytes 6291464 | tf_op jit(solution)/shard_map/ppermute | solution.py:23
  5.9 16.2 %all-to-all-start = ((bf16[4,2,16,512]{3,2,1,0:T(8,128)(2,1)}), bf16[4,2,16,512]{3,2,1,0:T(8,128)(2,1)S(1)}, u32[]{:S(2)}, u32[]{:S(2)}) async-start(bf16[4,2,16,512]{3,2,1,0:T(8,128)(2,1)} %broadcast_in_dim.6), calls=%async_computation | async-start | bytes 262144 | tf_op jit(solution)/shard_map/all_to_all | solution.py:15
  23.0 11.4 %all-to-all-start.1 = ((bf16[4,4,2,16,512]{4,3,2,1,0:T(8,128)(2,1)}), bf16[4,4,2,16,512]{4,3,2,1,0:T(8,128)(2,1)S(1)}, u32[]{:S(2)}, u32[]{:S(2)}) async-start(bf16[4,4,2,16,512]{4,3,2,1,0:T(8,128)(2,1)} %broadcast_in_dim.7), calls=%async_computation.1 | async-start | bytes 1048576 | tf_op jit(solution)/shard_map/all_to_all | solution.py:15
  34.4 6.6 %collective-permute-start.1 = (bf16[16,2,16,512]{3,2,1,0:T(8,128)(2,1)S(1)}, bf16[16,2,16,512]{3,2,1,0:T(8,128)(2,1)S(1)}, u32[]{:S(2)}, u32[]{:S(2)}) collective-permute-start(bf16[16,2,16,512]{3,2,1,0:T(8,128)(2,1)S(1)} %bitcast.9), channel_id=1, source_target_pairs={{0,16},{16,0},{1,17},{17,1},{2,18},{18,2},{3,19},{19,3},{4,20},{20... | collective-permute-start | bytes 1572872 | tf_op jit(solution)/shard_map/ppermute | solution.py:23
  36.3 4.6 %collective-permute-start = (s32[2,2]{1,0:T(2,128)S(1)}, s32[2,2]{1,0:T(2,128)S(1)}, u32[]{:S(2)}, u32[]{:S(2)}) collective-permute-start(s32[2,2]{1,0:T(2,128)S(1)} %copy-done.1), channel_id=1, source_target_pairs={{0,16},{16,0},{1,17},{17,1},{2,18},{18,2},{3,19},{19,3},{4,20},{20... | collective-permute-start | bytes 56 | tf_op jit(solution)/shard_map/ppermute | solution.py:23
  41.0 1.3 %copy-start.2 = (bf16[2,2,512,512]{3,2,1,0:T(8,128)(2,1)}, bf16[2,2,512,512]{3,2,1,0:T(8,128)(2,1)S(1)}, u32[]{:S(2)}) copy-start(bf16[2,2,512,512]{3,2,1,0:T(8,128)(2,1)S(1)} %collective-permute-done.2) | copy-start | bytes 6291460
  59.7 12.5 %all-to-all-start.2 = ((bf16[16,2,16,512]{3,2,1,0:T(8,128)(2,1)}), bf16[16,2,16,512]{3,2,1,0:T(8,128)(2,1)S(1)}, u32[]{:S(2)}, u32[]{:S(2)}) async-start(bf16[16,2,16,512]{3,2,1,0:T(8,128)(2,1)} %get-tuple-element.15), calls=%async_computation.2 | async-start | bytes 1048576 | tf_op jit(solution)/shard_map/all_to_all | solution.py:15
  65.3 7.0 %collective-permute-start.5 = (bf16[4,2,16,512]{3,2,1,0:T(8,128)(2,1)S(1)}, bf16[4,2,16,512]{3,2,1,0:T(8,128)(2,1)S(1)}, u32[]{:S(2)}, u32[]{:S(2)}) collective-permute-start(bf16[4,2,16,512]{3,2,1,0:T(8,128)(2,1)S(1)} %reduce_sum.31), channel_id=1, source_target_pairs={{0,1},{1,2},{2,3},{3,4},{4,5},{5,6},{6,7},{7,8},{8,9},{9,10},{10,1... | collective-permute-start | bytes 393224 | tf_op jit(solution)/shard_map/ppermute | solution.py:33
  67.4 12.1 %collective-permute-start.4 = (bf16[4,2,16,512]{3,2,1,0:T(8,128)(2,1)S(1)}, bf16[4,2,16,512]{3,2,1,0:T(8,128)(2,1)S(1)}, u32[]{:S(2)}, u32[]{:S(2)}) collective-permute-start(bf16[4,2,16,512]{3,2,1,0:T(8,128)(2,1)S(1)} %reduce_sum.31), channel_id=1, source_target_pairs={{15,0},{31,16},{47,32},{63,48},{79,64},{95,80},{111,96},{127,112},... | collective-permute-start | bytes 393224 | tf_op jit(solution)/shard_map/ppermute | solution.py:28

commit v7 on v6

--- a/solution.py
+++ b/solution.py
@@ -95,15 +95,21 @@
     cols = lax.broadcasted_iota(jnp.int32, (tall, width), 1)
     row = lax.broadcasted_iota(jnp.int32, (tall, width), 0)
 
-    @pl.loop(0, chips)
-    def _(chip):
-        for s in range(sdev):
-            size = dims_ref[s]
-            for ref, seat in ((near_ref, core), (far_ref, 1 - core)):
-                start = pl.multiple_of((chip * 2 + seat) * tall, tall)
-                kept = (cols < size) & (row + start < size)
-                psi_ref[s, pl.ds(start, tall), :] = jnp.where(kept, ref[chip, s].astype(F32), 0.0).astype(BF16)
-
+    def mask_chip(s, chip):
+        size = dims_ref[s]
+        for ref, seat in ((near_ref, core), (far_ref, 1 - core)):
+            start = pl.multiple_of((chip * 2 + seat) * tall, tall)
+            kept = (cols < size) & (row + start < size)
+            psi_ref[s, pl.ds(start, tall), :] = jnp.where(kept, ref[chip, s].astype(F32), 0.0).astype(BF16)
+
+    @pl.loop(0, chips // 2)
+    def _(pair):
+        mask_chip(0, 2 * pair)
+        mask_chip(0, 2 * pair + 1)
+
+    for s in range(1, sdev):
+        for chip in range(chips):
+            mask_chip(s, chip)
     sum_ref[...] = jnp.zeros_like(sum_ref)
     for whose, s, rows, rights, fetches in steps:
         for fetch in fetches:

time: 92 us -> 92 us (level)
  no operation moved by 1% of the time
where the time goes in v7:
time: 92 us; the launch traced here: 91.3 us
  starting transfers between devices  29.6 us (32%)
  waiting for transfers between devices  25.6 us (28%)
  blocking collectives  23.4 us (25%)
  Pallas kernels  7.12 us (8%)
  local copies, waits for them, and re-layouts  3.58 us (4%)
  other arithmetic  1.82 us (2%)
    all_to_all x2, blocking collectives, exchanged(): return lax.all_to_all(x, axis, split_axis=0, concat_axis=0, tiled=True)  23.4 us
    all_to_all x3, waiting for transfers between devices, exchanged(): return lax.all_to_all(x, axis, split_axis=0, concat_axis=0, tiled=True)  18.3 us
    all_to_all x3, starting transfers between devices, exchanged(): return lax.all_to_all(x, axis, split_axis=0, concat_axis=0, tiled=True)  17.4 us
    ppermute x4, starting transfers between devices, from_partner(): return lax.ppermute(x, 'c', [(0, 1), (1, 0)])  8.77 us
    ppermute x1, waiting for transfers between devices, around(): return lax.ppermute(x, 'sec', [(n - 1, 0)])  7.23 us
    pallas_call x1, Pallas kernels, slot_sums(): pl.pallas_call(sums_kernel, in_specs=[smem] * 4 + [vmem] * 4 + [hbm] * 3,...  5 us
    broadcast_in_dim x2, local copies, waits for them, and re-layouts, shared(): jnp.broadcast_to(x[None], (lax.axis_size(axis),) + x.shape)  2.29 us
    ppermute x1, starting transfers between devices, ahead(): return lax.ppermute(x, 'sec', [(i, i + 1) for i in range(n - 1)])  2.15 us
  transfers between devices with their start and end apart: 9, of which 4 were waited for; matrix products, arithmetic and copies ran while one was open for 4% of the time, Pallas kernels for 2%

profile of v7, /device:TPU:6, one launch (start us, length us, event | category | flops | bytes accessed | tf_op | source)
XLA Modules:
  0.0 91.3 jit_solution(17771761569069019584)
XLA Ops:
  0.0 0.0 copy-start
  0.0 0.0 copy-start.1
  0.0 2.0 %collective-permute-start.2 = (bf16[2,2,512,512]{3,2,1,0:T(8,128)(2,1)}, bf16[2,2,512,512]{3,2,1,0:T(8,128)(2,1)S(1)}, u32[]{:S(2)}, u32[]{:S(2)}) collective-permute-start(bf16[2,2,512,512]{3,2,1,0:T(8,128)(2,1)} %param.6), channel_id=1, source_target_pairs={{0,16},{16,0},{1,17},{17,1},{2,18},{18,2},{3,19},{19,3},{4,20},{20... | collective-permute-start | bytes 6291464 | tf_op jit(solution)/shard_map/ppermute | solution.py:23
  2.1 2.4 %collective-permute-start.3 = (bf16[2,2,512,512]{3,2,1,0:T(8,128)(2,1)}, bf16[2,2,512,512]{3,2,1,0:T(8,128)(2,1)}, u32[]{:S(2)}, u32[]{:S(2)}) collective-permute-start(bf16[2,2,512,512]{3,2,1,0:T(8,128)(2,1)} %right_ref.3), channel_id=1, source_target_pairs={{0,16},{16,0},{1,17},{17,1},{2,18},{18,2},{3,19},{19,3},{4,20},{20... | collective-permute-start | bytes 6291464 | tf_op jit(solution)/shard_map/ppermute | solution.py:23
  4.5 1.4 %broadcast_in_dim.6 = bf16[4,2,16,512]{3,2,1,0:T(8,128)(2,1)} broadcast(bf16[2,16,512]{2,1,0:T(8,128)(2,1)} %param.5), dimensions={1,2,3} | broadcast | bytes 163840 | tf_op jit(solution)/shard_map/broadcast_in_dim | solution.py:19
  5.9 7.1 %all-to-all-start = ((bf16[4,2,16,512]{3,2,1,0:T(8,128)(2,1)}), bf16[4,2,16,512]{3,2,1,0:T(8,128)(2,1)S(1)}, u32[]{:S(2)}, u32[]{:S(2)}) async-start(bf16[4,2,16,512]{3,2,1,0:T(8,128)(2,1)} %broadcast_in_dim.6), calls=%async_computation | async-start | bytes 262144 | tf_op jit(solution)/shard_map/all_to_all | solution.py:15
  13.0 0.7 iota_compare_fusion
  13.7 8.4 %all-to-all-done = bf16[4,2,16,512]{3,2,1,0:T(8,128)(2,1)S(1)} async-done(((bf16[4,2,16,512]{3,2,1,0:T(8,128)(2,1)}), bf16[4,2,16,512]{3,2,1,0:T(8,128)(2,1)S(1)}, u32[]{:S(2)}, u32[]{:S(2)}) %all-to-all-start) | async-done | bytes 131104 | tf_op jit(solution)/shard_map/all_to_all | solution.py:15
  22.1 0.9 broadcast_in_dim.7
  23.0 4.8 %all-to-all-start.1 = ((bf16[4,4,2,16,512]{4,3,2,1,0:T(8,128)(2,1)}), bf16[4,4,2,16,512]{4,3,2,1,0:T(8,128)(2,1)S(1)}, u32[]{:S(2)}, u32[]{:S(2)}) async-start(bf16[4,4,2,16,512]{4,3,2,1,0:T(8,128)(2,1)} %broadcast_in_dim.7), calls=%async_computation.1 | async-start | bytes 1048576 | tf_op jit(solution)/shard_map/all_to_all | solution.py:15
  27.8 0.0 copy-done
  27.8 0.1 broadcast_compare_fusion
  27.9 0.1 broadcast_and_fusion
  28.0 6.5 %all-to-all-done.1 = bf16[4,4,2,16,512]{4,3,2,1,0:T(8,128)(2,1)S(1)} async-done(((bf16[4,4,2,16,512]{4,3,2,1,0:T(8,128)(2,1)}), bf16[4,4,2,16,512]{4,3,2,1,0:T(8,128)(2,1)S(1)}, u32[]{:S(2)}, u32[]{:S(2)}) %all-to-all-start.1) | async-done | bytes 524320 | tf_op jit(solution)/shard_map/all_to_all | solution.py:15
  34.4 1.9 %collective-permute-start.1 = (bf16[16,2,16,512]{3,2,1,0:T(8,128)(2,1)S(1)}, bf16[16,2,16,512]{3,2,1,0:T(8,128)(2,1)S(1)}, u32[]{:S(2)}, u32[]{:S(2)}) collective-permute-start(bf16[16,2,16,512]{3,2,1,0:T(8,128)(2,1)S(1)} %bitcast.9), channel_id=1, source_target_pairs={{0,16},{16,0},{1,17},{17,1},{2,18},{18,2},{3,19},{19,3},{4,20},{20... | collective-permute-start | bytes 1572872 | tf_op jit(solution)/shard_map/ppermute | solution.py:23
  36.3 0.0 copy-done.1
  36.3 2.4 %collective-permute-start = (s32[2,2]{1,0:T(2,128)S(1)}, s32[2,2]{1,0:T(2,128)S(1)}, u32[]{:S(2)}, u32[]{:S(2)}) collective-permute-start(s32[2,2]{1,0:T(2,128)S(1)} %copy-done.1), channel_id=1, source_target_pairs={{0,16},{16,0},{1,17},{17,1},{2,18},{18,2},{3,19},{19,3},{4,20},{20... | collective-permute-start | bytes 56 | tf_op jit(solution)/shard_map/ppermute | solution.py:23
  38.8 0.1 pad_add_fusion.where_ref
  38.8 2.1 %fetch.1 = (bf16[2,2,16,16,512]{4,3,2,1,0:T(8,128)(2,1)S(1)}, bf16[2,512,512]{2,1,0:T(8,128)(2,1)S(1)}) custom-call(s32[3]{0:T(128)S(1)} %pad_add_fusion.where_ref, bf16[2,2,16,2,16,512]{5,4,3,2,1,0:T(8,128)(2,1)} %bitcast.11, bf16[2,2,512,512]{3,2,1,0:T(8,128)(2,1)} %right_ref.3), custom_call_target="tpu_custom_call" | custom-call | tf_op jit(solution)/shard_map/fetch/pallas_call | solution.py:61
  41.0 0.0 collective-permute-done.conn2_ref
  41.0 0.0 collective-permute-done.1.far_ref
  41.0 0.0 collective-permute-done.2
  41.0 0.0 copy-start.2
  41.0 0.0 collective-permute-done.3.right2_ref
  41.0 1.3 %copy-done.2 = bf16[2,2,512,512]{3,2,1,0:T(8,128)(2,1)} copy-done((bf16[2,2,512,512]{3,2,1,0:T(8,128)(2,1)}, bf16[2,2,512,512]{3,2,1,0:T(8,128)(2,1)S(1)}, u32[]{:S(2)}) %copy-start.2) | copy-done | bytes 2097176
  42.3 5.0 %slot_sums.1 = (bf16[16,2,16,512]{3,2,1,0:T(8,128)(2,1)}, bf16[16,2,16,512]{3,2,1,0:T(8,128)(2,1)S(1)}) custom-call(s32[3]{0:T(128)S(1)} %pad_add_fusion.where_ref, s32[2,2]{1,0:T(2,128)S(1)} %copy-done.1, s32[2,2]{1,0:T(2,128)S(1)} %collective-permute-done.conn2_ref, s32[2]{0:T(128)S(1)} %copy-done, bf16[16,2,16,512]{3,2,1,0:T(8,128)(2,1)S(1)} %bitcast.10, ...), custom_call_target="tpu_custom_call" | custom-call | tf_op jit(solution)/shard_map/slot_sums/pallas_call | solution.py:152
  47.3 12.3 %all_to_all.25 = bf16[16,2,16,512]{3,2,1,0:T(8,128)(2,1)S(1)} all-to-all(bf16[16,2,16,512]{3,2,1,0:T(8,128)(2,1)S(1)} %get-tuple-element.16), channel_id=1, replica_groups=mesh['x'=4,'y'=4,'c'=2,'sec'=16] {'x'}, dimensions={0} | all-to-all | bytes 1048576 | tf_op jit(solution)/shard_map/all_to_all | solution.py:15
  59.6 5.5 %all-to-all-start.2 = ((bf16[16,2,16,512]{3,2,1,0:T(8,128)(2,1)}), bf16[16,2,16,512]{3,2,1,0:T(8,128)(2,1)S(1)}, u32[]{:S(2)}, u32[]{:S(2)}) async-start(bf16[16,2,16,512]{3,2,1,0:T(8,128)(2,1)} %get-tuple-element.15), calls=%async_computation.2 | async-start | bytes 1048576 | tf_op jit(solution)/shard_map/all_to_all | solution.py:15
  65.2 0.1 reduce_sum.31
  65.2 2.2 %collective-permute-start.5 = (bf16[4,2,16,512]{3,2,1,0:T(8,128)(2,1)S(1)}, bf16[4,2,16,512]{3,2,1,0:T(8,128)(2,1)S(1)}, u32[]{:S(2)}, u32[]{:S(2)}) collective-permute-start(bf16[4,2,16,512]{3,2,1,0:T(8,128)(2,1)S(1)} %reduce_sum.31), channel_id=1, source_target_pairs={{0,1},{1,2},{2,3},{3,4},{4,5},{5,6},{6,7},{7,8},{8,9},{9,10},{10,1... | collective-permute-start | bytes 393224 | tf_op jit(solution)/shard_map/ppermute | solution.py:33
  67.4 1.3 %collective-permute-start.4 = (bf16[4,2,16,512]{3,2,1,0:T(8,128)(2,1)S(1)}, bf16[4,2,16,512]{3,2,1,0:T(8,128)(2,1)S(1)}, u32[]{:S(2)}, u32[]{:S(2)}) collective-permute-start(bf16[4,2,16,512]{3,2,1,0:T(8,128)(2,1)S(1)} %reduce_sum.31), channel_id=1, source_target_pairs={{15,0},{31,16},{47,32},{63,48},{79,64},{95,80},{111,96},{127,112},... | collective-permute-start | bytes 393224 | tf_op jit(solution)/shard_map/ppermute | solution.py:28
  68.7 3.5 %all-to-all-done.2 = bf16[16,2,16,512]{3,2,1,0:T(8,128)(2,1)S(1)} async-done(((bf16[16,2,16,512]{3,2,1,0:T(8,128)(2,1)}), bf16[16,2,16,512]{3,2,1,0:T(8,128)(2,1)S(1)}, u32[]{:S(2)}, u32[]{:S(2)}) %all-to-all-start.2) | async-done | bytes 524320 | tf_op jit(solution)/shard_map/all_to_all | solution.py:15
  72.2 0.1 convert_reduce_fusion
  72.2 0.0 collective-permute-done.5
  72.3 7.2 %collective-permute-done.4 = bf16[4,2,16,512]{3,2,1,0:T(8,128)(2,1)S(1)} collective-permute-done((bf16[4,2,16,512]{3,2,1,0:T(8,128)(2,1)S(1)}, bf16[4,2,16,512]{3,2,1,0:T(8,128)(2,1)S(1)}, u32[]{:S(2)}, u32[]{:S(2)}) %collective-permute-start.4) | collective-permute-done | bytes 131104 | tf_op jit(solution)/shard_map/ppermute | solution.py:28
  79.5 11.1 %all_to_all.26 = bf16[4,2,16,512]{3,2,1,0:T(8,128)(2,1)S(1)} all-to-all(bf16[4,2,16,512]{3,2,1,0:T(8,128)(2,1)S(1)} %add_convert_fusion), channel_id=1, replica_groups=mesh['x'=4,'y'=4,'c'=2,'sec'=16] {'y'}, dimensions={0} | all-to-all | bytes 262144 | tf_op jit(solution)/shard_map/all_to_all | solution.py:15
  90.7 0.6 select_convert_fusion
  (3 shorter events, 0.1 us)
Async XLA Ops:
  0.0 27.8 %copy-start = (s32[2]{0:T(128)S(1)}, s32[2]{0:T(128)}, u32[]{:S(2)}) copy-start(s32[2]{0:T(128)} %dims_ref.1) | copy-start | bytes 28
  0.0 36.3 %copy-start.1 = (s32[2,2]{1,0:T(2,128)S(1)}, s32[2,2]{1,0:T(2,128)}, u32[]{:S(2)}) copy-start(s32[2,2]{1,0:T(2,128)} %conn_ref.1) | copy-start | bytes 52
  0.0 41.0 %collective-permute-start.2 = (bf16[2,2,512,512]{3,2,1,0:T(8,128)(2,1)}, bf16[2,2,512,512]{3,2,1,0:T(8,128)(2,1)S(1)}, u32[]{:S(2)}, u32[]{:S(2)}) collective-permute-start(bf16[2,2,512,512]{3,2,1,0:T(8,128)(2,1)} %param.6), channel_id=1, source_target_pairs={{0,16},{16,0},{1,17},{17,1},{2,18},{18,2},{3,19},{19,3},{4,20},{20... | collective-permute-start | bytes 6291464 | tf_op jit(solution)/shard_map/ppermute | solution.py:23
  2.1 39.0 %collective-permute-start.3 = (bf16[2,2,512,512]{3,2,1,0:T(8,128)(2,1)}, bf16[2,2,512,512]{3,2,1,0:T(8,128)(2,1)}, u32[]{:S(2)}, u32[]{:S(2)}) collective-permute-start(bf16[2,2,512,512]{3,2,1,0:T(8,128)(2,1)} %right_ref.3), channel_id=1, source_target_pairs={{0,16},{16,0},{1,17},{17,1},{2,18},{18,2},{3,19},{19,3},{4,20},{20... | collective-permute-start | bytes 6291464 | tf_op jit(solution)/shard_map/ppermute | solution.py:23
  5.9 16.2 %all-to-all-start = ((bf16[4,2,16,512]{3,2,1,0:T(8,128)(2,1)}), bf16[4,2,16,512]{3,2,1,0:T(8,128)(2,1)S(1)}, u32[]{:S(2)}, u32[]{:S(2)}) async-start(bf16[4,2,16,512]{3,2,1,0:T(8,128)(2,1)} %broadcast_in_dim.6), calls=%async_computation | async-start | bytes 262144 | tf_op jit(solution)/shard_map/all_to_all | solution.py:15
  23.0 11.4 %all-to-all-start.1 = ((bf16[4,4,2,16,512]{4,3,2,1,0:T(8,128)(2,1)}), bf16[4,4,2,16,512]{4,3,2,1,0:T(8,128)(2,1)S(1)}, u32[]{:S(2)}, u32[]{:S(2)}) async-start(bf16[4,4,2,16,512]{4,3,2,1,0:T(8,128)(2,1)} %broadcast_in_dim.7), calls=%async_computation.1 | async-start | bytes 1048576 | tf_op jit(solution)/shard_map/all_to_all | solution.py:15
  34.4 6.6 %collective-permute-start.1 = (bf16[16,2,16,512]{3,2,1,0:T(8,128)(2,1)S(1)}, bf16[16,2,16,512]{3,2,1,0:T(8,128)(2,1)S(1)}, u32[]{:S(2)}, u32[]{:S(2)}) collective-permute-start(bf16[16,2,16,512]{3,2,1,0:T(8,128)(2,1)S(1)} %bitcast.9), channel_id=1, source_target_pairs={{0,16},{16,0},{1,17},{17,1},{2,18},{18,2},{3,19},{19,3},{4,20},{20... | collective-permute-start | bytes 1572872 | tf_op jit(solution)/shard_map/ppermute | solution.py:23
  36.3 4.6 %collective-permute-start = (s32[2,2]{1,0:T(2,128)S(1)}, s32[2,2]{1,0:T(2,128)S(1)}, u32[]{:S(2)}, u32[]{:S(2)}) collective-permute-start(s32[2,2]{1,0:T(2,128)S(1)} %copy-done.1), channel_id=1, source_target_pairs={{0,16},{16,0},{1,17},{17,1},{2,18},{18,2},{3,19},{19,3},{4,20},{20... | collective-permute-start | bytes 56 | tf_op jit(solution)/shard_map/ppermute | solution.py:23
  41.0 1.3 %copy-start.2 = (bf16[2,2,512,512]{3,2,1,0:T(8,128)(2,1)}, bf16[2,2,512,512]{3,2,1,0:T(8,128)(2,1)S(1)}, u32[]{:S(2)}) copy-start(bf16[2,2,512,512]{3,2,1,0:T(8,128)(2,1)S(1)} %collective-permute-done.2) | copy-start | bytes 6291460
  59.6 12.5 %all-to-all-start.2 = ((bf16[16,2,16,512]{3,2,1,0:T(8,128)(2,1)}), bf16[16,2,16,512]{3,2,1,0:T(8,128)(2,1)S(1)}, u32[]{:S(2)}, u32[]{:S(2)}) async-start(bf16[16,2,16,512]{3,2,1,0:T(8,128)(2,1)} %get-tuple-element.15), calls=%async_computation.2 | async-start | bytes 1048576 | tf_op jit(solution)/shard_map/all_to_all | solution.py:15
  65.2 7.0 %collective-permute-start.5 = (bf16[4,2,16,512]{3,2,1,0:T(8,128)(2,1)S(1)}, bf16[4,2,16,512]{3,2,1,0:T(8,128)(2,1)S(1)}, u32[]{:S(2)}, u32[]{:S(2)}) collective-permute-start(bf16[4,2,16,512]{3,2,1,0:T(8,128)(2,1)S(1)} %reduce_sum.31), channel_id=1, source_target_pairs={{0,1},{1,2},{2,3},{3,4},{4,5},{5,6},{6,7},{7,8},{8,9},{9,10},{10,1... | collective-permute-start | bytes 393224 | tf_op jit(solution)/shard_map/ppermute | solution.py:33
  67.4 12.1 %collective-permute-start.4 = (bf16[4,2,16,512]{3,2,1,0:T(8,128)(2,1)S(1)}, bf16[4,2,16,512]{3,2,1,0:T(8,128)(2,1)S(1)}, u32[]{:S(2)}, u32[]{:S(2)}) collective-permute-start(bf16[4,2,16,512]{3,2,1,0:T(8,128)(2,1)S(1)} %reduce_sum.31), channel_id=1, source_target_pairs={{15,0},{31,16},{47,32},{63,48},{79,64},{95,80},{111,96},{127,112},... | collective-permute-start | bytes 393224 | tf_op jit(solution)/shard_map/ppermute | solution.py:28

commit v8 on v7

--- a/solution.py
+++ b/solution.py
@@ -41,57 +41,26 @@
     return pltpu.with_memory_space_constraint(x, pltpu.HBM)
 
 
-def fetch_kernel(where_ref, left_ref, right_ref, rows_ref, rights_ref, sems):
-    kdev, sdev = right_ref.shape[:2]
-    core = where_ref[1]
-    fetches = []
-    for k in range(kdev):
-        for s in range(sdev):
-            fetches.append(pltpu.make_async_copy(left_ref.at[k, s, :, core], rows_ref.at[s, k], sems.at[s, k]))
-        fetches.append(pltpu.make_async_copy(right_ref.at[k, 0], rights_ref.at[k], sems.at[sdev, k]))
-    for fetch in fetches:
-        fetch.start()
-    for fetch in fetches:
-        fetch.wait()
-
-
-def fetched(where, left, right):
-    kdev, sdev, chips, _, tall, width = left.shape
-    hbm = pl.BlockSpec(memory_space=pltpu.HBM)
-    return pl.pallas_call(
-        fetch_kernel,
-        in_specs=[pl.BlockSpec(memory_space=pltpu.SMEM), hbm, hbm],
-        out_specs=[pl.BlockSpec(memory_space=pltpu.VMEM)] * 2,
-        out_shape=[
-            pltpu.VMEM((sdev, kdev, chips, tall, width), BF16),
-            pltpu.VMEM((kdev, width, width), BF16),
-        ],
-        scratch_shapes=[pltpu.SemaphoreType.DMA((sdev + 1, kdev))],
-        compiler_params=pltpu.CompilerParams(vmem_limit_bytes=2**20),
-        name="fetch",
-    )(where, in_hbm(left), in_hbm(right))
-
-
-def sums_kernel(where_ref, conn_ref, conn2_ref, dims_ref, near_ref, far_ref, rows0_ref, right0_ref, right_ref, left2_ref, right2_ref, own_ref, onward_ref, psi_ref, rows_ref, rights_ref, half_ref, sum_ref, staged_ref, sems, out_sem):
+def sums_kernel(where_ref, conn_ref, conn2_ref, dims_ref, near_ref, far_ref, right_ref, left_ref, left2_ref, right2_ref, own_ref, onward_ref, psi_ref, rows_ref, rights_ref, half_ref, sum_ref, staged_ref, sems, out_sem):
     kdev, sdev, width, _ = right_ref.shape
     chips, _, tall, _ = near_ref.shape
     group = where_ref[0]
     core = where_ref[1]
     many = chips * tall
-    steps = [(0, 0, rows0_ref.at[0], right0_ref, ())]
-    for whose, s in ((0, 1), (1, 0), (1, 1)):
-        n = len(steps) - 1
-        rights = (right_ref, right2_ref)[whose]
+    steps = []
+    for n, (whose, s) in enumerate(((0, 0), (0, 1), (1, 0), (1, 1))):
         fetches = []
-        rows = rows0_ref.at[s]
         for k in range(kdev):
-            if whose == 1:
-                rows = rows_ref.at[s]
-                fetches.append(pltpu.make_async_copy(left2_ref.at[k, s, :, core], rows.at[k], sems.at[0, n, k]))
-            fetches.append(pltpu.make_async_copy(rights.at[k, s], rights_ref.at[n, k], sems.at[1, n, k]))
+            source = (left_ref, left2_ref)[whose].at[k, s, :, core]
+            fetches.append(pltpu.make_async_copy(source, rows_ref.at[n, k], sems.at[n, k]))
+        rights = right_ref.at[:, s]
+        if whose == 1:
+            rights = rights_ref.at[:, s]
+            for k in range(kdev):
+                fetches.append(pltpu.make_async_copy(right2_ref.at[k, s], rights_ref.at[k, s], sems.at[2 * sdev + s, k]))
         for fetch in fetches:
             fetch.start()
-        steps.append((whose, s, rows, rights_ref.at[n], fetches))
+        steps.append((whose, s, rows_ref.at[n], rights, fetches))
     cols = lax.broadcasted_iota(jnp.int32, (tall, width), 1)
     row = lax.broadcasted_iota(jnp.int32, (tall, width), 0)
 
@@ -140,10 +109,9 @@
     leave.wait()
 
 
-def slot_sums(where, conn, conn2, dims, near, far, rows0, right0, right, left2, right2):
+def slot_sums(where, conn, conn2, dims, near, far, right, left, left2, right2):
     kdev, sdev, chips, _, tall, width = left2.shape
     assert sdev == 2
-    rest = 2 * sdev - 1
     block = (chips, sdev, tall, width)
     smem = pl.BlockSpec(memory_space=pltpu.SMEM)
     vmem = pl.BlockSpec(memory_space=pltpu.VMEM)
@@ -151,22 +119,22 @@
     many = chips * tall
     return pl.pallas_call(
         sums_kernel,
-        in_specs=[smem] * 4 + [vmem] * 4 + [hbm] * 3,
+        in_specs=[smem] * 4 + [vmem] * 3 + [hbm] * 3,
         out_specs=[hbm, vmem],
         out_shape=[pltpu.HBM(block, BF16), pltpu.VMEM(block, BF16)],
         scratch_shapes=[
             pltpu.VMEM((sdev, width, width), BF16),
-            pltpu.VMEM((sdev, kdev, chips, tall, width), BF16),
-            pltpu.VMEM((rest, kdev, width, width), BF16),
+            pltpu.VMEM((2 * sdev, kdev, chips, tall, width), BF16),
+            pltpu.VMEM((kdev, sdev, width, width), BF16),
             pltpu.VMEM((kdev * many, width), BF16),
             pltpu.VMEM((2 * sdev, many, width), F32),
             pltpu.VMEM(block, BF16),
-            pltpu.SemaphoreType.DMA((2, rest, kdev)),
+            pltpu.SemaphoreType.DMA((3 * sdev, kdev)),
             pltpu.SemaphoreType.DMA,
         ],
         compiler_params=pltpu.CompilerParams(vmem_limit_bytes=24 * 2**20),
         name="slot_sums",
-    )(where, conn, conn2, dims, *(in_vmem(x) for x in (near, far, rows0, right0)), *(in_hbm(x) for x in (right, left2, right2)))
+    )(where, conn, conn2, dims, *(in_vmem(x) for x in (near, far, right)), *(in_hbm(x) for x in (left, left2, right2)))
 
 
 def kept_entries(dims, row_start, rows, width):
@@ -186,14 +154,12 @@
     left2 = from_partner(left_ops).reshape(by_row)
     right2 = from_partner(right_ops)
     conn2 = from_partner(conn)
-    left = left_ops.reshape(by_row)
-    rows0, right0 = fetched(where, left, right_ops)
     by_y = shared(psi, "y").reshape(ny, sdev, tall, width)
     by_x = shared(by_y, "x").reshape(nx * ny, sdev, tall, width)
     kept = kept_entries(dims, places[2], tall, width)
     by_x, kept = lax.optimization_barrier((by_x, kept))
     other = from_partner(by_x)
-    own, onward = slot_sums(where, conn, conn2, dims, by_x, other, rows0, right0, right_ops, left2, right2)
+    own, onward = slot_sums(where, conn, conn2, dims, by_x, other, right_ops, left_ops.reshape(by_row), left2, right2)
     by_chip = (nx, ny, sdev, tall, width)
     onward = exchanged(onward, "x").reshape(by_chip).astype(F32).sum(axis=0).astype(BF16)
     far = around(onward)

time: 92 us -> 90.1 us (0.979)
  Pallas kernels: 7.12 us -> 5.54 us
  local copies, waits for them, and re-layouts: 3.58 us -> 2.28 us
    pallas_call x2 -> x1, Pallas kernels: 7.12 us -> 5.54 us  [slot_sums(): pl.pallas_call(sums_kernel, in_specs=[smem] * 4 + [vmem] * 3 + [hbm] * 3,...]
    unnamed x6, local copies, waits for them, and re-layouts: 1.29 us -> 0.01 us
  transfers between devices with their start and end apart: 9 -> 9, of which waited for: 4 -> 5; matrix products, arithmetic and copies ran while one was open for 4% -> 4% of each run, Pallas kernels for 2% -> 0%
where the time goes in v8:
time: 90.1 us; the launch traced here: 89.4 us
  starting transfers between devices  29.6 us (33%)
  waiting for transfers between devices  26.3 us (29%)
  blocking collectives  23.8 us (26%)
  Pallas kernels  5.54 us (6%)
  local copies, waits for them, and re-layouts  2.28 us (3%)
  other arithmetic  1.82 us (2%)
    all_to_all x2, blocking collectives, exchanged(): return lax.all_to_all(x, axis, split_axis=0, concat_axis=0, tiled=True)  23.8 us
    all_to_all x3, waiting for transfers between devices, exchanged(): return lax.all_to_all(x, axis, split_axis=0, concat_axis=0, tiled=True)  18.5 us
    all_to_all x3, starting transfers between devices, exchanged(): return lax.all_to_all(x, axis, split_axis=0, concat_axis=0, tiled=True)  17.4 us
    ppermute x4, starting transfers between devices, from_partner(): return lax.ppermute(x, 'c', [(0, 1), (1, 0)])  8.78 us
    ppermute x1, waiting for transfers between devices, around(): return lax.ppermute(x, 'sec', [(n - 1, 0)])  7.06 us
    pallas_call x1, Pallas kernels, slot_sums(): pl.pallas_call(sums_kernel, in_specs=[smem] * 4 + [vmem] * 3 + [hbm] * 3,...  5.54 us
    broadcast_in_dim x2, local copies, waits for them, and re-layouts, shared(): jnp.broadcast_to(x[None], (lax.axis_size(axis),) + x.shape)  2.26 us
    ppermute x1, starting transfers between devices, ahead(): return lax.ppermute(x, 'sec', [(i, i + 1) for i in range(n - 1)])  2.17 us
  transfers between devices with their start and end apart: 9, of which 5 were waited for; matrix products, arithmetic and copies ran while one was open for 4% of the time, Pallas kernels for 0%

profile of v8, /device:TPU:6, one launch (start us, length us, event | category | flops | bytes accessed | tf_op | source)
XLA Modules:
  0.0 89.4 jit_solution(13279612817689995882)
XLA Ops:
  0.0 0.0 copy-start
  0.0 0.0 copy-start.1
  0.0 0.0 copy-start.2
  0.0 2.1 %collective-permute-start.2 = (bf16[2,2,512,512]{3,2,1,0:T(8,128)(2,1)}, bf16[2,2,512,512]{3,2,1,0:T(8,128)(2,1)}, u32[]{:S(2)}, u32[]{:S(2)}) collective-permute-start(bf16[2,2,512,512]{3,2,1,0:T(8,128)(2,1)} %param.6), channel_id=1, source_target_pairs={{0,16},{16,0},{1,17},{17,1},{2,18},{18,2},{3,19},{19,3},{4,20},{20... | collective-permute-start | bytes 6291464 | tf_op jit(solution)/shard_map/ppermute | solution.py:23
  2.1 2.4 %collective-permute-start.3 = (bf16[2,2,512,512]{3,2,1,0:T(8,128)(2,1)}, bf16[2,2,512,512]{3,2,1,0:T(8,128)(2,1)}, u32[]{:S(2)}, u32[]{:S(2)}) collective-permute-start(bf16[2,2,512,512]{3,2,1,0:T(8,128)(2,1)} %right_ref.1), channel_id=1, source_target_pairs={{0,16},{16,0},{1,17},{17,1},{2,18},{18,2},{3,19},{19,3},{4,20},{20... | collective-permute-start | bytes 6291464 | tf_op jit(solution)/shard_map/ppermute | solution.py:23
  4.5 1.4 %broadcast_in_dim.6 = bf16[4,2,16,512]{3,2,1,0:T(8,128)(2,1)} broadcast(bf16[2,16,512]{2,1,0:T(8,128)(2,1)} %param.5), dimensions={1,2,3} | broadcast | bytes 163840 | tf_op jit(solution)/shard_map/broadcast_in_dim | solution.py:19
  5.9 7.1 %all-to-all-start = ((bf16[4,2,16,512]{3,2,1,0:T(8,128)(2,1)}), bf16[4,2,16,512]{3,2,1,0:T(8,128)(2,1)S(1)}, u32[]{:S(2)}, u32[]{:S(2)}) async-start(bf16[4,2,16,512]{3,2,1,0:T(8,128)(2,1)} %broadcast_in_dim.6), calls=%async_computation | async-start | bytes 262144 | tf_op jit(solution)/shard_map/all_to_all | solution.py:15
  13.0 0.7 iota_compare_fusion
  13.7 8.4 %all-to-all-done = bf16[4,2,16,512]{3,2,1,0:T(8,128)(2,1)S(1)} async-done(((bf16[4,2,16,512]{3,2,1,0:T(8,128)(2,1)}), bf16[4,2,16,512]{3,2,1,0:T(8,128)(2,1)S(1)}, u32[]{:S(2)}, u32[]{:S(2)}) %all-to-all-start) | async-done | bytes 131104 | tf_op jit(solution)/shard_map/all_to_all | solution.py:15
  22.1 0.9 broadcast_in_dim.7
  23.0 4.8 %all-to-all-start.1 = ((bf16[4,4,2,16,512]{4,3,2,1,0:T(8,128)(2,1)}), bf16[4,4,2,16,512]{4,3,2,1,0:T(8,128)(2,1)S(1)}, u32[]{:S(2)}, u32[]{:S(2)}) async-start(bf16[4,4,2,16,512]{4,3,2,1,0:T(8,128)(2,1)} %broadcast_in_dim.7), calls=%async_computation.1 | async-start | bytes 1048576 | tf_op jit(solution)/shard_map/all_to_all | solution.py:15
  27.8 0.0 copy-done.1
  27.8 0.1 broadcast_compare_fusion
  27.9 0.1 broadcast_and_fusion
  27.9 6.5 %all-to-all-done.1 = bf16[4,4,2,16,512]{4,3,2,1,0:T(8,128)(2,1)S(1)} async-done(((bf16[4,4,2,16,512]{4,3,2,1,0:T(8,128)(2,1)}), bf16[4,4,2,16,512]{4,3,2,1,0:T(8,128)(2,1)S(1)}, u32[]{:S(2)}, u32[]{:S(2)}) %all-to-all-start.1) | async-done | bytes 524320 | tf_op jit(solution)/shard_map/all_to_all | solution.py:15
  34.4 1.9 %collective-permute-start.1 = (bf16[16,2,16,512]{3,2,1,0:T(8,128)(2,1)S(1)}, bf16[16,2,16,512]{3,2,1,0:T(8,128)(2,1)S(1)}, u32[]{:S(2)}, u32[]{:S(2)}) collective-permute-start(bf16[16,2,16,512]{3,2,1,0:T(8,128)(2,1)S(1)} %bitcast.9), channel_id=1, source_target_pairs={{0,16},{16,0},{1,17},{17,1},{2,18},{18,2},{3,19},{19,3},{4,20},{20... | collective-permute-start | bytes 1572872 | tf_op jit(solution)/shard_map/ppermute | solution.py:23
  36.3 0.0 copy-done.2
  36.3 2.4 %collective-permute-start = (s32[2,2]{1,0:T(2,128)S(1)}, s32[2,2]{1,0:T(2,128)S(1)}, u32[]{:S(2)}, u32[]{:S(2)}) collective-permute-start(s32[2,2]{1,0:T(2,128)S(1)} %copy-done.2), channel_id=1, source_target_pairs={{0,16},{16,0},{1,17},{17,1},{2,18},{18,2},{3,19},{19,3},{4,20},{20... | collective-permute-start | bytes 56 | tf_op jit(solution)/shard_map/ppermute | solution.py:23
  38.7 0.1 pad_add_fusion.where_ref
  38.8 0.7 collective-permute-done.conn2_ref
  39.5 0.0 collective-permute-done.1.far_ref
  39.5 0.0 collective-permute-done.2
  39.5 0.0 collective-permute-done.3.right2_ref
  39.5 0.0 copy-done
  39.6 5.5 %slot_sums.1 = (bf16[16,2,16,512]{3,2,1,0:T(8,128)(2,1)}, bf16[16,2,16,512]{3,2,1,0:T(8,128)(2,1)S(1)}) custom-call(s32[3]{0:T(128)S(1)} %pad_add_fusion.where_ref, s32[2,2]{1,0:T(2,128)S(1)} %copy-done.2, s32[2,2]{1,0:T(2,128)S(1)} %collective-permute-done.conn2_ref, s32[2]{0:T(128)S(1)} %copy-done.1, bf16[16,2,16,512]{3,2,1,0:T(8,128)(2,1)S(1)} %bitcast.10, ...), custom_call_target="tpu_custom_call" | custom-call | tf_op jit(solution)/shard_map/slot_sums/pallas_call | solution.py:120
  45.1 12.7 %all_to_all.25 = bf16[16,2,16,512]{3,2,1,0:T(8,128)(2,1)S(1)} all-to-all(bf16[16,2,16,512]{3,2,1,0:T(8,128)(2,1)S(1)} %get-tuple-element.12), channel_id=1, replica_groups=mesh['x'=4,'y'=4,'c'=2,'sec'=16] {'x'}, dimensions={0} | all-to-all | bytes 1048576 | tf_op jit(solution)/shard_map/all_to_all | solution.py:15
  57.8 5.5 %all-to-all-start.2 = ((bf16[16,2,16,512]{3,2,1,0:T(8,128)(2,1)}), bf16[16,2,16,512]{3,2,1,0:T(8,128)(2,1)S(1)}, u32[]{:S(2)}, u32[]{:S(2)}) async-start(bf16[16,2,16,512]{3,2,1,0:T(8,128)(2,1)} %get-tuple-element.11), calls=%async_computation.2 | async-start | bytes 1048576 | tf_op jit(solution)/shard_map/all_to_all | solution.py:15
  63.3 0.1 reduce_sum.31
  63.4 2.2 %collective-permute-start.5 = (bf16[4,2,16,512]{3,2,1,0:T(8,128)(2,1)S(1)}, bf16[4,2,16,512]{3,2,1,0:T(8,128)(2,1)S(1)}, u32[]{:S(2)}, u32[]{:S(2)}) collective-permute-start(bf16[4,2,16,512]{3,2,1,0:T(8,128)(2,1)S(1)} %reduce_sum.31), channel_id=1, source_target_pairs={{0,1},{1,2},{2,3},{3,4},{4,5},{5,6},{6,7},{7,8},{8,9},{9,10},{10,1... | collective-permute-start | bytes 393224 | tf_op jit(solution)/shard_map/ppermute | solution.py:33
  65.5 1.3 %collective-permute-start.4 = (bf16[4,2,16,512]{3,2,1,0:T(8,128)(2,1)S(1)}, bf16[4,2,16,512]{3,2,1,0:T(8,128)(2,1)S(1)}, u32[]{:S(2)}, u32[]{:S(2)}) collective-permute-start(bf16[4,2,16,512]{3,2,1,0:T(8,128)(2,1)S(1)} %reduce_sum.31), channel_id=1, source_target_pairs={{15,0},{31,16},{47,32},{63,48},{79,64},{95,80},{111,96},{127,112},... | collective-permute-start | bytes 393224 | tf_op jit(solution)/shard_map/ppermute | solution.py:28
  66.8 3.6 %all-to-all-done.2 = bf16[16,2,16,512]{3,2,1,0:T(8,128)(2,1)S(1)} async-done(((bf16[16,2,16,512]{3,2,1,0:T(8,128)(2,1)}), bf16[16,2,16,512]{3,2,1,0:T(8,128)(2,1)S(1)}, u32[]{:S(2)}, u32[]{:S(2)}) %all-to-all-start.2) | async-done | bytes 524320 | tf_op jit(solution)/shard_map/all_to_all | solution.py:15
  70.5 0.1 convert_reduce_fusion
  70.5 0.0 collective-permute-done.5
  70.6 7.1 %collective-permute-done.4 = bf16[4,2,16,512]{3,2,1,0:T(8,128)(2,1)S(1)} collective-permute-done((bf16[4,2,16,512]{3,2,1,0:T(8,128)(2,1)S(1)}, bf16[4,2,16,512]{3,2,1,0:T(8,128)(2,1)S(1)}, u32[]{:S(2)}, u32[]{:S(2)}) %collective-permute-start.4) | collective-permute-done | bytes 131104 | tf_op jit(solution)/shard_map/ppermute | solution.py:28
  77.7 11.1 %all_to_all.26 = bf16[4,2,16,512]{3,2,1,0:T(8,128)(2,1)S(1)} all-to-all(bf16[4,2,16,512]{3,2,1,0:T(8,128)(2,1)S(1)} %add_convert_fusion), channel_id=1, replica_groups=mesh['x'=4,'y'=4,'c'=2,'sec'=16] {'y'}, dimensions={0} | all-to-all | bytes 262144 | tf_op jit(solution)/shard_map/all_to_all | solution.py:15
  88.8 0.6 select_convert_fusion
  (3 shorter events, 0.1 us)
Async XLA Ops:
  0.0 39.5 %copy-start = (bf16[2,2,512,512]{3,2,1,0:T(8,128)(2,1)S(1)}, bf16[2,2,512,512]{3,2,1,0:T(8,128)(2,1)}, u32[]{:S(2)}) copy-start(bf16[2,2,512,512]{3,2,1,0:T(8,128)(2,1)} %right_ref.1) | copy-start | bytes 6291460
  0.0 27.8 %copy-start.1 = (s32[2]{0:T(128)S(1)}, s32[2]{0:T(128)}, u32[]{:S(2)}) copy-start(s32[2]{0:T(128)} %dims_ref.1) | copy-start | bytes 28
  0.0 36.3 %copy-start.2 = (s32[2,2]{1,0:T(2,128)S(1)}, s32[2,2]{1,0:T(2,128)}, u32[]{:S(2)}) copy-start(s32[2,2]{1,0:T(2,128)} %conn_ref.1) | copy-start | bytes 52
  0.0 39.5 %collective-permute-start.2 = (bf16[2,2,512,512]{3,2,1,0:T(8,128)(2,1)}, bf16[2,2,512,512]{3,2,1,0:T(8,128)(2,1)}, u32[]{:S(2)}, u32[]{:S(2)}) collective-permute-start(bf16[2,2,512,512]{3,2,1,0:T(8,128)(2,1)} %param.6), channel_id=1, source_target_pairs={{0,16},{16,0},{1,17},{17,1},{2,18},{18,2},{3,19},{19,3},{4,20},{20... | collective-permute-start | bytes 6291464 | tf_op jit(solution)/shard_map/ppermute | solution.py:23
  2.1 37.5 %collective-permute-start.3 = (bf16[2,2,512,512]{3,2,1,0:T(8,128)(2,1)}, bf16[2,2,512,512]{3,2,1,0:T(8,128)(2,1)}, u32[]{:S(2)}, u32[]{:S(2)}) collective-permute-start(bf16[2,2,512,512]{3,2,1,0:T(8,128)(2,1)} %right_ref.1), channel_id=1, source_target_pairs={{0,16},{16,0},{1,17},{17,1},{2,18},{18,2},{3,19},{19,3},{4,20},{20... | collective-permute-start | bytes 6291464 | tf_op jit(solution)/shard_map/ppermute | solution.py:23
  5.9 16.2 %all-to-all-start = ((bf16[4,2,16,512]{3,2,1,0:T(8,128)(2,1)}), bf16[4,2,16,512]{3,2,1,0:T(8,128)(2,1)S(1)}, u32[]{:S(2)}, u32[]{:S(2)}) async-start(bf16[4,2,16,512]{3,2,1,0:T(8,128)(2,1)} %broadcast_in_dim.6), calls=%async_computation | async-start | bytes 262144 | tf_op jit(solution)/shard_map/all_to_all | solution.py:15
  23.0 11.4 %all-to-all-start.1 = ((bf16[4,4,2,16,512]{4,3,2,1,0:T(8,128)(2,1)}), bf16[4,4,2,16,512]{4,3,2,1,0:T(8,128)(2,1)S(1)}, u32[]{:S(2)}, u32[]{:S(2)}) async-start(bf16[4,4,2,16,512]{4,3,2,1,0:T(8,128)(2,1)} %broadcast_in_dim.7), calls=%async_computation.1 | async-start | bytes 1048576 | tf_op jit(solution)/shard_map/all_to_all | solution.py:15
  34.4 5.1 %collective-permute-start.1 = (bf16[16,2,16,512]{3,2,1,0:T(8,128)(2,1)S(1)}, bf16[16,2,16,512]{3,2,1,0:T(8,128)(2,1)S(1)}, u32[]{:S(2)}, u32[]{:S(2)}) collective-permute-start(bf16[16,2,16,512]{3,2,1,0:T(8,128)(2,1)S(1)} %bitcast.9), channel_id=1, source_target_pairs={{0,16},{16,0},{1,17},{17,1},{2,18},{18,2},{3,19},{19,3},{4,20},{20... | collective-permute-start | bytes 1572872 | tf_op jit(solution)/shard_map/ppermute | solution.py:23
  36.3 3.2 %collective-permute-start = (s32[2,2]{1,0:T(2,128)S(1)}, s32[2,2]{1,0:T(2,128)S(1)}, u32[]{:S(2)}, u32[]{:S(2)}) collective-permute-start(s32[2,2]{1,0:T(2,128)S(1)} %copy-done.2), channel_id=1, source_target_pairs={{0,16},{16,0},{1,17},{17,1},{2,18},{18,2},{3,19},{19,3},{4,20},{20... | collective-permute-start | bytes 56 | tf_op jit(solution)/shard_map/ppermute | solution.py:23
  57.8 12.7 %all-to-all-start.2 = ((bf16[16,2,16,512]{3,2,1,0:T(8,128)(2,1)}), bf16[16,2,16,512]{3,2,1,0:T(8,128)(2,1)S(1)}, u32[]{:S(2)}, u32[]{:S(2)}) async-start(bf16[16,2,16,512]{3,2,1,0:T(8,128)(2,1)} %get-tuple-element.11), calls=%async_computation.2 | async-start | bytes 1048576 | tf_op jit(solution)/shard_map/all_to_all | solution.py:15
  63.4 7.2 %collective-permute-start.5 = (bf16[4,2,16,512]{3,2,1,0:T(8,128)(2,1)S(1)}, bf16[4,2,16,512]{3,2,1,0:T(8,128)(2,1)S(1)}, u32[]{:S(2)}, u32[]{:S(2)}) collective-permute-start(bf16[4,2,16,512]{3,2,1,0:T(8,128)(2,1)S(1)} %reduce_sum.31), channel_id=1, source_target_pairs={{0,1},{1,2},{2,3},{3,4},{4,5},{5,6},{6,7},{7,8},{8,9},{9,10},{10,1... | collective-permute-start | bytes 393224 | tf_op jit(solution)/shard_map/ppermute | solution.py:33
  65.5 12.1 %collective-permute-start.4 = (bf16[4,2,16,512]{3,2,1,0:T(8,128)(2,1)S(1)}, bf16[4,2,16,512]{3,2,1,0:T(8,128)(2,1)S(1)}, u32[]{:S(2)}, u32[]{:S(2)}) collective-permute-start(bf16[4,2,16,512]{3,2,1,0:T(8,128)(2,1)S(1)} %reduce_sum.31), channel_id=1, source_target_pairs={{15,0},{31,16},{47,32},{63,48},{79,64},{95,80},{111,96},{127,112},... | collective-permute-start | bytes 393224 | tf_op jit(solution)/shard_map/ppermute | solution.py:28

commit v9 on v8

--- a/solution.py
+++ b/solution.py
@@ -41,59 +41,68 @@
     return pltpu.with_memory_space_constraint(x, pltpu.HBM)
 
 
-def sums_kernel(where_ref, conn_ref, conn2_ref, dims_ref, near_ref, far_ref, right_ref, left_ref, left2_ref, right2_ref, own_ref, onward_ref, psi_ref, rows_ref, rights_ref, half_ref, sum_ref, staged_ref, sems, out_sem):
+def sums_kernel(where_ref, conn_ref, conn2_ref, dims_ref, near_ref, far_ref, left_ref, right_ref, left2_ref, right2_ref, own_ref, onward_ref, psi_ref, rows_ref, rights_ref, half_ref, sum_ref, staged_ref, sems, out_sem):
     kdev, sdev, width, _ = right_ref.shape
     chips, _, tall, _ = near_ref.shape
     group = where_ref[0]
     core = where_ref[1]
     many = chips * tall
-    steps = []
-    for n, (whose, s) in enumerate(((0, 0), (0, 1), (1, 0), (1, 1))):
-        fetches = []
-        for k in range(kdev):
-            source = (left_ref, left2_ref)[whose].at[k, s, :, core]
-            fetches.append(pltpu.make_async_copy(source, rows_ref.at[n, k], sems.at[n, k]))
-        rights = right_ref.at[:, s]
-        if whose == 1:
-            rights = rights_ref.at[:, s]
+    fetches = {}
+    for whose in range(2):
+        for s in range(sdev):
+            copies = []
             for k in range(kdev):
-                fetches.append(pltpu.make_async_copy(right2_ref.at[k, s], rights_ref.at[k, s], sems.at[2 * sdev + s, k]))
-        for fetch in fetches:
-            fetch.start()
-        steps.append((whose, s, rows_ref.at[n], rights, fetches))
+                n = (whose * sdev + s) * kdev + k
+                if whose == 1:
+                    rows = rows_ref.at[whose, s, k]
+                    copies.append(pltpu.make_async_copy(left2_ref.at[k, s, :, core], rows, sems.at[0, n]))
+                right = (right_ref, right2_ref)[whose].at[k, s]
+                copies.append(pltpu.make_async_copy(right, rights_ref.at[whose, s, k], sems.at[1, n]))
+            for fetch in copies:
+                fetch.start()
+            fetches[whose, s] = copies
     cols = lax.broadcasted_iota(jnp.int32, (tall, width), 1)
     row = lax.broadcasted_iota(jnp.int32, (tall, width), 0)
 
-    def mask_chip(s, chip):
-        size = dims_ref[s]
-        for ref, seat in ((near_ref, core), (far_ref, 1 - core)):
-            start = pl.multiple_of((chip * 2 + seat) * tall, tall)
-            kept = (cols < size) & (row + start < size)
-            psi_ref[s, pl.ds(start, tall), :] = jnp.where(kept, ref[chip, s].astype(F32), 0.0).astype(BF16)
+    @pl.loop(0, chips)
+    def _(chip):
+        for s in range(sdev):
+            size = dims_ref[s]
+            for ref, seat in ((near_ref, core), (far_ref, 1 - core)):
+                start = pl.multiple_of((chip * 2 + seat) * tall, tall)
+                kept = (cols < size) & (row + start < size)
+                psi_ref[s, pl.ds(start, tall), :] = jnp.where(kept, ref[chip, s].astype(F32), 0.0).astype(BF16)
+            for k in range(kdev):
+                rows_ref[0, s, k, chip] = left_ref[k, s, chip, core]
 
-    @pl.loop(0, chips // 2)
-    def _(pair):
-        mask_chip(0, 2 * pair)
-        mask_chip(0, 2 * pair + 1)
+    sum_ref[...] = jnp.zeros_like(sum_ref)
 
-    for s in range(1, sdev):
-        for chip in range(chips):
-            mask_chip(s, chip)
-    sum_ref[...] = jnp.zeros_like(sum_ref)
-    for whose, s, rows, rights, fetches in steps:
-        for fetch in fetches:
-            fetch.wait()
-        left = rows[...].reshape(kdev * many, width)
-        half_ref[...] = jnp.dot(left, psi_ref[s], preferred_element_type=F32).astype(BF16)
+    def first_product(whose, s):
+        left = rows_ref[whose, s].reshape(kdev * many, width)
+        half_ref[s] = jnp.dot(left, psi_ref[s], preferred_element_type=F32).astype(BF16)
+
+    def second_product(whose, s):
         for k in range(kdev):
             target = (conn_ref, conn2_ref)[whose][k, s]
             place = target % sdev + jnp.where(target // sdev != group, sdev, 0)
             sum_ref[place] += lax.dot_general(
-                half_ref[k * many : (k + 1) * many, :],
-                rights[k],
+                half_ref[s, k * many : (k + 1) * many, :],
+                rights_ref[whose, s, k],
                 (((1,), (1,)), ((), ())),
                 preferred_element_type=F32,
             )
+
+    for s in range(sdev):
+        first_product(0, s)
+    for s in range(sdev):
+        for fetch in fetches[0, s]:
+            fetch.wait()
+        second_product(0, s)
+    for s in range(sdev):
+        for fetch in fetches[1, s]:
+            fetch.wait()
+        first_product(1, s)
+        second_product(1, s)
     for chip in range(chips):
         for t in range(sdev):
             staged_ref[chip, t] = sum_ref[t, chip * tall : (chip + 1) * tall, :].astype(BF16)
@@ -109,7 +118,7 @@
     leave.wait()
 
 
-def slot_sums(where, conn, conn2, dims, near, far, right, left, left2, right2):
+def slot_sums(where, conn, conn2, dims, near, far, left, right, left2, right2):
     kdev, sdev, chips, _, tall, width = left2.shape
     assert sdev == 2
     block = (chips, sdev, tall, width)
@@ -124,17 +133,17 @@
         out_shape=[pltpu.HBM(block, BF16), pltpu.VMEM(block, BF16)],
         scratch_shapes=[
             pltpu.VMEM((sdev, width, width), BF16),
-            pltpu.VMEM((2 * sdev, kdev, chips, tall, width), BF16),
-            pltpu.VMEM((kdev, sdev, width, width), BF16),
-            pltpu.VMEM((kdev * many, width), BF16),
+            pltpu.VMEM((2, sdev, kdev, chips, tall, width), BF16),
+            pltpu.VMEM((2, sdev, kdev, width, width), BF16),
+            pltpu.VMEM((sdev, kdev * many, width), BF16),
             pltpu.VMEM((2 * sdev, many, width), F32),
             pltpu.VMEM(block, BF16),
-            pltpu.SemaphoreType.DMA((3 * sdev, kdev)),
+            pltpu.SemaphoreType.DMA((2, 2 * sdev * kdev)),
             pltpu.SemaphoreType.DMA,
         ],
         compiler_params=pltpu.CompilerParams(vmem_limit_bytes=24 * 2**20),
         name="slot_sums",
-    )(where, conn, conn2, dims, *(in_vmem(x) for x in (near, far, right)), *(in_hbm(x) for x in (left, left2, right2)))
+    )(where, conn, conn2, dims, *(in_vmem(x) for x in (near, far, left)), *(in_hbm(x) for x in (right, left2, right2)))
 
 
 def kept_entries(dims, row_start, rows, width):
@@ -159,7 +168,7 @@
     kept = kept_entries(dims, places[2], tall, width)
     by_x, kept = lax.optimization_barrier((by_x, kept))
     other = from_partner(by_x)
-    own, onward = slot_sums(where, conn, conn2, dims, by_x, other, right_ops, left_ops.reshape(by_row), left2, right2)
+    own, onward = slot_sums(where, conn, conn2, dims, by_x, other, left_ops.reshape(by_row), right_ops, left2, right2)
     by_chip = (nx, ny, sdev, tall, width)
     onward = exchanged(onward, "x").reshape(by_chip).astype(F32).sum(axis=0).astype(BF16)
     far = around(onward)

time: 90.1 us -> 89.9 us (level)
  no operation moved by 1% of the time
where the time goes in v9:
time: 89.9 us; the launch traced here: 89.2 us
  starting transfers between devices  29.6 us (33%)
  waiting for transfers between devices  26.3 us (29%)
  blocking collectives  23.8 us (26%)
  Pallas kernels  5.31 us (6%)
  local copies, waits for them, and re-layouts  2.28 us (3%)
  other arithmetic  1.82 us (2%)
    all_to_all x2, blocking collectives, exchanged(): return lax.all_to_all(x, axis, split_axis=0, concat_axis=0, tiled=True)  23.8 us
    all_to_all x3, waiting for transfers between devices, exchanged(): return lax.all_to_all(x, axis, split_axis=0, concat_axis=0, tiled=True)  18.5 us
    all_to_all x3, starting transfers between devices, exchanged(): return lax.all_to_all(x, axis, split_axis=0, concat_axis=0, tiled=True)  17.4 us
    ppermute x4, starting transfers between devices, from_partner(): return lax.ppermute(x, 'c', [(0, 1), (1, 0)])  8.78 us
    ppermute x1, waiting for transfers between devices, around(): return lax.ppermute(x, 'sec', [(n - 1, 0)])  7.06 us
    pallas_call x1, Pallas kernels, slot_sums(): pl.pallas_call(sums_kernel, in_specs=[smem] * 4 + [vmem] * 3 + [hbm] * 3,...  5.31 us
    broadcast_in_dim x2, local copies, waits for them, and re-layouts, shared(): jnp.broadcast_to(x[None], (lax.axis_size(axis),) + x.shape)  2.26 us
    ppermute x1, starting transfers between devices, ahead(): return lax.ppermute(x, 'sec', [(i, i + 1) for i in range(n - 1)])  2.16 us
  transfers between devices with their start and end apart: 9, of which 5 were waited for; matrix products, arithmetic and copies ran while one was open for 4% of the time, Pallas kernels for 0%

profile of v9, /device:TPU:6, one launch (start us, length us, event | category | flops | bytes accessed | tf_op | source)
XLA Modules:
  0.0 89.2 jit_solution(8780104492114560927)
XLA Ops:
  0.0 0.0 copy-start
  0.0 0.0 copy-start.1
  0.0 0.0 copy-start.2
  0.0 2.1 %collective-permute-start.2 = (bf16[2,2,512,512]{3,2,1,0:T(8,128)(2,1)}, bf16[2,2,512,512]{3,2,1,0:T(8,128)(2,1)}, u32[]{:S(2)}, u32[]{:S(2)}) collective-permute-start(bf16[2,2,512,512]{3,2,1,0:T(8,128)(2,1)} %param.6), channel_id=1, source_target_pairs={{0,16},{16,0},{1,17},{17,1},{2,18},{18,2},{3,19},{19,3},{4,20},{20... | collective-permute-start | bytes 6291464 | tf_op jit(solution)/shard_map/ppermute | solution.py:23
  2.1 2.4 %collective-permute-start.3 = (bf16[2,2,512,512]{3,2,1,0:T(8,128)(2,1)}, bf16[2,2,512,512]{3,2,1,0:T(8,128)(2,1)}, u32[]{:S(2)}, u32[]{:S(2)}) collective-permute-start(bf16[2,2,512,512]{3,2,1,0:T(8,128)(2,1)} %right_ref.1), channel_id=1, source_target_pairs={{0,16},{16,0},{1,17},{17,1},{2,18},{18,2},{3,19},{19,3},{4,20},{20... | collective-permute-start | bytes 6291464 | tf_op jit(solution)/shard_map/ppermute | solution.py:23
  4.5 1.4 %broadcast_in_dim.6 = bf16[4,2,16,512]{3,2,1,0:T(8,128)(2,1)} broadcast(bf16[2,16,512]{2,1,0:T(8,128)(2,1)} %param.5), dimensions={1,2,3} | broadcast | bytes 163840 | tf_op jit(solution)/shard_map/broadcast_in_dim | solution.py:19
  5.9 7.1 %all-to-all-start = ((bf16[4,2,16,512]{3,2,1,0:T(8,128)(2,1)}), bf16[4,2,16,512]{3,2,1,0:T(8,128)(2,1)S(1)}, u32[]{:S(2)}, u32[]{:S(2)}) async-start(bf16[4,2,16,512]{3,2,1,0:T(8,128)(2,1)} %broadcast_in_dim.6), calls=%async_computation | async-start | bytes 262144 | tf_op jit(solution)/shard_map/all_to_all | solution.py:15
  13.0 0.7 iota_compare_fusion
  13.7 8.4 %all-to-all-done = bf16[4,2,16,512]{3,2,1,0:T(8,128)(2,1)S(1)} async-done(((bf16[4,2,16,512]{3,2,1,0:T(8,128)(2,1)}), bf16[4,2,16,512]{3,2,1,0:T(8,128)(2,1)S(1)}, u32[]{:S(2)}, u32[]{:S(2)}) %all-to-all-start) | async-done | bytes 131104 | tf_op jit(solution)/shard_map/all_to_all | solution.py:15
  22.1 0.9 broadcast_in_dim.7
  23.0 4.8 %all-to-all-start.1 = ((bf16[4,4,2,16,512]{4,3,2,1,0:T(8,128)(2,1)}), bf16[4,4,2,16,512]{4,3,2,1,0:T(8,128)(2,1)S(1)}, u32[]{:S(2)}, u32[]{:S(2)}) async-start(bf16[4,4,2,16,512]{4,3,2,1,0:T(8,128)(2,1)} %broadcast_in_dim.7), calls=%async_computation.1 | async-start | bytes 1048576 | tf_op jit(solution)/shard_map/all_to_all | solution.py:15
  27.8 0.0 copy-done.1
  27.8 0.1 broadcast_compare_fusion
  27.9 0.1 broadcast_and_fusion
  27.9 6.5 %all-to-all-done.1 = bf16[4,4,2,16,512]{4,3,2,1,0:T(8,128)(2,1)S(1)} async-done(((bf16[4,4,2,16,512]{4,3,2,1,0:T(8,128)(2,1)}), bf16[4,4,2,16,512]{4,3,2,1,0:T(8,128)(2,1)S(1)}, u32[]{:S(2)}, u32[]{:S(2)}) %all-to-all-start.1) | async-done | bytes 524320 | tf_op jit(solution)/shard_map/all_to_all | solution.py:15
  34.4 1.9 %collective-permute-start.1 = (bf16[16,2,16,512]{3,2,1,0:T(8,128)(2,1)S(1)}, bf16[16,2,16,512]{3,2,1,0:T(8,128)(2,1)S(1)}, u32[]{:S(2)}, u32[]{:S(2)}) collective-permute-start(bf16[16,2,16,512]{3,2,1,0:T(8,128)(2,1)S(1)} %bitcast.9), channel_id=1, source_target_pairs={{0,16},{16,0},{1,17},{17,1},{2,18},{18,2},{3,19},{19,3},{4,20},{20... | collective-permute-start | bytes 1572872 | tf_op jit(solution)/shard_map/ppermute | solution.py:23
  36.3 0.0 copy-done.2
  36.3 2.4 %collective-permute-start = (s32[2,2]{1,0:T(2,128)S(1)}, s32[2,2]{1,0:T(2,128)S(1)}, u32[]{:S(2)}, u32[]{:S(2)}) collective-permute-start(s32[2,2]{1,0:T(2,128)S(1)} %copy-done.2), channel_id=1, source_target_pairs={{0,16},{16,0},{1,17},{17,1},{2,18},{18,2},{3,19},{19,3},{4,20},{20... | collective-permute-start | bytes 56 | tf_op jit(solution)/shard_map/ppermute | solution.py:23
  38.7 0.1 pad_add_fusion.where_ref
  38.8 0.7 collective-permute-done.conn2_ref
  39.5 0.0 collective-permute-done.1.far_ref
  39.5 0.0 collective-permute-done.2
  39.5 0.0 collective-permute-done.3.right2_ref
  39.5 0.0 copy-done
  39.6 5.3 %slot_sums.1 = (bf16[16,2,16,512]{3,2,1,0:T(8,128)(2,1)}, bf16[16,2,16,512]{3,2,1,0:T(8,128)(2,1)S(1)}) custom-call(s32[3]{0:T(128)S(1)} %pad_add_fusion.where_ref, s32[2,2]{1,0:T(2,128)S(1)} %copy-done.2, s32[2,2]{1,0:T(2,128)S(1)} %collective-permute-done.conn2_ref, s32[2]{0:T(128)S(1)} %copy-done.1, bf16[16,2,16,512]{3,2,1,0:T(8,128)(2,1)S(1)} %bitcast.10, ...), custom_call_target="tpu_custom_call" | custom-call | tf_op jit(solution)/shard_map/slot_sums/pallas_call | solution.py:129
  44.9 12.7 %all_to_all.25 = bf16[16,2,16,512]{3,2,1,0:T(8,128)(2,1)S(1)} all-to-all(bf16[16,2,16,512]{3,2,1,0:T(8,128)(2,1)S(1)} %get-tuple-element.12), channel_id=1, replica_groups=mesh['x'=4,'y'=4,'c'=2,'sec'=16] {'x'}, dimensions={0} | all-to-all | bytes 1048576 | tf_op jit(solution)/shard_map/all_to_all | solution.py:15
  57.5 5.5 %all-to-all-start.2 = ((bf16[16,2,16,512]{3,2,1,0:T(8,128)(2,1)}), bf16[16,2,16,512]{3,2,1,0:T(8,128)(2,1)S(1)}, u32[]{:S(2)}, u32[]{:S(2)}) async-start(bf16[16,2,16,512]{3,2,1,0:T(8,128)(2,1)} %get-tuple-element.11), calls=%async_computation.2 | async-start | bytes 1048576 | tf_op jit(solution)/shard_map/all_to_all | solution.py:15
  63.0 0.1 reduce_sum.31
  63.1 2.2 %collective-permute-start.5 = (bf16[4,2,16,512]{3,2,1,0:T(8,128)(2,1)S(1)}, bf16[4,2,16,512]{3,2,1,0:T(8,128)(2,1)S(1)}, u32[]{:S(2)}, u32[]{:S(2)}) collective-permute-start(bf16[4,2,16,512]{3,2,1,0:T(8,128)(2,1)S(1)} %reduce_sum.31), channel_id=1, source_target_pairs={{0,1},{1,2},{2,3},{3,4},{4,5},{5,6},{6,7},{7,8},{8,9},{9,10},{10,1... | collective-permute-start | bytes 393224 | tf_op jit(solution)/shard_map/ppermute | solution.py:33
  65.3 1.3 %collective-permute-start.4 = (bf16[4,2,16,512]{3,2,1,0:T(8,128)(2,1)S(1)}, bf16[4,2,16,512]{3,2,1,0:T(8,128)(2,1)S(1)}, u32[]{:S(2)}, u32[]{:S(2)}) collective-permute-start(bf16[4,2,16,512]{3,2,1,0:T(8,128)(2,1)S(1)} %reduce_sum.31), channel_id=1, source_target_pairs={{15,0},{31,16},{47,32},{63,48},{79,64},{95,80},{111,96},{127,112},... | collective-permute-start | bytes 393224 | tf_op jit(solution)/shard_map/ppermute | solution.py:28
  66.6 3.6 %all-to-all-done.2 = bf16[16,2,16,512]{3,2,1,0:T(8,128)(2,1)S(1)} async-done(((bf16[16,2,16,512]{3,2,1,0:T(8,128)(2,1)}), bf16[16,2,16,512]{3,2,1,0:T(8,128)(2,1)S(1)}, u32[]{:S(2)}, u32[]{:S(2)}) %all-to-all-start.2) | async-done | bytes 524320 | tf_op jit(solution)/shard_map/all_to_all | solution.py:15
  70.2 0.1 convert_reduce_fusion
  70.3 0.0 collective-permute-done.5
  70.3 7.1 %collective-permute-done.4 = bf16[4,2,16,512]{3,2,1,0:T(8,128)(2,1)S(1)} collective-permute-done((bf16[4,2,16,512]{3,2,1,0:T(8,128)(2,1)S(1)}, bf16[4,2,16,512]{3,2,1,0:T(8,128)(2,1)S(1)}, u32[]{:S(2)}, u32[]{:S(2)}) %collective-permute-start.4) | collective-permute-done | bytes 131104 | tf_op jit(solution)/shard_map/ppermute | solution.py:28
  77.4 11.1 %all_to_all.26 = bf16[4,2,16,512]{3,2,1,0:T(8,128)(2,1)S(1)} all-to-all(bf16[4,2,16,512]{3,2,1,0:T(8,128)(2,1)S(1)} %add_convert_fusion), channel_id=1, replica_groups=mesh['x'=4,'y'=4,'c'=2,'sec'=16] {'y'}, dimensions={0} | all-to-all | bytes 262144 | tf_op jit(solution)/shard_map/all_to_all | solution.py:15
  88.6 0.6 select_convert_fusion
  (3 shorter events, 0.1 us)
Async XLA Ops:
  0.0 39.5 %copy-start = (bf16[2,2,512,512]{3,2,1,0:T(8,128)(2,1)S(1)}, bf16[2,2,512,512]{3,2,1,0:T(8,128)(2,1)}, u32[]{:S(2)}) copy-start(bf16[2,2,512,512]{3,2,1,0:T(8,128)(2,1)} %param.6) | copy-start | bytes 6291460
  0.0 27.8 %copy-start.1 = (s32[2]{0:T(128)S(1)}, s32[2]{0:T(128)}, u32[]{:S(2)}) copy-start(s32[2]{0:T(128)} %dims_ref.1) | copy-start | bytes 28
  0.0 36.3 %copy-start.2 = (s32[2,2]{1,0:T(2,128)S(1)}, s32[2,2]{1,0:T(2,128)}, u32[]{:S(2)}) copy-start(s32[2,2]{1,0:T(2,128)} %conn_ref.1) | copy-start | bytes 52
  0.0 39.5 %collective-permute-start.2 = (bf16[2,2,512,512]{3,2,1,0:T(8,128)(2,1)}, bf16[2,2,512,512]{3,2,1,0:T(8,128)(2,1)}, u32[]{:S(2)}, u32[]{:S(2)}) collective-permute-start(bf16[2,2,512,512]{3,2,1,0:T(8,128)(2,1)} %param.6), channel_id=1, source_target_pairs={{0,16},{16,0},{1,17},{17,1},{2,18},{18,2},{3,19},{19,3},{4,20},{20... | collective-permute-start | bytes 6291464 | tf_op jit(solution)/shard_map/ppermute | solution.py:23
  2.1 37.5 %collective-permute-start.3 = (bf16[2,2,512,512]{3,2,1,0:T(8,128)(2,1)}, bf16[2,2,512,512]{3,2,1,0:T(8,128)(2,1)}, u32[]{:S(2)}, u32[]{:S(2)}) collective-permute-start(bf16[2,2,512,512]{3,2,1,0:T(8,128)(2,1)} %right_ref.1), channel_id=1, source_target_pairs={{0,16},{16,0},{1,17},{17,1},{2,18},{18,2},{3,19},{19,3},{4,20},{20... | collective-permute-start | bytes 6291464 | tf_op jit(solution)/shard_map/ppermute | solution.py:23
  5.9 16.2 %all-to-all-start = ((bf16[4,2,16,512]{3,2,1,0:T(8,128)(2,1)}), bf16[4,2,16,512]{3,2,1,0:T(8,128)(2,1)S(1)}, u32[]{:S(2)}, u32[]{:S(2)}) async-start(bf16[4,2,16,512]{3,2,1,0:T(8,128)(2,1)} %broadcast_in_dim.6), calls=%async_computation | async-start | bytes 262144 | tf_op jit(solution)/shard_map/all_to_all | solution.py:15
  23.0 11.4 %all-to-all-start.1 = ((bf16[4,4,2,16,512]{4,3,2,1,0:T(8,128)(2,1)}), bf16[4,4,2,16,512]{4,3,2,1,0:T(8,128)(2,1)S(1)}, u32[]{:S(2)}, u32[]{:S(2)}) async-start(bf16[4,4,2,16,512]{4,3,2,1,0:T(8,128)(2,1)} %broadcast_in_dim.7), calls=%async_computation.1 | async-start | bytes 1048576 | tf_op jit(solution)/shard_map/all_to_all | solution.py:15
  34.4 5.1 %collective-permute-start.1 = (bf16[16,2,16,512]{3,2,1,0:T(8,128)(2,1)S(1)}, bf16[16,2,16,512]{3,2,1,0:T(8,128)(2,1)S(1)}, u32[]{:S(2)}, u32[]{:S(2)}) collective-permute-start(bf16[16,2,16,512]{3,2,1,0:T(8,128)(2,1)S(1)} %bitcast.9), channel_id=1, source_target_pairs={{0,16},{16,0},{1,17},{17,1},{2,18},{18,2},{3,19},{19,3},{4,20},{20... | collective-permute-start | bytes 1572872 | tf_op jit(solution)/shard_map/ppermute | solution.py:23
  36.3 3.2 %collective-permute-start = (s32[2,2]{1,0:T(2,128)S(1)}, s32[2,2]{1,0:T(2,128)S(1)}, u32[]{:S(2)}, u32[]{:S(2)}) collective-permute-start(s32[2,2]{1,0:T(2,128)S(1)} %copy-done.2), channel_id=1, source_target_pairs={{0,16},{16,0},{1,17},{17,1},{2,18},{18,2},{3,19},{19,3},{4,20},{20... | collective-permute-start | bytes 56 | tf_op jit(solution)/shard_map/ppermute | solution.py:23
  57.5 12.7 %all-to-all-start.2 = ((bf16[16,2,16,512]{3,2,1,0:T(8,128)(2,1)}), bf16[16,2,16,512]{3,2,1,0:T(8,128)(2,1)S(1)}, u32[]{:S(2)}, u32[]{:S(2)}) async-start(bf16[16,2,16,512]{3,2,1,0:T(8,128)(2,1)} %get-tuple-element.11), calls=%async_computation.2 | async-start | bytes 1048576 | tf_op jit(solution)/shard_map/all_to_all | solution.py:15
  63.1 7.2 %collective-permute-start.5 = (bf16[4,2,16,512]{3,2,1,0:T(8,128)(2,1)S(1)}, bf16[4,2,16,512]{3,2,1,0:T(8,128)(2,1)S(1)}, u32[]{:S(2)}, u32[]{:S(2)}) collective-permute-start(bf16[4,2,16,512]{3,2,1,0:T(8,128)(2,1)S(1)} %reduce_sum.31), channel_id=1, source_target_pairs={{0,1},{1,2},{2,3},{3,4},{4,5},{5,6},{6,7},{7,8},{8,9},{9,10},{10,1... | collective-permute-start | bytes 393224 | tf_op jit(solution)/shard_map/ppermute | solution.py:33
  65.3 12.1 %collective-permute-start.4 = (bf16[4,2,16,512]{3,2,1,0:T(8,128)(2,1)S(1)}, bf16[4,2,16,512]{3,2,1,0:T(8,128)(2,1)S(1)}, u32[]{:S(2)}, u32[]{:S(2)}) collective-permute-start(bf16[4,2,16,512]{3,2,1,0:T(8,128)(2,1)S(1)} %reduce_sum.31), channel_id=1, source_target_pairs={{15,0},{31,16},{47,32},{63,48},{79,64},{95,80},{111,96},{127,112},... | collective-permute-start | bytes 393224 | tf_op jit(solution)/shard_map/ppermute | solution.py:28

commit v10 on v7

--- a/solution.py
+++ b/solution.py
@@ -15,8 +15,8 @@
     return lax.all_to_all(x, axis, split_axis=0, concat_axis=0, tiled=True)
 
 
-def shared(x, axis):
-    return exchanged(jnp.broadcast_to(x[None], (lax.axis_size(axis),) + x.shape), axis)
+def shared(x, axes, count):
+    return exchanged(jnp.broadcast_to(x[None], (count,) + x.shape), axes)
 
 
 def from_partner(x):
@@ -188,8 +188,7 @@
     conn2 = from_partner(conn)
     left = left_ops.reshape(by_row)
     rows0, right0 = fetched(where, left, right_ops)
-    by_y = shared(psi, "y").reshape(ny, sdev, tall, width)
-    by_x = shared(by_y, "x").reshape(nx * ny, sdev, tall, width)
+    by_x = shared(psi, ("x", "y"), nx * ny)
     kept = kept_entries(dims, places[2], tall, width)
     by_x, kept = lax.optimization_barrier((by_x, kept))
     other = from_partner(by_x)

time: 92 us -> 89.5 us (0.973)
  starting transfers between devices: 29.6 us -> 26.8 us
    all_to_all x3 -> x2, starting transfers between devices: 17.4 us -> 15.6 us  [exchanged(): return lax.all_to_all(x, axis, split_axis=0, concat_axis=0, tiled=True)]
    all_to_all x3 -> x2, waiting for transfers between devices: 18.3 us -> 19.4 us  [exchanged(): return lax.all_to_all(x, axis, split_axis=0, concat_axis=0, tiled=True)]
    ppermute x1, waiting for transfers between devices: 7.23 us -> 6.14 us  [around(): return lax.ppermute(x, 'sec', [(n - 1, 0)])]
    broadcast_in_dim x2 -> x1, local copies, waits for them, and re-layouts: 2.29 us -> 1.62 us  [shared(): return exchanged(jnp.broadcast_to(x[None], (count,) + x.shape), axes)]
  transfers between devices with their start and end apart: 9 -> 8, of which waited for: 4 -> 3; matrix products, arithmetic and copies ran while one was open for 4% -> 4% of each run, Pallas kernels for 2% -> 2%
where the time goes in v10:
time: 89.5 us; the launch traced here: 88.9 us
  starting transfers between devices  26.8 us (30%)
  waiting for transfers between devices  25.6 us (29%)
  blocking collectives  23.9 us (27%)
  Pallas kernels  7.09 us (8%)
  local copies, waits for them, and re-layouts  2.92 us (3%)
  other arithmetic  2.47 us (3%)
    all_to_all x2, blocking collectives, exchanged(): return lax.all_to_all(x, axis, split_axis=0, concat_axis=0, tiled=True)  23.9 us
    all_to_all x2, waiting for transfers between devices, exchanged(): return lax.all_to_all(x, axis, split_axis=0, concat_axis=0, tiled=True)  19.4 us
    all_to_all x2, starting transfers between devices, exchanged(): return lax.all_to_all(x, axis, split_axis=0, concat_axis=0, tiled=True)  15.6 us
    ppermute x4, starting transfers between devices, from_partner(): return lax.ppermute(x, 'c', [(0, 1), (1, 0)])  8.64 us
    ppermute x1, waiting for transfers between devices, around(): return lax.ppermute(x, 'sec', [(n - 1, 0)])  6.14 us
    pallas_call x1, Pallas kernels, slot_sums(): pl.pallas_call(sums_kernel, in_specs=[smem] * 4 + [vmem] * 4 + [hbm] * 3,...  4.97 us
    pallas_call x1, Pallas kernels, fetched(): pl.pallas_call(fetch_kernel, in_specs=[pl.BlockSpec(memory_space=pltpu.SM...  2.11 us
  transfers between devices with their start and end apart: 8, of which 3 were waited for; matrix products, arithmetic and copies ran while one was open for 4% of the time, Pallas kernels for 2%

profile of v10, /device:TPU:6, one launch (start us, length us, event | category | flops | bytes accessed | tf_op | source)
XLA Modules:
  0.0 88.9 jit_solution(9115770954366400949)
XLA Ops:
  0.0 1.9 %collective-permute-start.2 = (bf16[2,2,512,512]{3,2,1,0:T(8,128)(2,1)}, bf16[2,2,512,512]{3,2,1,0:T(8,128)(2,1)S(1)}, u32[]{:S(2)}, u32[]{:S(2)}) collective-permute-start(bf16[2,2,512,512]{3,2,1,0:T(8,128)(2,1)} %param.6), channel_id=1, source_target_pairs={{0,16},{16,0},{1,17},{17,1},{2,18},{18,2},{3,19},{19,3},{4,20},{20... | collective-permute-start | bytes 6291464 | tf_op jit(solution)/shard_map/ppermute | solution.py:23
  1.9 2.4 %collective-permute-start.3 = (bf16[2,2,512,512]{3,2,1,0:T(8,128)(2,1)}, bf16[2,2,512,512]{3,2,1,0:T(8,128)(2,1)}, u32[]{:S(2)}, u32[]{:S(2)}) collective-permute-start(bf16[2,2,512,512]{3,2,1,0:T(8,128)(2,1)} %right_ref.3), channel_id=1, source_target_pairs={{0,16},{16,0},{1,17},{17,1},{2,18},{18,2},{3,19},{19,3},{4,20},{20... | collective-permute-start | bytes 6291464 | tf_op jit(solution)/shard_map/ppermute | solution.py:23
  4.3 1.6 %broadcast_in_dim.4 = bf16[16,2,16,512]{3,2,1,0:T(8,128)(2,1)} broadcast(bf16[2,16,512]{2,1,0:T(8,128)(2,1)} %param.5), dimensions={1,2,3} | broadcast | bytes 557056 | tf_op jit(solution)/shard_map/broadcast_in_dim | solution.py:19
  6.0 10.1 %all-to-all-start = ((bf16[16,2,16,512]{3,2,1,0:T(8,128)(2,1)}), bf16[16,2,16,512]{3,2,1,0:T(8,128)(2,1)S(1)}, u32[]{:S(2)}, u32[]{:S(2)}) async-start(bf16[16,2,16,512]{3,2,1,0:T(8,128)(2,1)} %broadcast_in_dim.4), calls=%async_computation | async-start | bytes 1048576 | tf_op jit(solution)/shard_map/all_to_all | solution.py:15
  16.0 0.7 broadcast_compare_fusion
  16.8 0.7 iota_compare_fusion
  17.5 0.1 broadcast_and_fusion
  17.6 15.1 %all-to-all-done.near_ref = bf16[16,2,16,512]{3,2,1,0:T(8,128)(2,1)S(1)} async-done(((bf16[16,2,16,512]{3,2,1,0:T(8,128)(2,1)}), bf16[16,2,16,512]{3,2,1,0:T(8,128)(2,1)S(1)}, u32[]{:S(2)}, u32[]{:S(2)}) %all-to-all-start) | async-done | bytes 524320 | tf_op jit(solution)/shard_map/all_to_all | solution.py:15
  32.7 1.9 %collective-permute-start.1 = (bf16[16,2,16,512]{3,2,1,0:T(8,128)(2,1)S(1)}, bf16[16,2,16,512]{3,2,1,0:T(8,128)(2,1)S(1)}, u32[]{:S(2)}, u32[]{:S(2)}) collective-permute-start(bf16[16,2,16,512]{3,2,1,0:T(8,128)(2,1)S(1)} %all-to-all-done.near_ref), channel_id=1, source_target_pairs={{0,16},{16,0},{1,17},{17,1},{2,18},{18,2},{3,19},{19,3},{4,20},{20... | collective-permute-start | bytes 1572872 | tf_op jit(solution)/shard_map/ppermute | solution.py:23
  34.6 2.4 %collective-permute-start = (s32[2,2]{1,0:T(2,128)}, s32[2,2]{1,0:T(2,128)S(1)}, u32[]{:S(2)}, u32[]{:S(2)}) collective-permute-start(s32[2,2]{1,0:T(2,128)} %conn_ref.1), channel_id=1, source_target_pairs={{0,16},{16,0},{1,17},{17,1},{2,18},{18,2},{3,19},{19,3},{4,20},{20... | collective-permute-start | bytes 56 | tf_op jit(solution)/shard_map/ppermute | solution.py:23
  37.0 0.1 pad_add_fusion.where_ref
  37.1 0.0 copy-start
  37.1 0.0 copy-start.1
  37.1 2.1 %fetch.1 = (bf16[2,2,16,16,512]{4,3,2,1,0:T(8,128)(2,1)S(1)}, bf16[2,512,512]{2,1,0:T(8,128)(2,1)S(1)}) custom-call(s32[3]{0:T(128)S(1)} %pad_add_fusion.where_ref, bf16[2,2,16,2,16,512]{5,4,3,2,1,0:T(8,128)(2,1)} %bitcast.8, bf16[2,2,512,512]{3,2,1,0:T(8,128)(2,1)} %right_ref.3), custom_call_target="tpu_custom_call" | custom-call | tf_op jit(solution)/shard_map/fetch/pallas_call | solution.py:61
  39.2 0.0 collective-permute-done.conn2_ref
  39.2 0.0 collective-permute-done.1.far_ref
  39.2 0.0 collective-permute-done.2
  39.3 0.0 copy-start.2
  39.3 0.0 collective-permute-done.3.right2_ref
  39.3 1.3 %copy-done.2 = bf16[2,2,512,512]{3,2,1,0:T(8,128)(2,1)} copy-done((bf16[2,2,512,512]{3,2,1,0:T(8,128)(2,1)}, bf16[2,2,512,512]{3,2,1,0:T(8,128)(2,1)S(1)}, u32[]{:S(2)}) %copy-start.2) | copy-done | bytes 2097176
  40.6 0.0 copy-done
  40.6 0.0 copy-done.1
  40.6 5.0 %slot_sums.1 = (bf16[16,2,16,512]{3,2,1,0:T(8,128)(2,1)}, bf16[16,2,16,512]{3,2,1,0:T(8,128)(2,1)S(1)}) custom-call(s32[3]{0:T(128)S(1)} %pad_add_fusion.where_ref, s32[2,2]{1,0:T(2,128)S(1)} %copy-done.1, s32[2,2]{1,0:T(2,128)S(1)} %collective-permute-done.conn2_ref, s32[2]{0:T(128)S(1)} %copy-done, bf16[16,2,16,512]{3,2,1,0:T(8,128)(2,1)S(1)} %all-to-all-done.near_ref, ...), custom_call_target="tpu_custom_call" | custom-call | tf_op jit(solution)/shard_map/slot_sums/pallas_call | solution.py:152
  45.6 12.6 %all_to_all.20 = bf16[16,2,16,512]{3,2,1,0:T(8,128)(2,1)S(1)} all-to-all(bf16[16,2,16,512]{3,2,1,0:T(8,128)(2,1)S(1)} %get-tuple-element.16), channel_id=1, replica_groups=mesh['x'=4,'y'=4,'c'=2,'sec'=16] {'x'}, dimensions={0} | all-to-all | bytes 1048576 | tf_op jit(solution)/shard_map/all_to_all | solution.py:15
  58.2 5.5 %all-to-all-start.1 = ((bf16[16,2,16,512]{3,2,1,0:T(8,128)(2,1)}), bf16[16,2,16,512]{3,2,1,0:T(8,128)(2,1)S(1)}, u32[]{:S(2)}, u32[]{:S(2)}) async-start(bf16[16,2,16,512]{3,2,1,0:T(8,128)(2,1)} %get-tuple-element.15), calls=%async_computation.1 | async-start | bytes 1048576 | tf_op jit(solution)/shard_map/all_to_all | solution.py:15
  63.7 0.1 reduce_sum.31
  63.8 1.3 %collective-permute-start.5 = (bf16[4,2,16,512]{3,2,1,0:T(8,128)(2,1)S(1)}, bf16[4,2,16,512]{3,2,1,0:T(8,128)(2,1)S(1)}, u32[]{:S(2)}, u32[]{:S(2)}) collective-permute-start(bf16[4,2,16,512]{3,2,1,0:T(8,128)(2,1)S(1)} %reduce_sum.31), channel_id=1, source_target_pairs={{0,1},{1,2},{2,3},{3,4},{4,5},{5,6},{6,7},{7,8},{8,9},{9,10},{10,1... | collective-permute-start | bytes 393224 | tf_op jit(solution)/shard_map/ppermute | solution.py:33
  65.1 1.3 %collective-permute-start.4 = (bf16[4,2,16,512]{3,2,1,0:T(8,128)(2,1)S(1)}, bf16[4,2,16,512]{3,2,1,0:T(8,128)(2,1)S(1)}, u32[]{:S(2)}, u32[]{:S(2)}) collective-permute-start(bf16[4,2,16,512]{3,2,1,0:T(8,128)(2,1)S(1)} %reduce_sum.31), channel_id=1, source_target_pairs={{15,0},{31,16},{47,32},{63,48},{79,64},{95,80},{111,96},{127,112},... | collective-permute-start | bytes 393224 | tf_op jit(solution)/shard_map/ppermute | solution.py:28
  66.4 4.3 %all-to-all-done.1 = bf16[16,2,16,512]{3,2,1,0:T(8,128)(2,1)S(1)} async-done(((bf16[16,2,16,512]{3,2,1,0:T(8,128)(2,1)}), bf16[16,2,16,512]{3,2,1,0:T(8,128)(2,1)S(1)}, u32[]{:S(2)}, u32[]{:S(2)}) %all-to-all-start.1) | async-done | bytes 524320 | tf_op jit(solution)/shard_map/all_to_all | solution.py:15
  70.7 0.1 convert_reduce_fusion
  70.8 0.0 collective-permute-done.5
  70.8 6.1 %collective-permute-done.4 = bf16[4,2,16,512]{3,2,1,0:T(8,128)(2,1)S(1)} collective-permute-done((bf16[4,2,16,512]{3,2,1,0:T(8,128)(2,1)S(1)}, bf16[4,2,16,512]{3,2,1,0:T(8,128)(2,1)S(1)}, u32[]{:S(2)}, u32[]{:S(2)}) %collective-permute-start.4) | collective-permute-done | bytes 131104 | tf_op jit(solution)/shard_map/ppermute | solution.py:28
  77.0 11.2 %all_to_all.21 = bf16[4,2,16,512]{3,2,1,0:T(8,128)(2,1)S(1)} all-to-all(bf16[4,2,16,512]{3,2,1,0:T(8,128)(2,1)S(1)} %add_convert_fusion), channel_id=1, replica_groups=mesh['x'=4,'y'=4,'c'=2,'sec'=16] {'y'}, dimensions={0} | all-to-all | bytes 262144 | tf_op jit(solution)/shard_map/all_to_all | solution.py:15
  88.2 0.6 select_convert_fusion
  (3 shorter events, 0.1 us)
Async XLA Ops:
  0.0 39.2 %collective-permute-start.2 = (bf16[2,2,512,512]{3,2,1,0:T(8,128)(2,1)}, bf16[2,2,512,512]{3,2,1,0:T(8,128)(2,1)S(1)}, u32[]{:S(2)}, u32[]{:S(2)}) collective-permute-start(bf16[2,2,512,512]{3,2,1,0:T(8,128)(2,1)} %param.6), channel_id=1, source_target_pairs={{0,16},{16,0},{1,17},{17,1},{2,18},{18,2},{3,19},{19,3},{4,20},{20... | collective-permute-start | bytes 6291464 | tf_op jit(solution)/shard_map/ppermute | solution.py:23
  1.9 37.3 %collective-permute-start.3 = (bf16[2,2,512,512]{3,2,1,0:T(8,128)(2,1)}, bf16[2,2,512,512]{3,2,1,0:T(8,128)(2,1)}, u32[]{:S(2)}, u32[]{:S(2)}) collective-permute-start(bf16[2,2,512,512]{3,2,1,0:T(8,128)(2,1)} %right_ref.3), channel_id=1, source_target_pairs={{0,16},{16,0},{1,17},{17,1},{2,18},{18,2},{3,19},{19,3},{4,20},{20... | collective-permute-start | bytes 6291464 | tf_op jit(solution)/shard_map/ppermute | solution.py:23
  6.0 26.7 %all-to-all-start = ((bf16[16,2,16,512]{3,2,1,0:T(8,128)(2,1)}), bf16[16,2,16,512]{3,2,1,0:T(8,128)(2,1)S(1)}, u32[]{:S(2)}, u32[]{:S(2)}) async-start(bf16[16,2,16,512]{3,2,1,0:T(8,128)(2,1)} %broadcast_in_dim.4), calls=%async_computation | async-start | bytes 1048576 | tf_op jit(solution)/shard_map/all_to_all | solution.py:15
  32.7 6.6 %collective-permute-start.1 = (bf16[16,2,16,512]{3,2,1,0:T(8,128)(2,1)S(1)}, bf16[16,2,16,512]{3,2,1,0:T(8,128)(2,1)S(1)}, u32[]{:S(2)}, u32[]{:S(2)}) collective-permute-start(bf16[16,2,16,512]{3,2,1,0:T(8,128)(2,1)S(1)} %all-to-all-done.near_ref), channel_id=1, source_target_pairs={{0,16},{16,0},{1,17},{17,1},{2,18},{18,2},{3,19},{19,3},{4,20},{20... | collective-permute-start | bytes 1572872 | tf_op jit(solution)/shard_map/ppermute | solution.py:23
  34.6 4.6 %collective-permute-start = (s32[2,2]{1,0:T(2,128)}, s32[2,2]{1,0:T(2,128)S(1)}, u32[]{:S(2)}, u32[]{:S(2)}) collective-permute-start(s32[2,2]{1,0:T(2,128)} %conn_ref.1), channel_id=1, source_target_pairs={{0,16},{16,0},{1,17},{17,1},{2,18},{18,2},{3,19},{19,3},{4,20},{20... | collective-permute-start | bytes 56 | tf_op jit(solution)/shard_map/ppermute | solution.py:23
  37.1 3.5 %copy-start = (s32[2]{0:T(128)S(1)}, s32[2]{0:T(128)}, u32[]{:S(2)}) copy-start(s32[2]{0:T(128)} %dims_ref.1) | copy-start | bytes 28
  37.1 3.5 %copy-start.1 = (s32[2,2]{1,0:T(2,128)S(1)}, s32[2,2]{1,0:T(2,128)}, u32[]{:S(2)}) copy-start(s32[2,2]{1,0:T(2,128)} %conn_ref.1) | copy-start | bytes 52
  39.3 1.3 %copy-start.2 = (bf16[2,2,512,512]{3,2,1,0:T(8,128)(2,1)}, bf16[2,2,512,512]{3,2,1,0:T(8,128)(2,1)S(1)}, u32[]{:S(2)}) copy-start(bf16[2,2,512,512]{3,2,1,0:T(8,128)(2,1)S(1)} %collective-permute-done.2) | copy-start | bytes 6291460
  58.2 12.5 %all-to-all-start.1 = ((bf16[16,2,16,512]{3,2,1,0:T(8,128)(2,1)}), bf16[16,2,16,512]{3,2,1,0:T(8,128)(2,1)S(1)}, u32[]{:S(2)}, u32[]{:S(2)}) async-start(bf16[16,2,16,512]{3,2,1,0:T(8,128)(2,1)} %get-tuple-element.15), calls=%async_computation.1 | async-start | bytes 1048576 | tf_op jit(solution)/shard_map/all_to_all | solution.py:15
  63.8 7.0 %collective-permute-start.5 = (bf16[4,2,16,512]{3,2,1,0:T(8,128)(2,1)S(1)}, bf16[4,2,16,512]{3,2,1,0:T(8,128)(2,1)S(1)}, u32[]{:S(2)}, u32[]{:S(2)}) collective-permute-start(bf16[4,2,16,512]{3,2,1,0:T(8,128)(2,1)S(1)} %reduce_sum.31), channel_id=1, source_target_pairs={{0,1},{1,2},{2,3},{3,4},{4,5},{5,6},{6,7},{7,8},{8,9},{9,10},{10,1... | collective-permute-start | bytes 393224 | tf_op jit(solution)/shard_map/ppermute | solution.py:33
  65.1 11.8 %collective-permute-start.4 = (bf16[4,2,16,512]{3,2,1,0:T(8,128)(2,1)S(1)}, bf16[4,2,16,512]{3,2,1,0:T(8,128)(2,1)S(1)}, u32[]{:S(2)}, u32[]{:S(2)}) collective-permute-start(bf16[4,2,16,512]{3,2,1,0:T(8,128)(2,1)S(1)} %reduce_sum.31), channel_id=1, source_target_pairs={{15,0},{31,16},{47,32},{63,48},{79,64},{95,80},{111,96},{127,112},... | collective-permute-start | bytes 393224 | tf_op jit(solution)/shard_map/ppermute | solution.py:28

commit v11 on v10

--- a/solution.py
+++ b/solution.py
@@ -1,3 +1,5 @@
+import functools
+
 import jax
 import jax.numpy as jnp
 from jax import lax
@@ -72,7 +74,7 @@
     )(where, in_hbm(left), in_hbm(right))
 
 
-def sums_kernel(where_ref, conn_ref, conn2_ref, dims_ref, near_ref, far_ref, rows0_ref, right0_ref, right_ref, left2_ref, right2_ref, own_ref, onward_ref, psi_ref, rows_ref, rights_ref, half_ref, sum_ref, staged_ref, sems, out_sem):
+def sums_kernel(nx, ny, where_ref, conn_ref, conn2_ref, dims_ref, near_ref, far_ref, rows0_ref, right0_ref, right_ref, left2_ref, right2_ref, own_ref, onward_ref, psi_ref, rows_ref, rights_ref, half_ref, sum_ref, staged_ref, sems, out_sem):
     kdev, sdev, width, _ = right_ref.shape
     chips, _, tall, _ = near_ref.shape
     group = where_ref[0]
@@ -95,21 +97,23 @@
     cols = lax.broadcasted_iota(jnp.int32, (tall, width), 1)
     row = lax.broadcasted_iota(jnp.int32, (tall, width), 0)
 
-    def mask_chip(s, chip):
+    def mask_chip(s, x, y):
         size = dims_ref[s]
         for ref, seat in ((near_ref, core), (far_ref, 1 - core)):
-            start = pl.multiple_of((chip * 2 + seat) * tall, tall)
+            start = pl.multiple_of(((x * ny + y) * 2 + seat) * tall, tall)
             kept = (cols < size) & (row + start < size)
-            psi_ref[s, pl.ds(start, tall), :] = jnp.where(kept, ref[chip, s].astype(F32), 0.0).astype(BF16)
-
-    @pl.loop(0, chips // 2)
-    def _(pair):
-        mask_chip(0, 2 * pair)
-        mask_chip(0, 2 * pair + 1)
+            psi_ref[s, pl.ds(start, tall), :] = jnp.where(kept, ref[y * nx + x, s].astype(F32), 0.0).astype(BF16)
+
+    @pl.loop(0, ny)
+    def _(y):
+        for x in range(nx):
+            mask_chip(0, x, y)
 
     for s in range(1, sdev):
-        for chip in range(chips):
-            mask_chip(s, chip)
+        for y in range(ny):
+            for x in range(nx):
+                mask_chip(s, x, y)
+
     sum_ref[...] = jnp.zeros_like(sum_ref)
     for whose, s, rows, rights, fetches in steps:
         for fetch in fetches:
@@ -140,7 +144,7 @@
     leave.wait()
 
 
-def slot_sums(where, conn, conn2, dims, near, far, rows0, right0, right, left2, right2):
+def slot_sums(nx, ny, where, conn, conn2, dims, near, far, rows0, right0, right, left2, right2):
     kdev, sdev, chips, _, tall, width = left2.shape
     assert sdev == 2
     rest = 2 * sdev - 1
@@ -150,7 +154,7 @@
     hbm = pl.BlockSpec(memory_space=pltpu.HBM)
     many = chips * tall
     return pl.pallas_call(
-        sums_kernel,
+        functools.partial(sums_kernel, nx, ny),
         in_specs=[smem] * 4 + [vmem] * 4 + [hbm] * 3,
         out_specs=[hbm, vmem],
         out_shape=[pltpu.HBM(block, BF16), pltpu.VMEM(block, BF16)],
@@ -188,11 +192,11 @@
     conn2 = from_partner(conn)
     left = left_ops.reshape(by_row)
     rows0, right0 = fetched(where, left, right_ops)
-    by_x = shared(psi, ("x", "y"), nx * ny)
+    by_x = shared(psi, ("y", "x"), nx * ny)
     kept = kept_entries(dims, places[2], tall, width)
     by_x, kept = lax.optimization_barrier((by_x, kept))
     other = from_partner(by_x)
-    own, onward = slot_sums(where, conn, conn2, dims, by_x, other, rows0, right0, right_ops, left2, right2)
+    own, onward = slot_sums(nx, ny, where, conn, conn2, dims, by_x, other, rows0, right0, right_ops, left2, right2)
     by_chip = (nx, ny, sdev, tall, width)
     onward = exchanged(onward, "x").reshape(by_chip).astype(F32).sum(axis=0).astype(BF16)
     far = around(onward)

time: 89.5 us -> 89.5 us (level)
    all_to_all x2, waiting for transfers between devices: 19.4 us -> 18.5 us  [exchanged(): return lax.all_to_all(x, axis, split_axis=0, concat_axis=0, tiled=True)]
where the time goes in v11:
time: 89.5 us; the launch traced here: 88.9 us
  starting transfers between devices  26.8 us (30%)
  waiting for transfers between devices  24.9 us (28%)
  blocking collectives  24.5 us (27%)
  Pallas kernels  7.09 us (8%)
  local copies, waits for them, and re-layouts  2.92 us (3%)
  other arithmetic  2.47 us (3%)
    all_to_all x2, blocking collectives, exchanged(): return lax.all_to_all(x, axis, split_axis=0, concat_axis=0, tiled=True)  24.5 us
    all_to_all x2, waiting for transfers between devices, exchanged(): return lax.all_to_all(x, axis, split_axis=0, concat_axis=0, tiled=True)  18.5 us
    all_to_all x2, starting transfers between devices, exchanged(): return lax.all_to_all(x, axis, split_axis=0, concat_axis=0, tiled=True)  15.6 us
    ppermute x4, starting transfers between devices, from_partner(): return lax.ppermute(x, 'c', [(0, 1), (1, 0)])  8.64 us
    ppermute x1, waiting for transfers between devices, around(): return lax.ppermute(x, 'sec', [(n - 1, 0)])  6.4 us
    pallas_call x1, Pallas kernels, slot_sums(): pl.pallas_call(functools.partial(sums_kernel, nx, ny), in_specs=[smem] *...  4.97 us
    pallas_call x1, Pallas kernels, fetched(): pl.pallas_call(fetch_kernel, in_specs=[pl.BlockSpec(memory_space=pltpu.SM...  2.11 us
  transfers between devices with their start and end apart: 8, of which 3 were waited for; matrix products, arithmetic and copies ran while one was open for 4% of the time, Pallas kernels for 2%

profile of v11, /device:TPU:6, one launch (start us, length us, event | category | flops | bytes accessed | tf_op | source)
XLA Modules:
  0.0 88.9 jit_solution(9883463271134080562)
XLA Ops:
  0.0 1.9 %collective-permute-start.2 = (bf16[2,2,512,512]{3,2,1,0:T(8,128)(2,1)}, bf16[2,2,512,512]{3,2,1,0:T(8,128)(2,1)S(1)}, u32[]{:S(2)}, u32[]{:S(2)}) collective-permute-start(bf16[2,2,512,512]{3,2,1,0:T(8,128)(2,1)} %param.6), channel_id=1, source_target_pairs={{0,16},{16,0},{1,17},{17,1},{2,18},{18,2},{3,19},{19,3},{4,20},{20... | collective-permute-start | bytes 6291464 | tf_op jit(solution)/shard_map/ppermute | solution.py:25
  1.9 2.4 %collective-permute-start.3 = (bf16[2,2,512,512]{3,2,1,0:T(8,128)(2,1)}, bf16[2,2,512,512]{3,2,1,0:T(8,128)(2,1)}, u32[]{:S(2)}, u32[]{:S(2)}) collective-permute-start(bf16[2,2,512,512]{3,2,1,0:T(8,128)(2,1)} %right_ref.3), channel_id=1, source_target_pairs={{0,16},{16,0},{1,17},{17,1},{2,18},{18,2},{3,19},{19,3},{4,20},{20... | collective-permute-start | bytes 6291464 | tf_op jit(solution)/shard_map/ppermute | solution.py:25
  4.3 1.6 %broadcast_in_dim.4 = bf16[16,2,16,512]{3,2,1,0:T(8,128)(2,1)} broadcast(bf16[2,16,512]{2,1,0:T(8,128)(2,1)} %param.5), dimensions={1,2,3} | broadcast | bytes 557056 | tf_op jit(solution)/shard_map/broadcast_in_dim | solution.py:21
  6.0 10.1 %all-to-all-start = ((bf16[16,2,16,512]{3,2,1,0:T(8,128)(2,1)}), bf16[16,2,16,512]{3,2,1,0:T(8,128)(2,1)S(1)}, u32[]{:S(2)}, u32[]{:S(2)}) async-start(bf16[16,2,16,512]{3,2,1,0:T(8,128)(2,1)} %broadcast_in_dim.4), calls=%async_computation | async-start | bytes 1048576 | tf_op jit(solution)/shard_map/all_to_all | solution.py:17
  16.0 0.7 broadcast_compare_fusion
  16.7 0.7 iota_compare_fusion
  17.5 0.1 broadcast_and_fusion
  17.6 14.7 %all-to-all-done.near_ref = bf16[16,2,16,512]{3,2,1,0:T(8,128)(2,1)S(1)} async-done(((bf16[16,2,16,512]{3,2,1,0:T(8,128)(2,1)}), bf16[16,2,16,512]{3,2,1,0:T(8,128)(2,1)S(1)}, u32[]{:S(2)}, u32[]{:S(2)}) %all-to-all-start) | async-done | bytes 524320 | tf_op jit(solution)/shard_map/all_to_all | solution.py:17
  32.3 1.9 %collective-permute-start.1 = (bf16[16,2,16,512]{3,2,1,0:T(8,128)(2,1)S(1)}, bf16[16,2,16,512]{3,2,1,0:T(8,128)(2,1)S(1)}, u32[]{:S(2)}, u32[]{:S(2)}) collective-permute-start(bf16[16,2,16,512]{3,2,1,0:T(8,128)(2,1)S(1)} %all-to-all-done.near_ref), channel_id=1, source_target_pairs={{0,16},{16,0},{1,17},{17,1},{2,18},{18,2},{3,19},{19,3},{4,20},{20... | collective-permute-start | bytes 1572872 | tf_op jit(solution)/shard_map/ppermute | solution.py:25
  34.2 2.4 %collective-permute-start = (s32[2,2]{1,0:T(2,128)}, s32[2,2]{1,0:T(2,128)S(1)}, u32[]{:S(2)}, u32[]{:S(2)}) collective-permute-start(s32[2,2]{1,0:T(2,128)} %conn_ref.1), channel_id=1, source_target_pairs={{0,16},{16,0},{1,17},{17,1},{2,18},{18,2},{3,19},{19,3},{4,20},{20... | collective-permute-start | bytes 56 | tf_op jit(solution)/shard_map/ppermute | solution.py:25
  36.6 0.1 pad_add_fusion.where_ref
  36.7 0.0 copy-start
  36.7 0.0 copy-start.1
  36.7 2.1 %fetch.1 = (bf16[2,2,16,16,512]{4,3,2,1,0:T(8,128)(2,1)S(1)}, bf16[2,512,512]{2,1,0:T(8,128)(2,1)S(1)}) custom-call(s32[3]{0:T(128)S(1)} %pad_add_fusion.where_ref, bf16[2,2,16,2,16,512]{5,4,3,2,1,0:T(8,128)(2,1)} %bitcast.8, bf16[2,2,512,512]{3,2,1,0:T(8,128)(2,1)} %right_ref.3), custom_call_target="tpu_custom_call" | custom-call | tf_op jit(solution)/shard_map/fetch/pallas_call | solution.py:63
  38.8 0.0 collective-permute-done.conn2_ref
  38.8 0.0 collective-permute-done.1.far_ref
  38.8 0.0 collective-permute-done.2
  38.9 0.0 copy-start.2
  38.9 0.0 collective-permute-done.3.right2_ref
  38.9 1.3 %copy-done.2 = bf16[2,2,512,512]{3,2,1,0:T(8,128)(2,1)} copy-done((bf16[2,2,512,512]{3,2,1,0:T(8,128)(2,1)}, bf16[2,2,512,512]{3,2,1,0:T(8,128)(2,1)S(1)}, u32[]{:S(2)}) %copy-start.2) | copy-done | bytes 2097176
  40.2 0.0 copy-done
  40.2 0.0 copy-done.1
  40.2 5.0 %slot_sums.1 = (bf16[16,2,16,512]{3,2,1,0:T(8,128)(2,1)}, bf16[16,2,16,512]{3,2,1,0:T(8,128)(2,1)S(1)}) custom-call(s32[3]{0:T(128)S(1)} %pad_add_fusion.where_ref, s32[2,2]{1,0:T(2,128)S(1)} %copy-done.1, s32[2,2]{1,0:T(2,128)S(1)} %collective-permute-done.conn2_ref, s32[2]{0:T(128)S(1)} %copy-done, bf16[16,2,16,512]{3,2,1,0:T(8,128)(2,1)S(1)} %all-to-all-done.near_ref, ...), custom_call_target="tpu_custom_call" | custom-call | tf_op jit(solution)/shard_map/slot_sums/pallas_call | solution.py:156
  45.2 12.5 %all_to_all.20 = bf16[16,2,16,512]{3,2,1,0:T(8,128)(2,1)S(1)} all-to-all(bf16[16,2,16,512]{3,2,1,0:T(8,128)(2,1)S(1)} %get-tuple-element.16), channel_id=1, replica_groups=mesh['x'=4,'y'=4,'c'=2,'sec'=16] {'x'}, dimensions={0} | all-to-all | bytes 1048576 | tf_op jit(solution)/shard_map/all_to_all | solution.py:17
  57.7 5.5 %all-to-all-start.1 = ((bf16[16,2,16,512]{3,2,1,0:T(8,128)(2,1)}), bf16[16,2,16,512]{3,2,1,0:T(8,128)(2,1)S(1)}, u32[]{:S(2)}, u32[]{:S(2)}) async-start(bf16[16,2,16,512]{3,2,1,0:T(8,128)(2,1)} %get-tuple-element.15), calls=%async_computation.1 | async-start | bytes 1048576 | tf_op jit(solution)/shard_map/all_to_all | solution.py:17
  63.2 0.1 reduce_sum.31
  63.2 1.3 %collective-permute-start.5 = (bf16[4,2,16,512]{3,2,1,0:T(8,128)(2,1)S(1)}, bf16[4,2,16,512]{3,2,1,0:T(8,128)(2,1)S(1)}, u32[]{:S(2)}, u32[]{:S(2)}) collective-permute-start(bf16[4,2,16,512]{3,2,1,0:T(8,128)(2,1)S(1)} %reduce_sum.31), channel_id=1, source_target_pairs={{0,1},{1,2},{2,3},{3,4},{4,5},{5,6},{6,7},{7,8},{8,9},{9,10},{10,1... | collective-permute-start | bytes 393224 | tf_op jit(solution)/shard_map/ppermute | solution.py:35
  64.6 1.3 %collective-permute-start.4 = (bf16[4,2,16,512]{3,2,1,0:T(8,128)(2,1)S(1)}, bf16[4,2,16,512]{3,2,1,0:T(8,128)(2,1)S(1)}, u32[]{:S(2)}, u32[]{:S(2)}) collective-permute-start(bf16[4,2,16,512]{3,2,1,0:T(8,128)(2,1)S(1)} %reduce_sum.31), channel_id=1, source_target_pairs={{15,0},{31,16},{47,32},{63,48},{79,64},{95,80},{111,96},{127,112},... | collective-permute-start | bytes 393224 | tf_op jit(solution)/shard_map/ppermute | solution.py:30
  65.9 3.8 %all-to-all-done.1 = bf16[16,2,16,512]{3,2,1,0:T(8,128)(2,1)S(1)} async-done(((bf16[16,2,16,512]{3,2,1,0:T(8,128)(2,1)}), bf16[16,2,16,512]{3,2,1,0:T(8,128)(2,1)S(1)}, u32[]{:S(2)}, u32[]{:S(2)}) %all-to-all-start.1) | async-done | bytes 524320 | tf_op jit(solution)/shard_map/all_to_all | solution.py:17
  69.6 0.1 convert_reduce_fusion
  69.7 0.0 collective-permute-done.5
  69.7 6.4 %collective-permute-done.4 = bf16[4,2,16,512]{3,2,1,0:T(8,128)(2,1)S(1)} collective-permute-done((bf16[4,2,16,512]{3,2,1,0:T(8,128)(2,1)S(1)}, bf16[4,2,16,512]{3,2,1,0:T(8,128)(2,1)S(1)}, u32[]{:S(2)}, u32[]{:S(2)}) %collective-permute-start.4) | collective-permute-done | bytes 131104 | tf_op jit(solution)/shard_map/ppermute | solution.py:30
  76.2 12.1 %all_to_all.21 = bf16[4,2,16,512]{3,2,1,0:T(8,128)(2,1)S(1)} all-to-all(bf16[4,2,16,512]{3,2,1,0:T(8,128)(2,1)S(1)} %add_convert_fusion), channel_id=1, replica_groups=mesh['x'=4,'y'=4,'c'=2,'sec'=16] {'y'}, dimensions={0} | all-to-all | bytes 262144 | tf_op jit(solution)/shard_map/all_to_all | solution.py:17
  88.2 0.6 select_convert_fusion
  (3 shorter events, 0.1 us)
Async XLA Ops:
  0.0 38.8 %collective-permute-start.2 = (bf16[2,2,512,512]{3,2,1,0:T(8,128)(2,1)}, bf16[2,2,512,512]{3,2,1,0:T(8,128)(2,1)S(1)}, u32[]{:S(2)}, u32[]{:S(2)}) collective-permute-start(bf16[2,2,512,512]{3,2,1,0:T(8,128)(2,1)} %param.6), channel_id=1, source_target_pairs={{0,16},{16,0},{1,17},{17,1},{2,18},{18,2},{3,19},{19,3},{4,20},{20... | collective-permute-start | bytes 6291464 | tf_op jit(solution)/shard_map/ppermute | solution.py:25
  1.9 36.9 %collective-permute-start.3 = (bf16[2,2,512,512]{3,2,1,0:T(8,128)(2,1)}, bf16[2,2,512,512]{3,2,1,0:T(8,128)(2,1)}, u32[]{:S(2)}, u32[]{:S(2)}) collective-permute-start(bf16[2,2,512,512]{3,2,1,0:T(8,128)(2,1)} %right_ref.3), channel_id=1, source_target_pairs={{0,16},{16,0},{1,17},{17,1},{2,18},{18,2},{3,19},{19,3},{4,20},{20... | collective-permute-start | bytes 6291464 | tf_op jit(solution)/shard_map/ppermute | solution.py:25
  6.0 26.3 %all-to-all-start = ((bf16[16,2,16,512]{3,2,1,0:T(8,128)(2,1)}), bf16[16,2,16,512]{3,2,1,0:T(8,128)(2,1)S(1)}, u32[]{:S(2)}, u32[]{:S(2)}) async-start(bf16[16,2,16,512]{3,2,1,0:T(8,128)(2,1)} %broadcast_in_dim.4), calls=%async_computation | async-start | bytes 1048576 | tf_op jit(solution)/shard_map/all_to_all | solution.py:17
  32.3 6.6 %collective-permute-start.1 = (bf16[16,2,16,512]{3,2,1,0:T(8,128)(2,1)S(1)}, bf16[16,2,16,512]{3,2,1,0:T(8,128)(2,1)S(1)}, u32[]{:S(2)}, u32[]{:S(2)}) collective-permute-start(bf16[16,2,16,512]{3,2,1,0:T(8,128)(2,1)S(1)} %all-to-all-done.near_ref), channel_id=1, source_target_pairs={{0,16},{16,0},{1,17},{17,1},{2,18},{18,2},{3,19},{19,3},{4,20},{20... | collective-permute-start | bytes 1572872 | tf_op jit(solution)/shard_map/ppermute | solution.py:25
  34.2 4.6 %collective-permute-start = (s32[2,2]{1,0:T(2,128)}, s32[2,2]{1,0:T(2,128)S(1)}, u32[]{:S(2)}, u32[]{:S(2)}) collective-permute-start(s32[2,2]{1,0:T(2,128)} %conn_ref.1), channel_id=1, source_target_pairs={{0,16},{16,0},{1,17},{17,1},{2,18},{18,2},{3,19},{19,3},{4,20},{20... | collective-permute-start | bytes 56 | tf_op jit(solution)/shard_map/ppermute | solution.py:25
  36.7 3.5 %copy-start = (s32[2]{0:T(128)S(1)}, s32[2]{0:T(128)}, u32[]{:S(2)}) copy-start(s32[2]{0:T(128)} %dims_ref.1) | copy-start | bytes 28
  36.7 3.5 %copy-start.1 = (s32[2,2]{1,0:T(2,128)S(1)}, s32[2,2]{1,0:T(2,128)}, u32[]{:S(2)}) copy-start(s32[2,2]{1,0:T(2,128)} %conn_ref.1) | copy-start | bytes 52
  38.9 1.3 %copy-start.2 = (bf16[2,2,512,512]{3,2,1,0:T(8,128)(2,1)}, bf16[2,2,512,512]{3,2,1,0:T(8,128)(2,1)S(1)}, u32[]{:S(2)}) copy-start(bf16[2,2,512,512]{3,2,1,0:T(8,128)(2,1)S(1)} %collective-permute-done.2) | copy-start | bytes 6291460
  57.7 12.0 %all-to-all-start.1 = ((bf16[16,2,16,512]{3,2,1,0:T(8,128)(2,1)}), bf16[16,2,16,512]{3,2,1,0:T(8,128)(2,1)S(1)}, u32[]{:S(2)}, u32[]{:S(2)}) async-start(bf16[16,2,16,512]{3,2,1,0:T(8,128)(2,1)} %get-tuple-element.15), calls=%async_computation.1 | async-start | bytes 1048576 | tf_op jit(solution)/shard_map/all_to_all | solution.py:17
  63.2 6.5 %collective-permute-start.5 = (bf16[4,2,16,512]{3,2,1,0:T(8,128)(2,1)S(1)}, bf16[4,2,16,512]{3,2,1,0:T(8,128)(2,1)S(1)}, u32[]{:S(2)}, u32[]{:S(2)}) collective-permute-start(bf16[4,2,16,512]{3,2,1,0:T(8,128)(2,1)S(1)} %reduce_sum.31), channel_id=1, source_target_pairs={{0,1},{1,2},{2,3},{3,4},{4,5},{5,6},{6,7},{7,8},{8,9},{9,10},{10,1... | collective-permute-start | bytes 393224 | tf_op jit(solution)/shard_map/ppermute | solution.py:35
  64.6 11.6 %collective-permute-start.4 = (bf16[4,2,16,512]{3,2,1,0:T(8,128)(2,1)S(1)}, bf16[4,2,16,512]{3,2,1,0:T(8,128)(2,1)S(1)}, u32[]{:S(2)}, u32[]{:S(2)}) collective-permute-start(bf16[4,2,16,512]{3,2,1,0:T(8,128)(2,1)S(1)} %reduce_sum.31), channel_id=1, source_target_pairs={{15,0},{31,16},{47,32},{63,48},{79,64},{95,80},{111,96},{127,112},... | collective-permute-start | bytes 393224 | tf_op jit(solution)/shard_map/ppermute | solution.py:30
